TPU v7x, 128 devices: a whole 4x4x4 slice. The times are simulated.
128 devices in a mesh: dp: 4 (over x), fsdp: 32 (over z, y, core).
Axes of the slice: x: 4, y: 4, z: 4, core: 2. Of those that a mesh axis runs over, the one named last changes fastest.
Arguments:
- gradient: bfloat16 [4, 4096, 8, 1024], P('dp', 'fsdp'), may hold values from -3 to 3
- block_owner_index: int32 [32], replicated, may hold values from 0 to 31, as said below
- block_grid_cell: int32 [32], replicated, may hold values from 0 to 31, each once
- left_eigen_basis: float32 [64, 1024, 1024], P('fsdp', None, 'dp'), may hold values from -0.1875 to 0.1875
- right_eigen_basis: float32 [64, 1024, 1024], P('fsdp', None, 'dp'), may hold values from -0.1875 to 0.1875
- left_statistic_matrix: float32 [64, 1024, 1024], P('fsdp', None, 'dp'), may hold values from -6 to 6
- right_statistic_matrix: float32 [64, 1024, 1024], P('fsdp', None, 'dp'), may hold values from -6 to 6
- first_adam_moment: float32 [64, 1024, 1024], P('fsdp', None, 'dp'), may hold values from -0.09 to 0.09
- second_adam_moment: float32 [64, 1024, 1024], P('fsdp', None, 'dp'), may hold values from 1e-05 to 0.001
Outputs:
- new_left_stat: float32 [64, 1024, 1024], P('fsdp', None, 'dp')
- new_right_stat: float32 [64, 1024, 1024], P('fsdp', None, 'dp')
- new_first: float32 [64, 1024, 1024], P('fsdp', None, 'dp')
- new_second: float32 [64, 1024, 1024], P('fsdp', None, 'dp')
- update: bfloat16 [4096, 8, 1024], P('fsdp', None, 'dp')
Inputs may be any that keep to these rules, and one draw needn't show every extreme that they name: `block_owner_index`: no fsdp index owns more than 2 blocks; a quarter of the fsdp indices own 2 blocks and a quarter own none.
All inputs are finite; a program needn't handle non-finite values.
Results may differ from a plain program's by a relative error of at most 0.013.
Values may be sent and summed in bfloat16 or wider, within the bound.
No kernel may reach another device: no remote copies, remote signals or barrier semaphores. Data moves between devices by JAX's collectives and lax.ppermute only.
A program may use at most 128 MiB of HBM per device.

v0:
```python
import jax
import jax.numpy as jnp
from jax import lax
from jax.sharding import PartitionSpec as P


def in_order(blocks, dim):
    blocks = jnp.moveaxis(blocks, 0, dim)
    dims = blocks.shape
    return blocks.reshape(*dims[:dim], dims[dim] * dims[dim + 1], *dims[dim + 2 :])


def on_gathered_pieces(array, axis, dim, work, out_dim):
    width = array.shape[dim]
    pieces = jnp.split(array, 2, axis=dim) if width % 2 == 0 else [array]
    initial = jnp.arange(lax.axis_size(axis)) * width
    blocks = [lax.all_gather(piece, axis) for piece in pieces]
    made = [jax.vmap(work)(b, initial + k * (width // len(pieces))) for k, b in enumerate(blocks)]
    return in_order(jnp.concatenate(made, axis=out_dim + 1), out_dim)


def slot_lookup_table(block_owner_index, block_grid_cell, slot_count, per_owner):
    block_ids = jnp.arange(block_owner_index.shape[0], dtype=jnp.int32)
    shared = (block_owner_index[:, None] == block_owner_index[None, :]) & (
        block_ids[None, :] < block_ids[:, None]
    )
    rank_in = jnp.sum(shared.astype(jnp.int32), axis=1)
    block_slot_index = block_owner_index * per_owner + rank_in
    slot_ids = jnp.arange(slot_count, dtype=jnp.int32)
    matches = (block_slot_index[None, :] == slot_ids[:, None]).astype(jnp.int32)
    filled_marker = jnp.sum(matches, axis=1)
    slot_grid_cell = jnp.sum(matches * block_grid_cell[None, :], axis=1)
    return (block_slot_index, filled_marker, slot_grid_cell)


def local(
    gradient,
    block_owner_index,
    block_grid_cell,
    left_eigen_basis,
    right_eigen_basis,
    left_statistic_matrix,
    right_statistic_matrix,
    first_adam_moment,
    second_adam_moment,
):
    replicas = lax.axis_size("dp")
    members = lax.axis_size("fsdp")
    member = lax.axis_index("fsdp")
    column_group = lax.axis_index("dp")
    per_owner = left_eigen_basis.shape[0]
    block = left_eigen_basis.shape[1]
    width = left_eigen_basis.shape[2]
    band_rows = gradient.shape[1]
    grid_cols = gradient.shape[2]
    bands = block // band_rows
    grid_rows = members // bands
    piece_rows = band_rows // members
    slot_count = per_owner * members
    partial_terms = gradient.reshape(band_rows, grid_cols, replicas, width).astype(jnp.float32)
    reduced = lax.psum_scatter(
        partial_terms.astype(jnp.bfloat16), "dp", scatter_dimension=2, tiled=True
    ).astype(jnp.float32)
    reduced = reduced.reshape(band_rows, grid_cols, width).astype(jnp.bfloat16)
    block_slot_index, filled_marker, slot_grid_cell = slot_lookup_table(
        block_owner_index, block_grid_cell, slot_count, per_owner
    )
    my_filled = lax.dynamic_slice_in_dim(filled_marker, member * per_owner, per_owner, 0)
    split_band = reduced.reshape(members, piece_rows, grid_cols, width)
    received = lax.all_to_all(split_band, "fsdp", split_axis=0, concat_axis=0, tiled=True)
    by_cell = received.reshape(grid_rows, bands, piece_rows, grid_cols, width)
    by_cell = jnp.transpose(by_cell, (0, 3, 1, 2, 4)).reshape(
        grid_rows * grid_cols, bands, piece_rows, width
    )
    leaving = jnp.take(by_cell, slot_grid_cell, axis=0)
    leaving = jnp.where((filled_marker > 0)[:, None, None, None], leaving, jnp.zeros_like(leaving))
    leaving = leaving.reshape(members, per_owner, bands, piece_rows, width)
    landed = lax.all_to_all(leaving, "fsdp", split_axis=0, concat_axis=0, tiled=True)
    col_piece = jnp.transpose(landed, (1, 2, 0, 3, 4)).reshape(per_owner, block, width)
    gathered = lax.all_gather(col_piece, "dp", axis=2, tiled=True)
    row_piece = lax.dynamic_slice_in_dim(gathered, column_group * width, width, 1)
    new_left = 0.95 * left_statistic_matrix + 0.05 * jnp.einsum(
        "sik,sjk->sij", gathered, row_piece, preferred_element_type=jnp.float32
    )
    new_right = 0.95 * right_statistic_matrix + 0.05 * jnp.einsum(
        "ski,skj->sij", gathered, col_piece, preferred_element_type=jnp.float32
    )
    half_turn = jnp.einsum("sik,sij->skj", left_eigen_basis, gathered.astype(jnp.float32)).astype(
        jnp.bfloat16
    )

    def turn_rows(piece, start):
        return jnp.einsum("skj,sjc->skc", piece.astype(jnp.float32), right_eigen_basis)

    turned = on_gathered_pieces(half_turn, "dp", 1, turn_rows, 1)
    new_first = 0.9 * first_adam_moment + 0.1 * turned
    new_second = 0.999 * second_adam_moment + 0.001 * turned * turned
    direction = new_first / (jnp.sqrt(new_second) + 1e-08)
    full_left = lax.all_gather(left_eigen_basis, "dp", axis=2, tiled=True)
    applied = jnp.einsum("sik,skc->sic", full_left, direction)
    piece = right_eigen_basis
    moved = lax.psum_scatter(
        jnp.einsum("sic,sjc->jsi", applied, piece), "dp", scatter_dimension=0, tiled=True
    )
    backward = jnp.transpose(moved.astype(jnp.bfloat16), (1, 2, 0))
    parted = backward.reshape(per_owner, bands, members, piece_rows, width)
    parted = jnp.transpose(parted, (2, 0, 1, 3, 4))
    parted = jnp.where((my_filled > 0)[None, :, None, None, None], parted, jnp.zeros_like(parted))
    homed = lax.all_to_all(parted, "fsdp", split_axis=0, concat_axis=0, tiled=True)
    homed = homed.reshape(slot_count, bands, piece_rows, width)
    all_cells = jnp.arange(grid_rows * grid_cols, dtype=jnp.int32)
    all_hits = (block_grid_cell[None, :] == all_cells[:, None]).astype(jnp.int32)
    cell_slot = jnp.sum(all_hits * block_slot_index[None, :], axis=1)
    per_cell = jnp.take(homed, cell_slot, axis=0).reshape(
        grid_rows, grid_cols, bands, piece_rows, width
    )
    per_cell = jnp.transpose(per_cell, (0, 2, 3, 1, 4)).reshape(
        members, piece_rows, grid_cols, width
    )
    update = lax.all_to_all(per_cell, "fsdp", split_axis=0, concat_axis=0, tiled=True).reshape(
        band_rows, grid_cols, width
    )
    return (new_left, new_right, new_first, new_second, update)


def solution(mesh):
    in_specs = (
        P("dp", "fsdp", None, None),
        P(),
        P(),
        P("fsdp", None, "dp"),
        P("fsdp", None, "dp"),
        P("fsdp", None, "dp"),
        P("fsdp", None, "dp"),
        P("fsdp", None, "dp"),
        P("fsdp", None, "dp"),
    )
    out_specs = (
        P("fsdp", None, "dp"),
        P("fsdp", None, "dp"),
        P("fsdp", None, "dp"),
        P("fsdp", None, "dp"),
        P("fsdp", None, "dp"),
    )
    return jax.shard_map(local, mesh=mesh, in_specs=in_specs, out_specs=out_specs, check_vma=False)
```

profile of v0, /device:TPU:1, one launch (start us, length us, event | category | flops | bytes accessed | tf_op | source)
XLA Modules:
  0.0 404.2 jit_solution(3661794692890048232)
XLA Ops:
  7.2 3.2 copy.61
  11.6 32.2 %reduce-scatter.3.cloned.1.call-done = bf16[128,8,1,256]{3,1,0,2:T(8,128)(2,1)} async-done(((bf16[128,8,4,256]{3,1,0,2:T(8,128)(2,1)}), bf16[128,8,1,256]{3,1,0,2:T(8,128)(2,1)}) %reduce-scatter.3.cloned.1.call-update) | async-done | bytes 524304 | tf_op jit(solution)/shard_map/reduce_scatter | solution.py:61
  43.8 7.8 %all-to-all-start = ((bf16[32,4,8,256]{3,2,1,0:T(8,128)(2,1)}), bf16[32,4,8,256]{3,2,1,0:T(8,128)(2,1)S(1)}, u32[]{:S(2)}, u32[]{:S(2)}) async-start(bf16[32,4,8,256]{3,2,1,0:T(8,128)(2,1)} %bitcast.89), calls=%async_computation.1 | async-start | bytes 1048576 | tf_op jit(solution)/shard_map/all_to_all | solution.py:70
  51.7 11.3 %all-to-all-done = bf16[32,4,8,256]{3,2,1,0:T(8,128)(2,1)S(1)} async-done(((bf16[32,4,8,256]{3,2,1,0:T(8,128)(2,1)}), bf16[32,4,8,256]{3,2,1,0:T(8,128)(2,1)S(1)}, u32[]{:S(2)}, u32[]{:S(2)}) %all-to-all-start) | async-done | bytes 524320 | tf_op jit(solution)/shard_map/all_to_all | solution.py:70
  66.3 20.7 %all_to_all.20 = bf16[32,2,8,4,256]{4,2,3,1,0:T(8,128)(2,1)S(1)} all-to-all(bf16[32,2,8,4,256]{4,2,3,1,0:T(8,128)(2,1)S(1)} %select_select_fusion), channel_id=1, replica_groups=mesh['dp'=4,'fsdp'=32] {'fsdp'}, dimensions={0} | all-to-all | bytes 2097152 | tf_op jit(solution)/shard_map/all_to_all | solution.py:78
  88.7 46.0 %all-gather.7.cloned.1.call-done = bf16[2,1024,1024]{2,1,0:T(8,128)(2,1)} async-done(((bf16[2,1024,256]{2,1,0:T(8,128)(2,1)}), bf16[2,1024,1024]{2,1,0:T(8,128)(2,1)}) %all-gather.7.cloned.1.call-update) | async-done | bytes 4194320 | tf_op jit(solution)/shard_map/all_gather | solution.py:80
  134.7 4.6 %fusion.16 = bf16[2,256,1024]{1,2,0:T(8,128)(2,1)S(1)} fusion(bf16[2,1024,1024]{2,1,0:T(8,128)(2,1)} %all-gather.7.cloned.1.call-done, f32[2,1024,256]{2,1,0:T(8,128)} %param.12), kind=kOutput, calls=%fused_computation.21 | convolution fusion | flops 1073741824 | bytes 7340032 | tf_op jit(solution)/shard_map/sik,sij->skj/dot_general | solution.py:88
  141.6 2.7 convert.4
  144.4 29.2 %all-gather.13.cloned.1.call-done = bf16[8,128,1024]{2,1,0:T(8,128)(2,1)} async-done(((bf16[2,128,1024]{2,1,0:T(8,128)(2,1)}), bf16[8,128,1024]{2,1,0:T(8,128)(2,1)}) %all-gather.13.cloned.1.call-update) | async-done | bytes 2097168 | tf_op jit(solution)/shard_map/all_gather | solution.py:17
  173.6 2.3 fusion.22
  175.9 30.6 %all-gather.11.cloned.1.call-done = bf16[8,128,1024]{2,1,0:T(8,128)(2,1)} async-done(((bf16[2,128,1024]{2,1,0:T(8,128)(2,1)}), bf16[8,128,1024]{2,1,0:T(8,128)(2,1)}) %all-gather.11.cloned.1.call-update) | async-done | bytes 2097168 | tf_op jit(solution)/shard_map/all_gather | solution.py:17
  206.5 2.3 fusion.17
  211.0 2.6 fusion
  213.6 45.1 %all-gather.9.cloned.1.call-done = bf16[2,1024,1024]{2,1,0:T(8,128)(2,1)} async-done(((bf16[2,1024,256]{2,1,0:T(8,128)(2,1)}), bf16[2,1024,1024]{2,1,0:T(8,128)(2,1)}) %all-gather.9.cloned.1.call-update) | async-done | bytes 4194320 | tf_op jit(solution)/shard_map/all_gather | solution.py:99
  258.7 9.2 %convolution_bitcast_fusion = f32[1024,2,1024]{0,2,1:T(8,128)} fusion(f32[2,1024,256]{2,1,0:T(8,128)S(1)} %copy-done, bf16[2,1024,1024]{2,1,0:T(8,128)(2,1)} %all-gather.9.cloned.1.call-done, f32[2,1024,256]{2,1,0:T(8,128)} %get-tuple-element.18, f32[2,1024,256]{2,1,0:T(8,128)} %get-tuple-element.19), kind=kOutput, calls=%fused_computation.2 | convolution fusion | flops 2148532224 | bytes 18874368 | tf_op jit(solution)/shard_map/sic,sjc->jsi/dot_general | solution.py:103
  268.2 82.6 %reduce-scatter.5.cloned.1.call-done = f32[256,2,1024]{0,2,1:T(8,128)} async-done(((f32[1024,2,1024]{0,2,1:T(8,128)}), f32[256,2,1024]{0,2,1:T(8,128)}) %reduce-scatter.5.cloned.1.call-update) | async-done | bytes 2097168 | tf_op jit(solution)/shard_map/reduce_scatter | solution.py:102
  350.9 1.7 convert_bitcast_fusion
  352.9 1.6 fusion.27
  354.5 7.8 %all-to-all-start.2 = ((bf16[32,2,8,4,256]{4,2,3,1,0:T(8,128)(2,1)}), bf16[32,2,8,4,256]{4,2,3,1,0:T(8,128)(2,1)S(1)}, u32[]{:S(2)}, u32[]{:S(2)}) async-start(bf16[32,2,8,4,256]{4,2,3,1,0:T(8,128)(2,1)} %fusion.27), calls=%async_computation.4 | async-start | bytes 2097152 | tf_op jit(solution)/shard_map/all_to_all | solution.py:109
  362.3 5.9 %multiply_add_fusion = f32[2,1024,256]{2,1,0:T(8,128)} fusion(f32[2,1024,256]{2,1,0:T(8,128)} %param.15, bf16[2,1024,1024]{2,1,0:T(8,128)(2,1)} %all-gather.7.cloned.1.call-done, bf16[2,1024,256]{2,1,0:T(8,128)(2,1)S(1)} %copy-done.2), kind=kOutput, calls=%fused_computation.18 | convolution fusion | flops 1075314688 | bytes 9437184 | tf_op jit(solution)/shard_map/ski,skj->sij/dot_general | solution.py:85
  368.2 11.1 %all-to-all-done.2 = bf16[32,2,8,4,256]{4,2,3,1,0:T(8,128)(2,1)S(1)} async-done(((bf16[32,2,8,4,256]{4,2,3,1,0:T(8,128)(2,1)}), bf16[32,2,8,4,256]{4,2,3,1,0:T(8,128)(2,1)S(1)}, u32[]{:S(2)}, u32[]{:S(2)}) %all-to-all-start.2) | async-done | bytes 1048608 | tf_op jit(solution)/shard_map/all_to_all | solution.py:109
  381.1 3.9 all-to-all-start.3
  385.0 6.0 %multiply_add_fusion.1 = f32[2,1024,256]{2,1,0:T(8,128)} fusion(f32[2,1024,256]{2,1,0:T(8,128)} %param.14, bf16[2,1024,1024]{2,1,0:T(8,128)(2,1)} %all-gather.7.cloned.1.call-done, s32[]{:T(128)S(6)} %select_n.66), kind=kOutput, calls=%fused_computation.19 | convolution fusion | flops 1075314688 | bytes 9437188 | tf_op jit(solution)/shard_map/sik,sjk->sij/dot_general | solution.py:82
  391.0 5.5 %all-to-all-done.3 = bf16[32,4,8,256]{3,2,1,0:T(8,128)(2,1)S(1)} async-done(((bf16[32,4,8,256]{3,2,1,0:T(8,128)(2,1)}), bf16[32,4,8,256]{3,2,1,0:T(8,128)(2,1)S(1)}, u32[]{:S(2)}, u32[]{:S(2)}) %all-to-all-start.3) | async-done | bytes 524320 | tf_op jit(solution)/shard_map/all_to_all | solution.py:120
  (55 shorter events, 14.0 us)
Async XLA Ops:
  7.2 166.4 %copy-start = (f32[2,1024,256]{2,1,0:T(8,128)S(1)}, f32[2,1024,256]{2,1,0:T(8,128)}, u32[]{:S(2)}) copy-start(f32[2,1024,256]{2,1,0:T(8,128)} %param.13) | copy-start | bytes 6291460
  7.2 36.6 %reduce-scatter.3.cloned.1.call-start = ((), (), s32[]{:S(2)}) async-start(), calls=%async_computation.6 | async-start | bytes 2621440 | tf_op jit(solution)/shard_map/reduce_scatter | solution.py:61
  10.4 0.7 copy-start.6
  10.4 0.8 copy-start.5
  43.8 19.2 %all-to-all-start = ((bf16[32,4,8,256]{3,2,1,0:T(8,128)(2,1)}), bf16[32,4,8,256]{3,2,1,0:T(8,128)(2,1)S(1)}, u32[]{:S(2)}, u32[]{:S(2)}) async-start(bf16[32,4,8,256]{3,2,1,0:T(8,128)(2,1)} %bitcast.89), calls=%async_computation.1 | async-start | bytes 1048576 | tf_op jit(solution)/shard_map/all_to_all | solution.py:70
  51.6 83.1 %all-gather.7.cloned.1.call-start = ((), (), s32[]{:S(2)}) async-start(), calls=%async_computation.7 | async-start | bytes 5242880 | tf_op jit(solution)/shard_map/all_gather | solution.py:80
  88.6 84.9 %all-gather.13.cloned.1.call-start = ((), (), s32[]{:S(2)}) async-start(), calls=%async_computation.11 | async-start | bytes 2621440 | tf_op jit(solution)/shard_map/all_gather | solution.py:17
  140.5 66.0 %all-gather.11.cloned.1.call-start = ((), (), s32[]{:S(2)}) async-start(), calls=%async_computation.10 | async-start | bytes 2621440 | tf_op jit(solution)/shard_map/all_gather | solution.py:17
  141.6 117.2 %all-gather.9.cloned.1.call-start = ((), (), s32[]{:S(2)}) async-start(), calls=%async_computation.8 | async-start | bytes 5242880 | tf_op jit(solution)/shard_map/all_gather | solution.py:99
  144.3 206.5 %reduce-scatter.5.cloned.1.call-start = ((), (), s32[]{:S(2)}) async-start(), calls=%async_computation.9 | async-start | bytes 10485760 | tf_op jit(solution)/shard_map/reduce_scatter | solution.py:102
  208.8 1.6 copy-start.3
  208.8 2.2 copy-start.4
  352.9 9.4 %copy-start.2 = (bf16[2,1024,256]{2,1,0:T(8,128)(2,1)S(1)}, bf16[2,1024,256]{2,1,0:T(8,128)(2,1)}, u32[]{:S(2)}) copy-start(bf16[2,1024,256]{2,1,0:T(8,128)(2,1)} %reshape.101) | copy-start | bytes 3145732
  354.5 24.8 %all-to-all-start.2 = ((bf16[32,2,8,4,256]{4,2,3,1,0:T(8,128)(2,1)}), bf16[32,2,8,4,256]{4,2,3,1,0:T(8,128)(2,1)S(1)}, u32[]{:S(2)}, u32[]{:S(2)}) async-start(bf16[32,2,8,4,256]{4,2,3,1,0:T(8,128)(2,1)} %fusion.27), calls=%async_computation.4 | async-start | bytes 2097152 | tf_op jit(solution)/shard_map/all_to_all | solution.py:109
  381.1 15.5 %all-to-all-start.3 = ((bf16[32,4,8,256]{3,2,1,0:T(8,128)(2,1)}), bf16[32,4,8,256]{3,2,1,0:T(8,128)(2,1)S(1)}, u32[]{:S(2)}, u32[]{:S(2)}) async-start(bf16[32,4,8,256]{3,2,1,0:T(8,128)(2,1)} %bitcast.28), calls=%async_computation.5 | async-start | bytes 1048576 | tf_op jit(solution)/shard_map/all_to_all | solution.py:120
  385.0 12.3 %copy-start.1 = (f32[2,1024,256]{2,1,0:T(8,128)S(1)}, f32[2,1024,256]{2,1,0:T(8,128)}, u32[]{:S(2)}) copy-start(f32[2,1024,256]{2,1,0:T(8,128)} %param.13) | copy-start | bytes 6291460
Sparse Core Ops, SparseCore 0:
  11.0 32.7 reduce-scatter.2
  88.8 45.8 all-gather.6
  140.6 32.8 all-gather.12
  175.6 30.7 all-gather.10
  208.5 50.1 all-gather.8
  268.1 82.7 reduce-scatter.4
where the time goes:
time: 405 us; the launch traced here: 404 us
  waiting for transfers between devices  294 us (73%)
  matrix products  30.3 us (7%)
  blocking collectives  20.7 us (5%)
  starting transfers between devices  19.7 us (5%)
  local copies, waits for them, and re-layouts  14.6 us (4%)
  between operations  14.3 us (4%)
  other arithmetic  10.8 us (3%)
    reduce_scatter x1, waiting for transfers between devices, local(): lax.psum_scatter(jnp.einsum('sic,sjc->jsi', applied, piece), 'dp', scatte...  82.6 us
    all_gather x2, waiting for transfers between devices, on_gathered_pieces(): blocks = [lax.all_gather(piece, axis) for piece in pieces]  59.8 us
    all_gather x1, waiting for transfers between devices, local(): gathered = lax.all_gather(col_piece, 'dp', axis=2, tiled=True)  46 us
    all_gather x1, waiting for transfers between devices, local(): full_left = lax.all_gather(left_eigen_basis, 'dp', axis=2, tiled=True)  45.1 us
    reduce_scatter x1, waiting for transfers between devices, local(): lax.psum_scatter(partial_terms.astype(jnp.bfloat16), 'dp', scatter_dimens...  32.2 us
    all_to_all x1, blocking collectives, local(): lax.all_to_all(leaving, 'fsdp', split_axis=0, concat_axis=0, tiled=True)  20.7 us
    all_to_all x1, waiting for transfers between devices, local(): lax.all_to_all(split_band, 'fsdp', split_axis=0, concat_axis=0, tiled=True)  11.3 us
    all_to_all x1, waiting for transfers between devices, local(): lax.all_to_all(parted, 'fsdp', split_axis=0, concat_axis=0, tiled=True)  11.1 us
  transfers between devices with their start and end apart: 9, of which 9 were waited for; matrix products, arithmetic and copies ran while one was open for 6% of the time, Pallas kernels for 0%

commit v1 on v0

v1 whole, which is shorter than its diff:
```python
import jax
import jax.numpy as jnp
from jax import lax
from jax.sharding import Mesh, PartitionSpec as P

BF = jnp.bfloat16
F32 = jnp.float32


def shift(x, by, n):
    return lax.ppermute(x, "dp", [(i, (i + by) % n) for i in range(n)])


def place(parts, me, n):
    width = parts[0].shape[-1]
    own, left, right, across = parts
    out = jnp.zeros(own.shape[:-1] + (n * width,), own.dtype)
    for piece, by in ((own, 0), (left, n - 1), (right, 1), (across, 2)):
        at = lax.rem(me + by, n) * width
        out = lax.dynamic_update_slice_in_dim(out, piece, at, out.ndim - 1)
    return out


def gather_columns(x, me, n):
    left = shift(x, 1, n)
    right = shift(x, n - 1, n)
    a = shift(left[0], 1, n)
    b = shift(right[1], n - 1, n)
    across = jnp.stack([a, b])
    return place((x, left, right, across), me, n)


def slot_tables(owner, cell, slot_count, per_owner):
    ids = jnp.arange(owner.shape[0], dtype=jnp.int32)
    shared = (owner[:, None] == owner[None, :]) & (ids[None, :] < ids[:, None])
    rank = jnp.sum(shared.astype(jnp.int32), axis=1)
    block_slot = owner * per_owner + rank
    slot_ids = jnp.arange(slot_count, dtype=jnp.int32)
    match = (block_slot[None, :] == slot_ids[:, None]).astype(jnp.int32)
    filled = jnp.sum(match, axis=1)
    slot_cell = jnp.sum(match * cell[None, :], axis=1)
    cells = jnp.arange(owner.shape[0], dtype=jnp.int32)
    hit = (cell[None, :] == cells[:, None]).astype(jnp.int32)
    cell_slot = jnp.sum(hit * block_slot[None, :], axis=1)
    return filled, slot_cell, cell_slot


def local(gradient, owner, cell, left_basis, right_basis, left_stat, right_stat, first, second):
    n = lax.axis_size("dp")
    me = lax.axis_index("dp")
    grid_rows = lax.axis_size("gr")
    bands = lax.axis_size("band")
    members = grid_rows * bands
    per_owner, block, width = left_basis.shape
    band_rows, grid_cols = gradient.shape[1], gradient.shape[2]
    piece = band_rows // grid_rows
    slot_count = per_owner * members
    half = band_rows // 2
    g = gradient[0]

    def chunk(by):
        return lax.dynamic_slice_in_dim(g, lax.rem(me + by, n) * width, width, 2)

    def added(x, y):
        return (x.astype(F32) + y.astype(F32)).astype(BF)

    filled, slot_cell, cell_slot = slot_tables(owner, cell, slot_count, per_owner)
    across = chunk(2)
    from_left = shift(across[:half], 1, n)
    from_right = shift(across[half:], n - 1, n)
    to_right, to_left = chunk(1), chunk(n - 1)
    to_right = jnp.concatenate([added(to_right[:half], from_left), to_right[half:]])
    to_left = jnp.concatenate([to_left[:half], added(to_left[half:], from_right)])
    in_left = shift(to_right, 1, n)
    in_right = shift(to_left, n - 1, n)
    summed = (chunk(0).astype(F32) + in_left.astype(F32) + in_right.astype(F32)).astype(BF)

    left_bf, summed = lax.optimization_barrier((left_basis.astype(BF), summed))
    right_bf = right_basis.astype(BF)
    full_left = gather_columns(left_bf, me, n)

    spread = lax.all_to_all(
        summed.reshape(grid_rows, piece, grid_cols, width), "gr", 0, 0, tiled=True
    )
    by_cell = jnp.transpose(spread, (0, 2, 1, 3)).reshape(grid_rows * grid_cols, piece, width)
    leaving = jnp.take(by_cell, slot_cell, axis=0)
    leaving = jnp.where((filled > 0)[:, None, None], leaving, jnp.zeros_like(leaving))
    landed = lax.all_to_all(
        leaving.reshape(members, per_owner, piece, width), ("gr", "band"), 0, 0, tiled=True
    )
    landed = landed.reshape(grid_rows, bands, per_owner, piece, width)
    mine = jnp.transpose(landed, (2, 1, 0, 3, 4)).reshape(per_owner, block, width)
    grad = gather_columns(mine, me, n)

    z = jnp.einsum("sij,sjc->sic", grad, right_bf, preferred_element_type=F32).astype(BF)
    turned = jnp.einsum("sik,sic->skc", full_left, z, preferred_element_type=F32)
    new_first = 0.9 * first + 0.1 * turned
    new_second = 0.999 * second + 0.001 * turned * turned
    direction = (new_first / (jnp.sqrt(new_second) + 1e-8)).astype(BF)
    applied = jnp.einsum("sik,skc->sic", full_left, direction, preferred_element_type=F32).astype(BF)

    def partial(by):
        rows = lax.dynamic_slice_in_dim(right_bf, lax.rem(me + by, n) * width, width, 1)
        return jnp.einsum("sic,sjc->sij", applied, rows, preferred_element_type=F32)

    across = partial(2).astype(BF)
    from_left = shift(across[0], 1, n)
    from_right = shift(across[1], n - 1, n)
    to_right, to_left = partial(1), partial(n - 1)
    to_right = jnp.stack([(to_right[0] + from_left.astype(F32)).astype(BF), to_right[1].astype(BF)])
    to_left = jnp.stack([to_left[0].astype(BF), (to_left[1] + from_right.astype(F32)).astype(BF)])
    in_left = shift(to_right, 1, n)
    in_right = shift(to_left, n - 1, n)
    back = (partial(0) + in_left.astype(F32) + in_right.astype(F32)).astype(BF)

    parted = back.reshape(per_owner, bands, grid_rows, piece, width)
    parted = jnp.transpose(parted, (2, 1, 0, 3, 4)).reshape(members, per_owner, piece, width)
    homed = lax.all_to_all(parted, ("gr", "band"), 0, 0, tiled=True)
    homed = homed.reshape(slot_count, piece, width)
    per_cell = jnp.take(homed, cell_slot, axis=0).reshape(grid_rows, grid_cols, piece, width)
    final = lax.all_to_all(per_cell, "gr", 0, 0, tiled=True)
    update = jnp.transpose(final, (0, 2, 1, 3)).reshape(band_rows, grid_cols, width)

    rows = lax.dynamic_slice_in_dim(grad, me * width, width, 1)
    new_left = 0.95 * left_stat + 0.05 * jnp.einsum(
        "sik,sjk->sij", grad, rows, preferred_element_type=F32
    )
    new_right = 0.95 * right_stat + 0.05 * jnp.einsum(
        "ski,skj->sij", grad, mine, preferred_element_type=F32
    )
    return new_left, new_right, new_first, new_second, update


def solution(mesh):
    n, members = mesh.shape["dp"], mesh.shape["fsdp"]

    def run(gradient, owner, cell, *state):
        bands = state[0].shape[1] // (gradient.shape[1] // members)
        inner = Mesh(mesh.devices.reshape(n, members // bands, bands), ("dp", "gr", "band"))
        fsdp = ("gr", "band")
        part = P(fsdp, None, "dp")
        f = jax.shard_map(
            local,
            mesh=inner,
            in_specs=(P("dp", fsdp, None, None), P(), P()) + (part,) * 6,
            out_specs=(part,) * 5,
            check_vma=False,
        )
        return f(gradient, owner, cell, *state)

    return run
```

time: 405 us -> 222 us (0.55)
  waiting for transfers between devices: 294 us -> 112 us
  starting transfers between devices: 19.7 us -> 51.3 us
  blocking collectives: 20.7 us -> 0 us
  between operations: 14.3 us -> 0.98 us
    all_gather x4 -> x0, waiting for transfers between devices: 151 us -> none  [the longest x2 59.8 us: on_gathered_pieces(): blocks = [lax.all_gather(piece, axis) for piece in pieces]]
    reduce_scatter x2 -> x0, waiting for transfers between devices: 115 us -> none  [the longest x1 82.6 us: local(): lax.psum_scatter(jnp.einsum('sic,sjc->jsi', applied, piece), 'dp', scatte...]
    ppermute x0 -> x16, waiting for transfers between devices: none -> 75.7 us  [shift(): return lax.ppermute(x, 'dp', [(i, (i + by) % n) for i in range(n)])]
    ppermute x0 -> x16, starting transfers between devices: none -> 23.7 us  [shift(): return lax.ppermute(x, 'dp', [(i, (i + by) % n) for i in range(n)])]
    all_to_all x1 -> x0, blocking collectives: 20.7 us -> none  [local(): lax.all_to_all(leaving, 'fsdp', split_axis=0, concat_axis=0, tiled=True)]
    all_to_all x3 -> x4, starting transfers between devices: 19.5 us -> 27.6 us  [the longest x1 9.69 us: local(): homed = lax.all_to_all(parted, ('gr', 'band'), 0, 0, tiled=True)]
    all_to_all x3 -> x4, waiting for transfers between devices: 27.9 us -> 35.8 us  [the longest x1 14.1 us: local(): lax.all_to_all(leaving.reshape(members, per_owner, piece, width), ('gr',...]
    dynamic_update_slice x0 -> x6, local copies, waits for them, and re-layouts: none -> 6.61 us  [place(): out = lax.dynamic_update_slice_in_dim(out, piece, at, out.ndim - 1)]
  transfers between devices with their start and end apart: 9 -> 20, of which waited for: 9 -> 13; matrix products, arithmetic and copies ran while one was open for 6% -> 13% of each run, Pallas kernels for 0% -> 0%
where the time goes in v1:
time: 222 us; the launch traced here: 221 us
  waiting for transfers between devices  112 us (50%)
  starting transfers between devices  51.3 us (23%)
  matrix products  27.3 us (12%)
  local copies, waits for them, and re-layouts  17.7 us (8%)
  other arithmetic  12.3 us (6%)
    ppermute x16, waiting for transfers between devices, shift(): return lax.ppermute(x, 'dp', [(i, (i + by) % n) for i in range(n)])  75.7 us
    ppermute x16, starting transfers between devices, shift(): return lax.ppermute(x, 'dp', [(i, (i + by) % n) for i in range(n)])  23.7 us
    all_to_all x1, waiting for transfers between devices, local(): lax.all_to_all(leaving.reshape(members, per_owner, piece, width), ('gr',...  14.1 us
    all_to_all x1, waiting for transfers between devices, local(): homed = lax.all_to_all(parted, ('gr', 'band'), 0, 0, tiled=True)  11 us
    all_to_all x1, starting transfers between devices, local(): homed = lax.all_to_all(parted, ('gr', 'band'), 0, 0, tiled=True)  9.69 us
    dot_general x1, matrix products, local(): jnp.einsum('sik,sic->skc', full_left, z, preferred_element_type=F32)  9.38 us
    all_to_all x1, starting transfers between devices, local(): lax.all_to_all(leaving.reshape(members, per_owner, piece, width), ('gr',...  9.04 us
    all_to_all x1, waiting for transfers between devices, local(): lax.all_to_all(summed.reshape(grid_rows, piece, grid_cols, width), 'gr',...  6.68 us
  transfers between devices with their start and end apart: 20, of which 13 were waited for; matrix products, arithmetic and copies ran while one was open for 13% of the time, Pallas kernels for 0%

profile of v1, /device:TPU:1, one launch (start us, length us, event | category | flops | bytes accessed | tf_op | source)
XLA Modules:
  0.0 221.1 jit_solution(1625765978804174639)
XLA Ops:
  8.9 2.9 %collective-permute-done = bf16[64,8,256]{2,1,0:T(8,128)(2,1)S(1)} collective-permute-done((bf16[64,8,256]{2,1,0:T(8,128)(2,1)}, bf16[64,8,256]{2,1,0:T(8,128)(2,1)S(1)}, u32[]{:S(2)}, u32[]{:S(2)}) %collective-permute-start) | collective-permute-done | bytes 262176 | tf_op jit(solution)/shard_map/ppermute | solution.py:11
  15.0 10.2 %collective-permute-done.1 = bf16[128,8,256]{2,1,0:T(8,128)(2,1)S(1)} collective-permute-done((bf16[128,8,256]{2,1,0:T(8,128)(2,1)S(1)}, bf16[128,8,256]{2,1,0:T(8,128)(2,1)S(1)}, u32[]{:S(2)}, u32[]{:S(2)}) %collective-permute-start.1) | collective-permute-done | bytes 524320 | tf_op jit(solution)/shard_map/ppermute | solution.py:11
  26.2 5.4 %all-to-all-start = ((bf16[4,32,8,256]{3,2,1,0:T(8,128)(2,1)}), bf16[4,32,8,256]{3,2,1,0:T(8,128)(2,1)S(1)}, u32[]{:S(2)}, u32[]{:S(2)}) async-start(bf16[4,32,8,256]{3,2,1,0:T(8,128)(2,1)} %bitcast.7), calls=%async_computation | async-start | bytes 1048576 | tf_op jit(solution)/shard_map/all_to_all | solution.py:82
  31.9 6.7 %all-to-all-done = bf16[4,32,8,256]{3,2,1,0:T(8,128)(2,1)S(1)} async-done(((bf16[4,32,8,256]{3,2,1,0:T(8,128)(2,1)}), bf16[4,32,8,256]{3,2,1,0:T(8,128)(2,1)S(1)}, u32[]{:S(2)}, u32[]{:S(2)}) %all-to-all-start) | async-done | bytes 524320 | tf_op jit(solution)/shard_map/all_to_all | solution.py:82
  40.5 9.0 %all-to-all-start.1 = ((bf16[32,2,32,256]{3,2,1,0:T(8,128)(2,1)}), bf16[32,2,32,256]{3,2,1,0:T(8,128)(2,1)S(1)}, u32[]{:S(2)}, u32[]{:S(2)}) async-start(bf16[32,2,32,256]{3,2,1,0:T(8,128)(2,1)} %select_select_fusion), calls=%async_computation.1 | async-start | bytes 2097152 | tf_op jit(solution)/shard_map/all_to_all | solution.py:88
  52.5 14.1 %all-to-all-done.1 = bf16[32,2,32,256]{3,2,1,0:T(8,128)(2,1)S(1)} async-done(((bf16[32,2,32,256]{3,2,1,0:T(8,128)(2,1)}), bf16[32,2,32,256]{3,2,1,0:T(8,128)(2,1)S(1)}, u32[]{:S(2)}, u32[]{:S(2)}) %all-to-all-start.1) | async-done | bytes 1048608 | tf_op jit(solution)/shard_map/all_to_all | solution.py:88
  68.3 2.8 %collective-permute-start.5 = (bf16[2,1024,256]{2,1,0:T(8,128)(2,1)S(1)}, bf16[2,1024,256]{2,1,0:T(8,128)(2,1)S(1)}, u32[]{:S(2)}, u32[]{:S(2)}) collective-permute-start(bf16[2,1024,256]{2,1,0:T(8,128)(2,1)S(1)} %bitcast.93), channel_id=1, source_target_pairs={{0,96},{32,0},{64,32},{96,64},{1,97},{33,1},{65,33},{97,65},{2,98}... | collective-permute-start | bytes 3145736 | tf_op jit(solution)/shard_map/ppermute | solution.py:11
  73.0 2.7 %collective-permute-done.8 = bf16[2,1024,256]{2,1,0:T(8,128)(2,1)S(1)} collective-permute-done((bf16[2,1024,256]{2,1,0:T(8,128)(2,1)}, bf16[2,1024,256]{2,1,0:T(8,128)(2,1)S(1)}, u32[]{:S(2)}, u32[]{:S(2)}) %collective-permute-start.8) | collective-permute-done | bytes 1048608 | tf_op jit(solution)/shard_map/ppermute | solution.py:11
  76.9 2.7 %collective-permute-start.11 = (bf16[1024,256]{1,0:T(8,128)(2,1)S(1)}, bf16[1024,256]{1,0:T(8,128)(2,1)S(1)}, u32[]{:S(2)}, u32[]{:S(2)}) collective-permute-start(bf16[1024,256]{1,0:T(8,128)(2,1)S(1)} %slice_bitcast_fusion.4), channel_id=1, source_target_pairs={{0,96},{32,0},{64,32},{96,64},{1,97},{33,1},{65,33},{97,65},{2,98}... | collective-permute-start | bytes 1572872 | tf_op jit(solution)/shard_map/ppermute | solution.py:11
  81.2 17.0 %collective-permute-done.4 = bf16[2,1024,256]{2,1,0:T(8,128)(2,1)S(1)} collective-permute-done((bf16[2,1024,256]{2,1,0:T(8,128)(2,1)S(1)}, bf16[2,1024,256]{2,1,0:T(8,128)(2,1)S(1)}, u32[]{:S(2)}, u32[]{:S(2)}) %collective-permute-start.4) | collective-permute-done | bytes 1048608 | tf_op jit(solution)/shard_map/ppermute | solution.py:11
  98.4 2.9 %collective-permute-start.7 = (bf16[1024,256]{1,0:T(8,128)(2,1)S(1)}, bf16[1024,256]{1,0:T(8,128)(2,1)S(1)}, u32[]{:S(2)}, u32[]{:S(2)}) collective-permute-start(bf16[1024,256]{1,0:T(8,128)(2,1)S(1)} %slice_bitcast_fusion.6), channel_id=1, source_target_pairs={{0,96},{32,0},{64,32},{96,64},{1,97},{33,1},{65,33},{97,65},{2,98}... | collective-permute-start | bytes 1572872 | tf_op jit(solution)/shard_map/ppermute | solution.py:11
  104.9 4.5 %collective-permute-done.10 = bf16[1024,256]{1,0:T(8,128)(2,1)S(1)} collective-permute-done((bf16[1024,256]{1,0:T(8,128)(2,1)S(1)}, bf16[1024,256]{1,0:T(8,128)(2,1)S(1)}, u32[]{:S(2)}, u32[]{:S(2)}) %collective-permute-start.10) | collective-permute-done | bytes 524320 | tf_op jit(solution)/shard_map/ppermute | solution.py:11
  112.2 8.4 %collective-permute-done.6 = bf16[1024,256]{1,0:T(8,128)(2,1)S(1)} collective-permute-done((bf16[1024,256]{1,0:T(8,128)(2,1)S(1)}, bf16[1024,256]{1,0:T(8,128)(2,1)S(1)}, u32[]{:S(2)}, u32[]{:S(2)}) %collective-permute-start.6) | collective-permute-done | bytes 524320 | tf_op jit(solution)/shard_map/ppermute | solution.py:11
  121.8 9.4 %fusion = (f32[2,1024,256]{2,1,0:T(8,128)}, f32[2,1024,256]{2,1,0:T(8,128)}) fusion(f32[2,1024,256]{2,1,0:T(8,128)} %param.17, f32[2,1024,256]{2,1,0:T(8,128)} %param.16, bf16[2,1024,1024]{2,1,0:T(8,128)(2,1)} %copy-done, bf16[2,1024,1024]{2,1,0:T(8,128)(2,1)} %maximum_dynamic-update-slice_fusion, bf16[2,1024,256]{2,1,0:T(8,128)(2,1)S(1)} %convert_element_type.105), kind=kOutput, calls=%fused_computation.3 | convolution fusion | flops 2151677952 | bytes 17825792 | tf_op jit(solution)/shard_map/sik,sic->skc/dot_general | solution.py:96
  131.2 4.8 %convolution_convert_fusion.1 = bf16[2,1024,256]{2,1,0:T(8,128)(2,1)S(1)} fusion(bf16[2,1024,1024]{2,1,0:T(8,128)(2,1)} %copy-done, f32[2,1024,256]{2,1,0:T(8,128)} %get-tuple-element.12, f32[2,1024,256]{2,1,0:T(8,128)} %get-tuple-element.11), kind=kOutput, calls=%fused_computation.10 | convolution fusion | flops 1075838976 | bytes 9437184 | tf_op jit(solution)/shard_map/sik,skc->sic/dot_general | solution.py:100
  140.4 9.9 %collective-permute-done.12 = bf16[1024,256]{1,0:T(8,128)(2,1)S(1)} collective-permute-done((bf16[1024,256]{1,0:T(8,128)(2,1)S(1)}, bf16[1024,256]{1,0:T(8,128)(2,1)S(1)}, u32[]{:S(2)}, u32[]{:S(2)}) %collective-permute-start.12) | collective-permute-done | bytes 524320 | tf_op jit(solution)/shard_map/ppermute | solution.py:11
  152.7 2.7 %collective-permute-start.15 = (bf16[2,1024,256]{2,1,0:T(8,128)(2,1)}, bf16[2,1024,256]{2,1,0:T(8,128)(2,1)}, u32[]{:S(2)}, u32[]{:S(2)}) collective-permute-start(bf16[2,1024,256]{2,1,0:T(8,128)(2,1)} %pad_maximum_fusion.1), channel_id=1, source_target_pairs={{0,96},{32,0},{64,32},{96,64},{1,97},{33,1},{65,33},{97,65},{2,98}... | collective-permute-start | bytes 3145736 | tf_op jit(solution)/shard_map/ppermute | solution.py:11
  156.1 19.8 %collective-permute-done.13 = bf16[2,1024,256]{2,1,0:T(8,128)(2,1)} collective-permute-done((bf16[2,1024,256]{2,1,0:T(8,128)(2,1)}, bf16[2,1024,256]{2,1,0:T(8,128)(2,1)}, u32[]{:S(2)}, u32[]{:S(2)}) %collective-permute-start.13) | collective-permute-done | bytes 1048608 | tf_op jit(solution)/shard_map/ppermute | solution.py:11
  179.1 9.7 %all-to-all-start.2 = ((bf16[32,2,32,256]{3,2,1,0:T(8,128)(2,1)}), bf16[32,2,32,256]{3,2,1,0:T(8,128)(2,1)S(1)}, u32[]{:S(2)}, u32[]{:S(2)}) async-start(bf16[32,2,32,256]{3,2,1,0:T(8,128)(2,1)} %bitcast.32), calls=%async_computation.2 | async-start | bytes 2097152 | tf_op jit(solution)/shard_map/all_to_all | solution.py:118
  188.9 6.0 %multiply_add_fusion.1 = f32[2,1024,256]{2,1,0:T(8,128)} fusion(f32[2,1024,256]{2,1,0:T(8,128)} %param.15, bf16[2,1024,1024]{2,1,0:T(8,128)(2,1)} %maximum_dynamic-update-slice_fusion, bf16[2,1024,256]{2,1,0:T(8,128)(2,1)S(1)} %bitcast.95), kind=kOutput, calls=%fused_computation.7 | convolution fusion | flops 1075314688 | bytes 9437184 | tf_op jit(solution)/shard_map/ski,skj->sij/dot_general | solution.py:128
  194.9 11.0 %all-to-all-done.2 = bf16[32,2,32,256]{3,2,1,0:T(8,128)(2,1)S(1)} async-done(((bf16[32,2,32,256]{3,2,1,0:T(8,128)(2,1)}), bf16[32,2,32,256]{3,2,1,0:T(8,128)(2,1)S(1)}, u32[]{:S(2)}, u32[]{:S(2)}) %all-to-all-start.2) | async-done | bytes 1048608 | tf_op jit(solution)/shard_map/all_to_all | solution.py:118
  207.4 3.5 %all-to-all-start.3 = ((bf16[4,8,32,256]{3,2,1,0:T(8,128)(2,1)}), bf16[4,8,32,256]{3,2,1,0:T(8,128)(2,1)S(1)}, u32[]{:S(2)}, u32[]{:S(2)}) async-start(bf16[4,8,32,256]{3,2,1,0:T(8,128)(2,1)} %broadcast_select_fusion), calls=%async_computation.3 | async-start | bytes 1048576 | tf_op jit(solution)/shard_map/all_to_all | solution.py:121
  210.9 5.2 %multiply_add_fusion.2 = f32[2,1024,256]{2,1,0:T(8,128)} fusion(f32[2,1024,256]{2,1,0:T(8,128)S(1)} %copy-done.4, bf16[2,1024,1024]{2,1,0:T(8,128)(2,1)} %maximum_dynamic-update-slice_fusion, s32[]{:T(128)S(6)} %select_n.84), kind=kOutput, calls=%fused_computation.8 | convolution fusion | flops 1075314688 | bytes 9437188 | tf_op jit(solution)/shard_map/sik,sjk->sij/dot_general | solution.py:125
  216.1 3.9 %all-to-all-done.3 = bf16[4,8,32,256]{3,2,1,0:T(8,128)(2,1)S(1)} async-done(((bf16[4,8,32,256]{3,2,1,0:T(8,128)(2,1)}), bf16[4,8,32,256]{3,2,1,0:T(8,128)(2,1)S(1)}, u32[]{:S(2)}, u32[]{:S(2)}) %all-to-all-start.3) | async-done | bytes 524320 | tf_op jit(solution)/shard_map/all_to_all | solution.py:121
  (87 shorter events, 44.7 us)
Async XLA Ops:
  2.6 6.0 %copy-start.5 = (s32[32]{0:T(128)S(1)}, s32[32]{0:T(128)}, u32[]{:S(2)}) copy-start(s32[32]{0:T(128)} %param.10) | copy-start | bytes 388
  2.6 9.2 %copy-start.1 = (bf16[1,128,8,1024]{3,2,1,0:T(8,128)(2,1)S(1)}, bf16[1,128,8,1024]{3,2,1,0:T(8,128)(2,1)}, u32[]{:S(2)}) copy-start(bf16[1,128,8,1024]{3,2,1,0:T(8,128)(2,1)} %param.9) | copy-start | bytes 6291460
  2.6 9.1 %collective-permute-start = (bf16[64,8,256]{2,1,0:T(8,128)(2,1)}, bf16[64,8,256]{2,1,0:T(8,128)(2,1)S(1)}, u32[]{:S(2)}, u32[]{:S(2)}) collective-permute-start(bf16[64,8,256]{2,1,0:T(8,128)(2,1)} %get-tuple-element.15), channel_id=1, source_target_pairs={{0,32},{32,64},{64,96},{96,0},{1,33},{33,65},{65,97},{97,1},{2,34}... | collective-permute-start | bytes 786440 | tf_op jit(solution)/shard_map/ppermute | solution.py:11
  4.7 7.1 %collective-permute-start.2 = (bf16[64,8,256]{2,1,0:T(8,128)(2,1)S(1)}, bf16[64,8,256]{2,1,0:T(8,128)(2,1)S(1)}, u32[]{:S(2)}, u32[]{:S(2)}) collective-permute-start(bf16[64,8,256]{2,1,0:T(8,128)(2,1)S(1)} %get-tuple-element.18), channel_id=1, source_target_pairs={{0,96},{32,0},{64,32},{96,64},{1,97},{33,1},{65,33},{97,65},{2,98}... | collective-permute-start | bytes 786440 | tf_op jit(solution)/shard_map/ppermute | solution.py:11
  8.7 6.3 %copy-start.3 = (s32[32]{0:T(128)S(1)}, s32[32]{0:T(128)}, u32[]{:S(2)}) copy-start(s32[32]{0:T(128)} %param.11) | copy-start | bytes 388
  12.1 13.1 %collective-permute-start.1 = (bf16[128,8,256]{2,1,0:T(8,128)(2,1)S(1)}, bf16[128,8,256]{2,1,0:T(8,128)(2,1)S(1)}, u32[]{:S(2)}, u32[]{:S(2)}) collective-permute-start(bf16[128,8,256]{2,1,0:T(8,128)(2,1)S(1)} %pad_maximum_fusion.2), channel_id=1, source_target_pairs={{0,32},{32,64},{64,96},{96,0},{1,33},{33,65},{65,97},{97,1},{2,34}... | collective-permute-start | bytes 1572872 | tf_op jit(solution)/shard_map/ppermute | solution.py:11
  13.2 12.0 %collective-permute-start.3 = (bf16[128,8,256]{2,1,0:T(8,128)(2,1)S(1)}, bf16[128,8,256]{2,1,0:T(8,128)(2,1)S(1)}, u32[]{:S(2)}, u32[]{:S(2)}) collective-permute-start(bf16[128,8,256]{2,1,0:T(8,128)(2,1)S(1)} %pad_maximum_fusion.3), channel_id=1, source_target_pairs={{0,96},{32,0},{64,32},{96,64},{1,97},{33,1},{65,33},{97,65},{2,98}... | collective-permute-start | bytes 1572872 | tf_op jit(solution)/shard_map/ppermute | solution.py:11
  26.2 12.3 %all-to-all-start = ((bf16[4,32,8,256]{3,2,1,0:T(8,128)(2,1)}), bf16[4,32,8,256]{3,2,1,0:T(8,128)(2,1)S(1)}, u32[]{:S(2)}, u32[]{:S(2)}) async-start(bf16[4,32,8,256]{3,2,1,0:T(8,128)(2,1)} %bitcast.7), calls=%async_computation | async-start | bytes 1048576 | tf_op jit(solution)/shard_map/all_to_all | solution.py:82
  40.5 26.1 %all-to-all-start.1 = ((bf16[32,2,32,256]{3,2,1,0:T(8,128)(2,1)}), bf16[32,2,32,256]{3,2,1,0:T(8,128)(2,1)S(1)}, u32[]{:S(2)}, u32[]{:S(2)}) async-start(bf16[32,2,32,256]{3,2,1,0:T(8,128)(2,1)} %select_select_fusion), calls=%async_computation.1 | async-start | bytes 2097152 | tf_op jit(solution)/shard_map/all_to_all | solution.py:88
  49.6 26.1 %collective-permute-start.8 = (bf16[2,1024,256]{2,1,0:T(8,128)(2,1)}, bf16[2,1024,256]{2,1,0:T(8,128)(2,1)S(1)}, u32[]{:S(2)}, u32[]{:S(2)}) collective-permute-start(bf16[2,1024,256]{2,1,0:T(8,128)(2,1)} %convert_element_type.91), channel_id=1, source_target_pairs={{0,32},{32,64},{64,96},{96,0},{1,33},{33,65},{65,97},{97,1},{2,34}... | collective-permute-start | bytes 3145736 | tf_op jit(solution)/shard_map/ppermute | solution.py:11
  50.2 25.7 %collective-permute-start.9 = (bf16[2,1024,256]{2,1,0:T(8,128)(2,1)}, bf16[2,1024,256]{2,1,0:T(8,128)(2,1)}, u32[]{:S(2)}, u32[]{:S(2)}) collective-permute-start(bf16[2,1024,256]{2,1,0:T(8,128)(2,1)} %convert_element_type.91), channel_id=1, source_target_pairs={{0,96},{32,0},{64,32},{96,64},{1,97},{33,1},{65,33},{97,65},{2,98}... | collective-permute-start | bytes 3145736 | tf_op jit(solution)/shard_map/ppermute | solution.py:11
  66.7 31.5 %collective-permute-start.4 = (bf16[2,1024,256]{2,1,0:T(8,128)(2,1)S(1)}, bf16[2,1024,256]{2,1,0:T(8,128)(2,1)S(1)}, u32[]{:S(2)}, u32[]{:S(2)}) collective-permute-start(bf16[2,1024,256]{2,1,0:T(8,128)(2,1)S(1)} %bitcast.92), channel_id=1, source_target_pairs={{0,32},{32,64},{64,96},{96,0},{1,33},{33,65},{65,97},{97,1},{2,34}... | collective-permute-start | bytes 3145736 | tf_op jit(solution)/shard_map/ppermute | solution.py:11
  68.3 30.0 %collective-permute-start.5 = (bf16[2,1024,256]{2,1,0:T(8,128)(2,1)S(1)}, bf16[2,1024,256]{2,1,0:T(8,128)(2,1)S(1)}, u32[]{:S(2)}, u32[]{:S(2)}) collective-permute-start(bf16[2,1024,256]{2,1,0:T(8,128)(2,1)S(1)} %bitcast.93), channel_id=1, source_target_pairs={{0,96},{32,0},{64,32},{96,64},{1,97},{33,1},{65,33},{97,65},{2,98}... | collective-permute-start | bytes 3145736 | tf_op jit(solution)/shard_map/ppermute | solution.py:11
  75.7 33.7 %collective-permute-start.10 = (bf16[1024,256]{1,0:T(8,128)(2,1)S(1)}, bf16[1024,256]{1,0:T(8,128)(2,1)S(1)}, u32[]{:S(2)}, u32[]{:S(2)}) collective-permute-start(bf16[1024,256]{1,0:T(8,128)(2,1)S(1)} %slice_bitcast_fusion.5), channel_id=1, source_target_pairs={{0,32},{32,64},{64,96},{96,0},{1,33},{33,65},{65,97},{97,1},{2,34}... | collective-permute-start | bytes 1572872 | tf_op jit(solution)/shard_map/ppermute | solution.py:11
  76.9 32.5 %collective-permute-start.11 = (bf16[1024,256]{1,0:T(8,128)(2,1)S(1)}, bf16[1024,256]{1,0:T(8,128)(2,1)S(1)}, u32[]{:S(2)}, u32[]{:S(2)}) collective-permute-start(bf16[1024,256]{1,0:T(8,128)(2,1)S(1)} %slice_bitcast_fusion.4), channel_id=1, source_target_pairs={{0,96},{32,0},{64,32},{96,64},{1,97},{33,1},{65,33},{97,65},{2,98}... | collective-permute-start | bytes 1572872 | tf_op jit(solution)/shard_map/ppermute | solution.py:11
  98.2 22.4 %collective-permute-start.6 = (bf16[1024,256]{1,0:T(8,128)(2,1)S(1)}, bf16[1024,256]{1,0:T(8,128)(2,1)S(1)}, u32[]{:S(2)}, u32[]{:S(2)}) collective-permute-start(bf16[1024,256]{1,0:T(8,128)(2,1)S(1)} %slice_bitcast_fusion.7), channel_id=1, source_target_pairs={{0,32},{32,64},{64,96},{96,0},{1,33},{33,65},{65,97},{97,1},{2,34}... | collective-permute-start | bytes 1572872 | tf_op jit(solution)/shard_map/ppermute | solution.py:11
  98.4 22.3 %collective-permute-start.7 = (bf16[1024,256]{1,0:T(8,128)(2,1)S(1)}, bf16[1024,256]{1,0:T(8,128)(2,1)S(1)}, u32[]{:S(2)}, u32[]{:S(2)}) collective-permute-start(bf16[1024,256]{1,0:T(8,128)(2,1)S(1)} %slice_bitcast_fusion.6), channel_id=1, source_target_pairs={{0,96},{32,0},{64,32},{96,64},{1,97},{33,1},{65,33},{97,65},{2,98}... | collective-permute-start | bytes 1572872 | tf_op jit(solution)/shard_map/ppermute | solution.py:11
  136.6 13.8 %collective-permute-start.12 = (bf16[1024,256]{1,0:T(8,128)(2,1)S(1)}, bf16[1024,256]{1,0:T(8,128)(2,1)S(1)}, u32[]{:S(2)}, u32[]{:S(2)}) collective-permute-start(bf16[1024,256]{1,0:T(8,128)(2,1)S(1)} %get-tuple-element.19), channel_id=1, source_target_pairs={{0,32},{32,64},{64,96},{96,0},{1,33},{33,65},{65,97},{97,1},{2,34}... | collective-permute-start | bytes 1572872 | tf_op jit(solution)/shard_map/ppermute | solution.py:11
  137.5 14.0 %collective-permute-start.14 = (bf16[1024,256]{1,0:T(8,128)(2,1)S(1)}, bf16[1024,256]{1,0:T(8,128)(2,1)S(1)}, u32[]{:S(2)}, u32[]{:S(2)}) collective-permute-start(bf16[1024,256]{1,0:T(8,128)(2,1)S(1)} %get-tuple-element.20), channel_id=1, source_target_pairs={{0,96},{32,0},{64,32},{96,64},{1,97},{33,1},{65,33},{97,65},{2,98}... | collective-permute-start | bytes 1572872 | tf_op jit(solution)/shard_map/ppermute | solution.py:11
  151.5 24.4 %collective-permute-start.13 = (bf16[2,1024,256]{2,1,0:T(8,128)(2,1)}, bf16[2,1024,256]{2,1,0:T(8,128)(2,1)}, u32[]{:S(2)}, u32[]{:S(2)}) collective-permute-start(bf16[2,1024,256]{2,1,0:T(8,128)(2,1)} %pad_maximum_fusion), channel_id=1, source_target_pairs={{0,32},{32,64},{64,96},{96,0},{1,33},{33,65},{65,97},{97,1},{2,34}... | collective-permute-start | bytes 3145736 | tf_op jit(solution)/shard_map/ppermute | solution.py:11
  152.7 23.4 %collective-permute-start.15 = (bf16[2,1024,256]{2,1,0:T(8,128)(2,1)}, bf16[2,1024,256]{2,1,0:T(8,128)(2,1)}, u32[]{:S(2)}, u32[]{:S(2)}) collective-permute-start(bf16[2,1024,256]{2,1,0:T(8,128)(2,1)} %pad_maximum_fusion.1), channel_id=1, source_target_pairs={{0,96},{32,0},{64,32},{96,64},{1,97},{33,1},{65,33},{97,65},{2,98}... | collective-permute-start | bytes 3145736 | tf_op jit(solution)/shard_map/ppermute | solution.py:11
  179.1 26.8 %all-to-all-start.2 = ((bf16[32,2,32,256]{3,2,1,0:T(8,128)(2,1)}), bf16[32,2,32,256]{3,2,1,0:T(8,128)(2,1)S(1)}, u32[]{:S(2)}, u32[]{:S(2)}) async-start(bf16[32,2,32,256]{3,2,1,0:T(8,128)(2,1)} %bitcast.32), calls=%async_computation.2 | async-start | bytes 2097152 | tf_op jit(solution)/shard_map/all_to_all | solution.py:118
  206.5 4.4 %copy-start.4 = (f32[2,1024,256]{2,1,0:T(8,128)S(1)}, f32[2,1024,256]{2,1,0:T(8,128)}, u32[]{:S(2)}) copy-start(f32[2,1024,256]{2,1,0:T(8,128)} %param.14) | copy-start | bytes 6291460
  207.4 12.6 %all-to-all-start.3 = ((bf16[4,8,32,256]{3,2,1,0:T(8,128)(2,1)}), bf16[4,8,32,256]{3,2,1,0:T(8,128)(2,1)S(1)}, u32[]{:S(2)}, u32[]{:S(2)}) async-start(bf16[4,8,32,256]{3,2,1,0:T(8,128)(2,1)} %broadcast_select_fusion), calls=%async_computation.3 | async-start | bytes 1048576 | tf_op jit(solution)/shard_map/all_to_all | solution.py:121
  (2 other events, 4.2 us)

commit v2 on v1

v2 whole, which is shorter than its diff:
```python
import functools

import jax
import jax.numpy as jnp
from jax import lax
from jax.experimental import pallas as pl
from jax.experimental.pallas import tpu as pltpu
from jax.sharding import Mesh, PartitionSpec as P


BF = jnp.bfloat16
F32 = jnp.float32
TILE = 512
VMEM_TURN = 60 * 2**20


def shift(x, by, n):
    return lax.ppermute(x, "dp", [(i, (i + by) % n) for i in range(n)])


def dot(x, y, dims):
    return lax.dot_general(x, y, (dims, ((), ())), preferred_element_type=F32)


NN = ((1,), (0,))
NT = ((1,), (1,))
TN = ((0,), (0,))


def rows_at(me, by, n, size):
    return pl.ds(pl.multiple_of(lax.rem(me + by, n) * size, size), size)


def flip_kernel(*refs):
    ins, out, buf, res, sems, out_sems = refs[:4], *refs[4:]
    width = buf.shape[2]
    copies = []
    for k, ref in enumerate(ins):
        c = pltpu.make_async_copy(ref, buf.at[k], sems.at[k])
        c.start()
        copies.append(c)
    stores = []
    for k in range(4):
        copies[k].wait()
        res[k] = buf[k].T
        c = pltpu.make_async_copy(res.at[k], out.at[pl.ds(k * width, width)], out_sems.at[k])
        c.start()
        stores.append(c)
    for c in stores:
        c.wait()


def flip(lb):
    block, width = lb[0].shape
    anyspec = pl.BlockSpec(memory_space=pltpu.HBM)
    return pl.pallas_call(
        flip_kernel,
        out_shape=jax.ShapeDtypeStruct((block, block), BF),
        in_specs=[anyspec] * 4,
        out_specs=anyspec,
        scratch_shapes=[
            pltpu.VMEM((4, block, width), BF),
            pltpu.VMEM((4, width, block), BF),
            pltpu.SemaphoreType.DMA((4,)),
            pltpu.SemaphoreType.DMA((4,)),
        ],
        compiler_params=pltpu.CompilerParams(vmem_limit_bytes=VMEM_TURN),
        cost_estimate=pl.CostEstimate(flops=2**22, bytes_accessed=4 * 2**20, transcendentals=0),
        name="flip",
    )(*lb)


def turn_kernel(n, s, *refs):
    me_ref = refs[0]
    g_own, g_left, g_right, g_top, g_bottom = refs[1:6]
    l_parts, lt_hbm = refs[6:10], refs[10]
    r_hbm, first_hbm, second_hbm = refs[11:14]
    (nf_hbm, ns_hbm, g_out, own_out, far_t, far_b, right_t, right_b, left_t, left_b) = refs[-23:-13]
    g, lb, lt, r, first, second, z, d, t, p, sems, out_sems, _ = refs[-13:]
    me = me_ref[0]
    _, pieces, piece, block = g.shape
    width = z.shape[1]
    half = pieces // 2
    loads, stores = [], []

    def load(src, dst):
        c = pltpu.make_async_copy(src, dst, sems.at[len(loads)])
        c.start()
        loads.append(c)
        return c

    def store(src, dst):
        c = pltpu.make_async_copy(src, dst, out_sems.at[len(stores)])
        c.start()
        stores.append(c)

    def cols(k):
        return pl.ds(k * width, width)

    offsets = (0, n - 1, 1, 2)
    w_g = [
        load(r_hbm.at[s, rows_at(me, offsets[k], n, width), :], r.at[cols(k), :]) for k in range(4)
    ]
    for k, ref in enumerate((g_own, g_left, g_right)):
        w_g += [load(ref.at[q], g.at[:, q, :, cols(k)]) for q in range(pieces)]
    for q in range(half):
        w_g.append(load(g_top.at[q], g.at[:, q, :, cols(3)]))
        w_g.append(load(g_bottom.at[q], g.at[:, q + half, :, cols(3)]))
    w_lt = load(lt_hbm, lt)
    w_m = [load(first_hbm.at[s], first), load(second_hbm.at[s], second)]
    w_l = [load(ref, lb.at[:, cols(k)]) for k, ref in enumerate(l_parts)]

    per = TILE // (pieces * piece)
    tiles = block // TILE
    for c in w_g:
        c.wait()
    store(g, g_out)

    @pl.loop(0, tiles)
    def _(i):
        rows = g[pl.ds(i * per, per)].reshape(TILE, block)
        at = pl.ds(pl.multiple_of(i * TILE, TILE), TILE)
        z[at, :] = dot(rows, r[...], NN).astype(BF)

    w_lt.wait()
    for c in w_m:
        c.wait()
    for k in range(4):
        at = rows_at(me, offsets[k], n, width)
        turned = dot(lt[cols(k), :], z[...], NN)
        nf = 0.9 * first[at, :] + 0.1 * turned
        ns = 0.999 * second[at, :] + 0.001 * turned * turned
        first[at, :] = nf
        second[at, :] = ns
        d[cols(k), :] = (nf / (jnp.sqrt(ns) + 1e-8)).astype(BF)
    store(first, nf_hbm.at[s])
    store(second, ns_hbm.at[s])
    for c in w_l:
        c.wait()

    @pl.loop(0, tiles)
    def _(i):
        at = pl.ds(pl.multiple_of(i * TILE, TILE), TILE)
        t[at, :] = dot(lb[at, :], d[...], NN).astype(BF)

    for k in (3, 2, 1, 0):

        @pl.loop(0, tiles)
        def _(i):
            at = pl.ds(pl.multiple_of(i * TILE, TILE), TILE)
            v = dot(t[at, :], r[cols(k), :], NT).astype(BF)
            p[pl.ds(i * per, per), :, :, cols(k)] = v.reshape(per, pieces, piece, width)

        for q in range(pieces):
            src = p.at[:, q, :, cols(k)]
            if k == 0:
                store(src, own_out.at[q])
            else:
                top, bottom = {3: (far_t, far_b), 2: (right_t, right_b), 1: (left_t, left_b)}[k]
                store(src, top.at[q] if q < half else bottom.at[q - half])
    for c in stores:
        c.wait()


def turn(me, s, g, lb, lt, r, first, second, before, n):
    _, block, width = r.shape
    pieces, bands, piece, _ = g[0].shape
    anyspec = pl.BlockSpec(memory_space=pltpu.HBM)
    state = jax.ShapeDtypeStruct(first.shape, F32)
    whole = jax.ShapeDtypeStruct(g[0].shape, BF)
    part = jax.ShapeDtypeStruct(g[3].shape, BF)
    full = jax.ShapeDtypeStruct((bands, pieces, piece, block), BF)
    return pl.pallas_call(
        functools.partial(turn_kernel, n, s),
        out_shape=[state, state, full, whole] + [part] * 6,
        in_specs=[pl.BlockSpec(memory_space=pltpu.SMEM)] + [anyspec] * (13 + len(before)),
        out_specs=[anyspec] * 10,
        scratch_shapes=[
            pltpu.VMEM((bands, pieces, piece, block), BF),
            pltpu.VMEM((block, block), BF),
            pltpu.VMEM((block, block), BF),
            pltpu.VMEM((block, width), BF),
            pltpu.VMEM((block, width), F32),
            pltpu.VMEM((block, width), F32),
            pltpu.VMEM((block, width), BF),
            pltpu.VMEM((block, width), BF),
            pltpu.VMEM((block, width), BF),
            pltpu.VMEM((bands, pieces, piece, block), BF),
            pltpu.SemaphoreType.DMA((27,)),
            pltpu.SemaphoreType.DMA((19,)),
            pltpu.SMEM((1,), jnp.int32),
        ],
        input_output_aliases={14 + i: i for i in range(len(before))},
        compiler_params=pltpu.CompilerParams(vmem_limit_bytes=VMEM_TURN),
        cost_estimate=pl.CostEstimate(
            flops=8 * block * block * width, bytes_accessed=14 * 2**20, transcendentals=0
        ),
        name="turn",
    )(me, *g, *lb, lt, r, first, second, *before)


def stats_kernel(n, me_ref, g, lstat, rstat, *rest):
    new_l, new_r = rest[-2:]
    me = me_ref[0]
    block = g.shape[0]
    width = lstat.shape[2]

    @pl.loop(0, block // TILE)
    def _(i):
        at = pl.ds(pl.multiple_of(i * TILE, TILE), TILE)
        acc = dot(g[at, :], g[rows_at(me, 0, n, width), :], NT)
        new_l[0, at, :] = 0.95 * lstat[0, at, :] + 0.05 * acc

    for k, by in enumerate((0, n - 1, 1, 2)):
        at = rows_at(me, by, n, width)
        acc = dot(g[:, k * width : (k + 1) * width], g[:, :width], TN)
        new_r[0, at, :] = 0.95 * rstat[0, at, :] + 0.05 * acc


def stats(me, s, g, lstat, rstat, before, n):
    _, block, width = lstat.shape
    slot = pl.BlockSpec((1, block, width), lambda i: (s, 0, 0))
    anyspec = pl.BlockSpec(memory_space=pltpu.HBM)
    out = jax.ShapeDtypeStruct(lstat.shape, F32)
    return pl.pallas_call(
        functools.partial(stats_kernel, n),
        grid=(1,),
        out_shape=[out, out],
        in_specs=[
            pl.BlockSpec(memory_space=pltpu.SMEM),
            pl.BlockSpec((block, block), lambda i: (0, 0)),
            slot,
            slot,
        ]
        + [anyspec] * len(before),
        out_specs=[slot, slot],
        input_output_aliases={4 + i: i for i in range(len(before))},
        compiler_params=pltpu.CompilerParams(vmem_limit_bytes=24 * 2**20),
        cost_estimate=pl.CostEstimate(
            flops=4 * block * block * width, bytes_accessed=6 * 2**20, transcendentals=0
        ),
        name="stats",
    )(me, g.reshape(block, block), lstat, rstat, *before)


def finish_kernel(*refs):
    out = refs[-1]

    def total(x, y, z):
        return (x.astype(F32) + y.astype(F32) + z.astype(F32)).astype(BF)

    for s in range(2):
        own, left_t, left_b, right_t, right_b = refs[5 * s : 5 * s + 5]
        half = left_t.shape[0]
        for q in range(half):
            out[q, :, s] = total(own[q], left_t[q], right_t[q])
            out[q + half, :, s] = total(own[q + half], left_b[q], right_b[q])


def finish(parts):
    pieces, bands, piece, width = parts[0].shape
    return pl.pallas_call(
        finish_kernel,
        out_shape=jax.ShapeDtypeStruct((pieces, bands, 2, piece, width), BF),
        in_specs=[pl.BlockSpec(memory_space=pltpu.VMEM)] * 10,
        out_specs=pl.BlockSpec(memory_space=pltpu.VMEM),
        compiler_params=pltpu.CompilerParams(vmem_limit_bytes=VMEM_TURN),
        cost_estimate=pl.CostEstimate(flops=2**20, bytes_accessed=4 * 2**20, transcendentals=0),
        name="finish",
    )(*parts)


def gather_pair(x, n):
    left0 = shift(x[0], 1, n)
    right1 = shift(x[1], n - 1, n)
    left1 = shift(x[1], 1, n)
    right0 = shift(x[0], n - 1, n)
    across0 = shift(left0, 1, n)
    across1 = shift(right1, n - 1, n)
    return (x[0], left0, right0, across0), (x[1], left1, right1, across1)


def gather_columns(x, n):
    half = x.shape[0] // 2
    left = shift(x, 1, n)
    right = shift(x, n - 1, n)
    top = shift(left[:half], 1, n)
    bottom = shift(right[half:], n - 1, n)
    return x, left, right, top, bottom


def slot_tables(owner, cell, members, per_owner):
    ids = jnp.arange(owner.shape[0], dtype=jnp.int32)
    shared = (owner[:, None] == owner[None, :]) & (ids[None, :] < ids[:, None])
    rank = jnp.sum(shared.astype(jnp.int32), axis=1)
    block_slot = owner * per_owner + rank
    slot_ids = jnp.arange(per_owner * members, dtype=jnp.int32)
    match = (block_slot[None, :] == slot_ids[:, None]).astype(jnp.int32)
    filled = jnp.sum(match, axis=1)
    slot_cell = jnp.sum(match * cell[None, :], axis=1)
    cells = jnp.arange(owner.shape[0], dtype=jnp.int32)
    hit = (cell[None, :] == cells[:, None]).astype(jnp.int32)
    cell_slot = jnp.sum(hit * block_slot[None, :], axis=1)
    return filled, slot_cell, cell_slot


def added(*xs):
    return sum(x.astype(F32) for x in xs).astype(BF)


def local(gradient, owner, cell, left_basis, right_basis, left_stat, right_stat, first, second):
    n = lax.axis_size("dp")
    me = lax.axis_index("dp")
    grid_rows = lax.axis_size("gr")
    bands = lax.axis_size("band")
    members = grid_rows * bands
    per_owner, _, width = left_basis.shape
    band_rows, grid_cols = gradient.shape[1], gradient.shape[2]
    piece = band_rows // grid_rows
    half = band_rows // 2
    g = gradient[0]

    def chunk(by, lo, hi):
        return lax.dynamic_slice(
            g, (lo, 0, lax.rem(me + by, n) * width), (hi - lo, grid_cols, width)
        )

    filled, slot_cell, cell_slot = slot_tables(owner, cell, members, per_owner)
    from_left = shift(chunk(2, 0, half), 1, n)
    from_right = shift(chunk(2, half, band_rows), n - 1, n)
    in_left_b = shift(chunk(1, half, band_rows), 1, n)
    in_right_a = shift(chunk(n - 1, 0, half), n - 1, n)
    right_sum = added(chunk(1, 0, half), from_left)
    left_sum = added(chunk(n - 1, half, band_rows), from_right)
    in_left_a = shift(right_sum, 1, n)
    in_right_b = shift(left_sum, n - 1, n)
    summed = jnp.concatenate(
        [
            added(chunk(0, 0, half), in_left_a, in_right_a),
            added(chunk(0, half, band_rows), in_left_b, in_right_b),
        ]
    )

    right_bf = right_basis.astype(BF)
    pieces_l = gather_pair([left_basis[s].astype(BF) for s in range(2)], n)

    spread = lax.all_to_all(
        summed.reshape(grid_rows, piece, grid_cols, width), "gr", 0, 0, tiled=True
    )
    by_cell = jnp.transpose(spread, (0, 2, 1, 3)).reshape(grid_rows * grid_cols, piece, width)
    leaving = jnp.take(by_cell, slot_cell, axis=0, mode="clip")
    leaving = jnp.where((filled > 0)[:, None, None], leaving, jnp.zeros_like(leaving))
    landed = lax.all_to_all(
        leaving.reshape(members, per_owner, piece, width), ("gr", "band"), 0, 0, tiled=True
    )
    landed = landed.reshape(grid_rows, bands, per_owner, piece, width)
    pieces_g = [gather_columns(landed[:, :, s], n) for s in range(per_owner)]

    me_s = me.reshape(1).astype(jnp.int32)
    state, fulls, terms = (), [], []
    flipped = []
    for s in range(per_owner):
        flipped.append(flip(pieces_l[s]))
    for s in range(per_owner):
        nf, ns, full, own, *parts = turn(
            me_s, s, pieces_g[s], pieces_l[s], flipped[s], right_bf, first, second, state, n
        )
        state = (nf, ns)
        fulls.append(full)
        far_t, far_b, right_t, right_b, left_t, left_b = parts
        from_left = shift(far_t, 1, n)
        from_right = shift(far_b, n - 1, n)
        in_left_b = shift(right_b, 1, n)
        in_right_t = shift(left_t, n - 1, n)
        right_sum, left_sum = added(right_t, from_left), added(left_b, from_right)
        in_left_t = shift(right_sum, 1, n)
        in_right_b = shift(left_sum, n - 1, n)
        terms += [own, in_left_t, in_left_b, in_right_t, in_right_b]
    homed = lax.all_to_all(
        finish(terms).reshape(members, per_owner, piece, width),
        ("gr", "band"), 0, 0, tiled=True,
    )
    per_cell = jnp.take(
        homed.reshape(members * per_owner, piece, width), cell_slot, axis=0, mode="clip"
    )
    final = lax.all_to_all(
        per_cell.reshape(grid_rows, grid_cols, piece, width), "gr", 0, 0, tiled=True
    )
    update = jnp.transpose(final, (0, 2, 1, 3)).reshape(band_rows, grid_cols, width)

    done = ()
    for s in range(per_owner):
        done = stats(me_s, s, fulls[s], left_stat, right_stat, done, n)
    return tuple(done) + state + (update,)


def solution(mesh):
    n, members = mesh.shape["dp"], mesh.shape["fsdp"]

    def run(gradient, owner, cell, *state):
        bands = state[0].shape[1] // (gradient.shape[1] // members)
        inner = Mesh(mesh.devices.reshape(n, members // bands, bands), ("dp", "gr", "band"))
        fsdp = ("gr", "band")
        part = P(fsdp, None, "dp")

        f = jax.shard_map(
            local,
            mesh=inner,
            in_specs=(P("dp", fsdp, None, None), P(), P()) + (part,) * 6,
            out_specs=(part,) * 5,
            check_vma=False,
        )
        return f(gradient, owner, cell, *state)

    return run
```

time: 222 us -> 221 us (level)
  Pallas kernels: 0 us -> 32.9 us
  matrix products: 27.3 us -> 0 us
  waiting for transfers between devices: 112 us -> 103 us
  starting transfers between devices: 51.3 us -> 60.2 us
  local copies, waits for them, and re-layouts: 17.7 us -> 14 us
  other arithmetic: 12.3 us -> 9.55 us
    pallas_call x0 -> x7, Pallas kernels: none -> 32.9 us  [the longest x2 18.7 us: turn(): pl.pallas_call(functools.partial(turn_kernel, n, s), out_shape=[state, st...]
    dot_general x8 -> x0, matrix products: 27.3 us -> none  [the longest x1 9.38 us: local(): jnp.einsum('sik,sic->skc', full_left, z, preferred_element_type=F32)]
    ppermute x16 -> x32, starting transfers between devices: 23.7 us -> 34.7 us  [shift(): return lax.ppermute(x, 'dp', [(i, (i + by) % n) for i in range(n)])]
    ppermute x16 -> x32, waiting for transfers between devices: 75.7 us -> 67.8 us  [shift(): return lax.ppermute(x, 'dp', [(i, (i + by) % n) for i in range(n)])]
    dynamic_update_slice x6 -> x0, local copies, waits for them, and re-layouts: 6.61 us -> none  [place(): out = lax.dynamic_update_slice_in_dim(out, piece, at, out.ndim - 1)]
    unnamed x12 -> x74, local copies, waits for them, and re-layouts: 0.9 us -> 6.23 us
    all_to_all x1, waiting for transfers between devices: 14.1 us -> 11 us  [local(): lax.all_to_all(leaving.reshape(members, per_owner, piece, width), ('gr',...]
    another operation x2 -> x0, local copies, waits for them, and re-layouts: 3.05 us -> none  [run(): return f(gradient, owner, cell, *state)]
  transfers between devices with their start and end apart: 20 -> 36, of which waited for: 13 -> 23; matrix products, arithmetic and copies ran while one was open for 13% -> 4% of each run, Pallas kernels for 0% -> 9%
where the time goes in v2:
time: 221 us
  waiting for transfers between devices  103 us (47%)
  starting transfers between devices  60.2 us (27%)
  Pallas kernels  32.9 us (15%)
  local copies, waits for them, and re-layouts  14 us (6%)
  other arithmetic  9.55 us (4%)
    ppermute x32, waiting for transfers between devices, shift(): return lax.ppermute(x, 'dp', [(i, (i + by) % n) for i in range(n)])  67.8 us
    ppermute x32, starting transfers between devices, shift(): return lax.ppermute(x, 'dp', [(i, (i + by) % n) for i in range(n)])  34.7 us
    pallas_call x2, Pallas kernels, turn(): pl.pallas_call(functools.partial(turn_kernel, n, s), out_shape=[state, st...  18.7 us
    all_to_all x1, waiting for transfers between devices, local(): lax.all_to_all(finish(terms).reshape(members, per_owner, piece, width), (...  16.9 us
    all_to_all x1, waiting for transfers between devices, local(): lax.all_to_all(leaving.reshape(members, per_owner, piece, width), ('gr',...  11 us
    all_to_all x1, starting transfers between devices, local(): lax.all_to_all(leaving.reshape(members, per_owner, piece, width), ('gr',...  8.92 us
    all_to_all x1, starting transfers between devices, local(): lax.all_to_all(finish(terms).reshape(members, per_owner, piece, width), (...  7.98 us
    all_to_all x1, waiting for transfers between devices, local(): lax.all_to_all(summed.reshape(grid_rows, piece, grid_cols, width), 'gr',...  6.7 us
  transfers between devices with their start and end apart: 36, of which 23 were waited for; matrix products, arithmetic and copies ran while one was open for 4% of the time, Pallas kernels for 9%

profile of v2, /device:TPU:1, one launch (start us, length us, event | category | flops | bytes accessed | tf_op | source)
XLA Modules:
  0.0 220.6 jit_solution(14297555479248642320)
XLA Ops:
  7.0 4.1 %collective-permute-done = bf16[64,8,256]{2,1,0:T(8,128)(2,1)S(1)} collective-permute-done((bf16[64,8,256]{2,1,0:T(8,128)(2,1)S(1)}, bf16[64,8,256]{2,1,0:T(8,128)(2,1)S(1)}, u32[]{:S(2)}, u32[]{:S(2)}) %collective-permute-start) | collective-permute-done | bytes 262176 | tf_op jit(solution)/shard_map/ppermute | solution.py:18
  16.7 4.9 %collective-permute-done.1 = bf16[64,8,256]{2,1,0:T(8,128)(2,1)S(1)} collective-permute-done((bf16[64,8,256]{2,1,0:T(8,128)(2,1)}, bf16[64,8,256]{2,1,0:T(8,128)(2,1)S(1)}, u32[]{:S(2)}, u32[]{:S(2)}) %collective-permute-start.1) | collective-permute-done | bytes 262176 | tf_op jit(solution)/shard_map/ppermute | solution.py:18
  23.8 5.2 %all-to-all-start = ((bf16[4,32,8,256]{3,2,1,0:T(8,128)(2,1)}), bf16[4,32,8,256]{3,2,1,0:T(8,128)(2,1)S(1)}, u32[]{:S(2)}, u32[]{:S(2)}) async-start(bf16[4,32,8,256]{3,2,1,0:T(8,128)(2,1)} %bitcast.9), calls=%async_computation | async-start | bytes 1048576 | tf_op jit(solution)/shard_map/all_to_all | solution.py:347
  29.3 6.7 %all-to-all-done = bf16[4,32,8,256]{3,2,1,0:T(8,128)(2,1)S(1)} async-done(((bf16[4,32,8,256]{3,2,1,0:T(8,128)(2,1)}), bf16[4,32,8,256]{3,2,1,0:T(8,128)(2,1)S(1)}, u32[]{:S(2)}, u32[]{:S(2)}) %all-to-all-start) | async-done | bytes 524320 | tf_op jit(solution)/shard_map/all_to_all | solution.py:347
  37.8 8.9 %all-to-all-start.1 = ((bf16[32,2,32,256]{3,2,1,0:T(8,128)(2,1)}), bf16[32,2,32,256]{3,2,1,0:T(8,128)(2,1)S(1)}, u32[]{:S(2)}, u32[]{:S(2)}) async-start(bf16[32,2,32,256]{3,2,1,0:T(8,128)(2,1)} %broadcast_select_fusion), calls=%async_computation.1 | async-start | bytes 2097152 | tf_op jit(solution)/shard_map/all_to_all | solution.py:353
  52.8 11.0 %all-to-all-done.1 = bf16[32,2,32,256]{3,2,1,0:T(8,128)(2,1)S(1)} async-done(((bf16[32,2,32,256]{3,2,1,0:T(8,128)(2,1)}), bf16[32,2,32,256]{3,2,1,0:T(8,128)(2,1)S(1)}, u32[]{:S(2)}, u32[]{:S(2)}) %all-to-all-start.1) | async-done | bytes 1048608 | tf_op jit(solution)/shard_map/all_to_all | solution.py:353
  69.6 4.5 %collective-permute-done.11.refs_2_.refs_8_ = bf16[1024,256]{1,0:T(8,128)(2,1)S(1)} collective-permute-done((bf16[1024,256]{1,0:T(8,128)(2,1)S(1)}, bf16[1024,256]{1,0:T(8,128)(2,1)S(1)}, u32[]{:S(2)}, u32[]{:S(2)}) %collective-permute-start.11) | collective-permute-done | bytes 524320 | tf_op jit(solution)/shard_map/ppermute | solution.py:18
  75.0 3.5 %collective-permute-done.13.refs_2_ = bf16[4,8,32,256]{3,2,1,0:T(8,128)(2,1)S(1)} collective-permute-done((bf16[4,8,32,256]{3,2,1,0:T(8,128)(2,1)S(1)}, bf16[4,8,32,256]{3,2,1,0:T(8,128)(2,1)S(1)}, u32[]{:S(2)}, u32[]{:S(2)}) %collective-permute-start.13) | collective-permute-done | bytes 524320 | tf_op jit(solution)/shard_map/ppermute | solution.py:18
  78.5 6.8 %collective-permute-done.14.refs_3_ = bf16[4,8,32,256]{3,2,1,0:T(8,128)(2,1)S(1)} collective-permute-done((bf16[4,8,32,256]{3,2,1,0:T(8,128)(2,1)S(1)}, bf16[4,8,32,256]{3,2,1,0:T(8,128)(2,1)S(1)}, u32[]{:S(2)}, u32[]{:S(2)}) %collective-permute-start.14) | collective-permute-done | bytes 524320 | tf_op jit(solution)/shard_map/ppermute | solution.py:18
  85.3 2.9 %collective-permute-start.12 = (bf16[1024,256]{1,0:T(8,128)(2,1)S(1)}, bf16[1024,256]{1,0:T(8,128)(2,1)S(1)}, u32[]{:S(2)}, u32[]{:S(2)}) collective-permute-start(bf16[1024,256]{1,0:T(8,128)(2,1)S(1)} %collective-permute-done.11.refs_2_.refs_8_), channel_id=1, source_target_pairs={{0,96},{32,0},{64,32},{96,64},{1,97},{33,1},{65,33},{97,65},{2,98}... | collective-permute-start | bytes 1572872 | tf_op jit(solution)/shard_map/ppermute | solution.py:18
  89.7 6.8 %collective-permute-done.7.refs_3_ = bf16[4,8,32,256]{3,2,1,0:T(8,128)(2,1)S(1)} collective-permute-done((bf16[4,8,32,256]{3,2,1,0:T(8,128)(2,1)S(1)}, bf16[4,8,32,256]{3,2,1,0:T(8,128)(2,1)S(1)}, u32[]{:S(2)}, u32[]{:S(2)}) %collective-permute-start.7) | collective-permute-done | bytes 524320 | tf_op jit(solution)/shard_map/ppermute | solution.py:18
  96.5 2.9 %collective-permute-start.16 = (bf16[2,8,32,256]{3,2,1,0:T(8,128)(2,1)}, bf16[2,8,32,256]{3,2,1,0:T(8,128)(2,1)}, u32[]{:S(2)}, u32[]{:S(2)}) collective-permute-start(bf16[2,8,32,256]{3,2,1,0:T(8,128)(2,1)} %slice.44), channel_id=1, source_target_pairs={{0,96},{32,0},{64,32},{96,64},{1,97},{33,1},{65,33},{97,65},{2,98}... | collective-permute-start | bytes 786440 | tf_op jit(solution)/shard_map/ppermute | solution.py:18
  101.0 11.2 %collective-permute-done.19.refs_3_.refs_9_ = bf16[1024,256]{1,0:T(8,128)(2,1)S(1)} collective-permute-done((bf16[1024,256]{1,0:T(8,128)(2,1)}, bf16[1024,256]{1,0:T(8,128)(2,1)S(1)}, u32[]{:S(2)}, u32[]{:S(2)}) %collective-permute-start.19) | collective-permute-done | bytes 524320 | tf_op jit(solution)/shard_map/ppermute | solution.py:18
  122.1 9.3 %turn.2 = (f32[2,1024,256]{2,1,0:T(8,128)}, f32[2,1024,256]{2,1,0:T(8,128)}, bf16[8,4,32,1024]{3,2,1,0:T(8,128)(2,1)}, bf16[4,8,32,256]{3,2,1,0:T(8,128)(2,1)}, ...) custom-call(s32[1]{0:T(128)} %bitcast.refs_0_.me_ref, ...), custom_call_target="tpu_custom_call" | custom-call | flops 2147483648 | bytes 14680064 | tf_op jit(solution)/shard_map/turn/pallas_call | solution.py:173
  132.2 9.4 %turn.3 = (f32[2,1024,256]{2,1,0:T(8,128)}, f32[2,1024,256]{2,1,0:T(8,128)}, bf16[8,4,32,1024]{3,2,1,0:T(8,128)(2,1)}, bf16[4,8,32,256]{3,2,1,0:T(8,128)(2,1)}, ...) custom-call(s32[1]{0:T(128)} %bitcast.refs_0_.me_ref, ...), custom_call_target="tpu_custom_call", output_to_operand_aliasing={{0}: (14, {}), {1}: (15, {})} | custom-call | flops 2147483648 | bytes 14680064 | tf_op jit(solution)/shard_map/turn/pallas_call | solution.py:173
  154.6 5.1 %collective-permute-done.28.refs_7_ = bf16[2,8,32,256]{3,2,1,0:T(8,128)(2,1)S(1)} collective-permute-done((bf16[2,8,32,256]{3,2,1,0:T(8,128)(2,1)}, bf16[2,8,32,256]{3,2,1,0:T(8,128)(2,1)S(1)}, u32[]{:S(2)}, u32[]{:S(2)}) %collective-permute-start.28) | collective-permute-done | bytes 262176 | tf_op jit(solution)/shard_map/ppermute | solution.py:18
  162.4 2.9 %collective-permute-done.22.refs_2_ = bf16[2,8,32,256]{3,2,1,0:T(8,128)(2,1)S(1)} collective-permute-done((bf16[2,8,32,256]{3,2,1,0:T(8,128)(2,1)S(1)}, bf16[2,8,32,256]{3,2,1,0:T(8,128)(2,1)S(1)}, u32[]{:S(2)}, u32[]{:S(2)}) %collective-permute-start.22) | collective-permute-done | bytes 262176 | tf_op jit(solution)/shard_map/ppermute | solution.py:18
  165.5 4.4 %collective-permute-done.31.refs_9_ = bf16[2,8,32,256]{3,2,1,0:T(8,128)(2,1)S(1)} collective-permute-done((bf16[2,8,32,256]{3,2,1,0:T(8,128)(2,1)S(1)}, bf16[2,8,32,256]{3,2,1,0:T(8,128)(2,1)S(1)}, u32[]{:S(2)}, u32[]{:S(2)}) %collective-permute-start.31) | collective-permute-done | bytes 262176 | tf_op jit(solution)/shard_map/ppermute | solution.py:18
  171.0 4.6 %collective-permute-done.25.refs_4_ = bf16[2,8,32,256]{3,2,1,0:T(8,128)(2,1)S(1)} collective-permute-done((bf16[2,8,32,256]{3,2,1,0:T(8,128)(2,1)S(1)}, bf16[2,8,32,256]{3,2,1,0:T(8,128)(2,1)S(1)}, u32[]{:S(2)}, u32[]{:S(2)}) %collective-permute-start.25) | collective-permute-done | bytes 262176 | tf_op jit(solution)/shard_map/ppermute | solution.py:18
  177.3 3.2 %finish.1 = bf16[4,8,2,32,256]{4,3,2,1,0:T(8,128)(2,1)} custom-call(bf16[4,8,32,256]{3,2,1,0:T(8,128)(2,1)} %get-tuple-element.39.refs_0_, bf16[2,8,32,256]{3,2,1,0:T(8,128)(2,1)} %copy-done.30, bf16[2,8,32,256]{3,2,1,0:T(8,128)(2,1)} %copy-done.24, bf16[2,8,32,256]{3,2,1,0:T(8,128)(2,1)} %copy-done.25, bf16[2,8,32,256]{3,2,1,0:T(8,128)(2,1)} %copy-done.29, ...), custom_call_target="tpu_custom_call" | custom-call | flops 1048576 | bytes 4194304 | tf_op jit(solution)/shard_map/finish/pallas_call | solution.py:262
  180.5 8.0 %all-to-all-start.2 = ((bf16[32,2,32,256]{3,2,1,0:T(8,128)(2,1)}), bf16[32,2,32,256]{3,2,1,0:T(8,128)(2,1)S(1)}, u32[]{:S(2)}, u32[]{:S(2)}) async-start(bf16[32,2,32,256]{3,2,1,0:T(8,128)(2,1)} %bitcast.46), calls=%async_computation.2 | async-start | bytes 2097152 | tf_op jit(solution)/shard_map/all_to_all | solution.py:379
  188.6 16.9 %all-to-all-done.2 = bf16[32,2,32,256]{3,2,1,0:T(8,128)(2,1)S(1)} async-done(((bf16[32,2,32,256]{3,2,1,0:T(8,128)(2,1)}), bf16[32,2,32,256]{3,2,1,0:T(8,128)(2,1)S(1)}, u32[]{:S(2)}, u32[]{:S(2)}) %all-to-all-start.2) | async-done | bytes 1048608 | tf_op jit(solution)/shard_map/all_to_all | solution.py:379
  206.9 3.5 %all-to-all-start.3 = ((bf16[4,8,32,256]{3,2,1,0:T(8,128)(2,1)}), bf16[4,8,32,256]{3,2,1,0:T(8,128)(2,1)S(1)}, u32[]{:S(2)}, u32[]{:S(2)}) async-start(bf16[4,8,32,256]{3,2,1,0:T(8,128)(2,1)} %bitcast.50), calls=%async_computation.3 | async-start | bytes 1048576 | tf_op jit(solution)/shard_map/all_to_all | solution.py:386
  216.4 2.8 %stats.3 = (f32[2,1024,256]{2,1,0:T(8,128)}, f32[2,1024,256]{2,1,0:T(8,128)}) custom-call(s32[1]{0:T(128)} %bitcast.refs_0_.me_ref, bf16[1024,1024]{1,0:T(8,128)(2,1)S(1)} %bitcast.42, f32[2,1024,256]{2,1,0:T(8,128)S(1)} %copy-done, f32[2,1024,256]{2,1,0:T(8,128)S(1)} %copy-done.1, ...), custom_call_target="tpu_custom_call", output_to_operand_aliasing={{0}: (4, {}), {1}: (5, {})} | custom-call | flops 1073741824 | bytes 6291456 | tf_op jit(solution)/shard_map/stats/pallas_call | solution.py:225
  (159 shorter events, 69.9 us)
Async XLA Ops:
  23.8 12.1 %all-to-all-start = ((bf16[4,32,8,256]{3,2,1,0:T(8,128)(2,1)}), bf16[4,32,8,256]{3,2,1,0:T(8,128)(2,1)S(1)}, u32[]{:S(2)}, u32[]{:S(2)}) async-start(bf16[4,32,8,256]{3,2,1,0:T(8,128)(2,1)} %bitcast.9), calls=%async_computation | async-start | bytes 1048576 | tf_op jit(solution)/shard_map/all_to_all | solution.py:347
  37.8 26.0 %all-to-all-start.1 = ((bf16[32,2,32,256]{3,2,1,0:T(8,128)(2,1)}), bf16[32,2,32,256]{3,2,1,0:T(8,128)(2,1)S(1)}, u32[]{:S(2)}, u32[]{:S(2)}) async-start(bf16[32,2,32,256]{3,2,1,0:T(8,128)(2,1)} %broadcast_select_fusion), calls=%async_computation.1 | async-start | bytes 2097152 | tf_op jit(solution)/shard_map/all_to_all | solution.py:353
  48.5 18.3 %collective-permute-start.17 = (bf16[1024,256]{1,0:T(8,128)(2,1)S(1)}, bf16[1024,256]{1,0:T(8,128)(2,1)}, u32[]{:S(2)}, u32[]{:S(2)}) collective-permute-start(bf16[1024,256]{1,0:T(8,128)(2,1)S(1)} %get-tuple-element.63.refs_0_.refs_6_), channel_id=1, source_target_pairs={{0,32},{32,64},{64,96},{96,0},{1,33},{33,65},{65,97},{97,1},{2,34}... | collective-permute-start | bytes 1572872 | tf_op jit(solution)/shard_map/ppermute | solution.py:18
  49.8 17.1 %collective-permute-start.18 = (bf16[1024,256]{1,0:T(8,128)(2,1)S(1)}, bf16[1024,256]{1,0:T(8,128)(2,1)}, u32[]{:S(2)}, u32[]{:S(2)}) collective-permute-start(bf16[1024,256]{1,0:T(8,128)(2,1)S(1)} %get-tuple-element.63.refs_0_.refs_6_), channel_id=1, source_target_pairs={{0,96},{32,0},{64,32},{96,64},{1,97},{33,1},{65,33},{97,65},{2,98}... | collective-permute-start | bytes 1572872 | tf_op jit(solution)/shard_map/ppermute | solution.py:18
  51.4 22.6 %collective-permute-start.11 = (bf16[1024,256]{1,0:T(8,128)(2,1)S(1)}, bf16[1024,256]{1,0:T(8,128)(2,1)S(1)}, u32[]{:S(2)}, u32[]{:S(2)}) collective-permute-start(bf16[1024,256]{1,0:T(8,128)(2,1)S(1)} %get-tuple-element.64.refs_0_.refs_6_), channel_id=1, source_target_pairs={{0,96},{32,0},{64,32},{96,64},{1,97},{33,1},{65,33},{97,65},{2,98}... | collective-permute-start | bytes 1572872 | tf_op jit(solution)/shard_map/ppermute | solution.py:18
  64.0 14.5 %collective-permute-start.13 = (bf16[4,8,32,256]{3,2,1,0:T(8,128)(2,1)S(1)}, bf16[4,8,32,256]{3,2,1,0:T(8,128)(2,1)S(1)}, u32[]{:S(2)}, u32[]{:S(2)}) collective-permute-start(bf16[4,8,32,256]{3,2,1,0:T(8,128)(2,1)S(1)} %get-tuple-element.65.refs_1_), channel_id=1, source_target_pairs={{0,32},{32,64},{64,96},{96,0},{1,33},{33,65},{65,97},{97,1},{2,34}... | collective-permute-start | bytes 1572872 | tf_op jit(solution)/shard_map/ppermute | solution.py:18
  65.3 20.0 %collective-permute-start.14 = (bf16[4,8,32,256]{3,2,1,0:T(8,128)(2,1)S(1)}, bf16[4,8,32,256]{3,2,1,0:T(8,128)(2,1)S(1)}, u32[]{:S(2)}, u32[]{:S(2)}) collective-permute-start(bf16[4,8,32,256]{3,2,1,0:T(8,128)(2,1)S(1)} %get-tuple-element.65.refs_1_), channel_id=1, source_target_pairs={{0,96},{32,0},{64,32},{96,64},{1,97},{33,1},{65,33},{97,65},{2,98}... | collective-permute-start | bytes 1572872 | tf_op jit(solution)/shard_map/ppermute | solution.py:18
  66.9 22.8 %collective-permute-start.6 = (bf16[4,8,32,256]{3,2,1,0:T(8,128)(2,1)S(1)}, bf16[4,8,32,256]{3,2,1,0:T(8,128)(2,1)S(1)}, u32[]{:S(2)}, u32[]{:S(2)}) collective-permute-start(bf16[4,8,32,256]{3,2,1,0:T(8,128)(2,1)S(1)} %get-tuple-element.66.refs_1_), channel_id=1, source_target_pairs={{0,32},{32,64},{64,96},{96,0},{1,33},{33,65},{65,97},{97,1},{2,34}... | collective-permute-start | bytes 1572872 | tf_op jit(solution)/shard_map/ppermute | solution.py:18
  66.9 29.6 %collective-permute-start.7 = (bf16[4,8,32,256]{3,2,1,0:T(8,128)(2,1)S(1)}, bf16[4,8,32,256]{3,2,1,0:T(8,128)(2,1)S(1)}, u32[]{:S(2)}, u32[]{:S(2)}) collective-permute-start(bf16[4,8,32,256]{3,2,1,0:T(8,128)(2,1)S(1)} %get-tuple-element.66.refs_1_), channel_id=1, source_target_pairs={{0,96},{32,0},{64,32},{96,64},{1,97},{33,1},{65,33},{97,65},{2,98}... | collective-permute-start | bytes 1572872 | tf_op jit(solution)/shard_map/ppermute | solution.py:18
  74.0 26.9 %collective-permute-start.10 = (bf16[1024,256]{1,0:T(8,128)(2,1)S(1)}, bf16[1024,256]{1,0:T(8,128)(2,1)S(1)}, u32[]{:S(2)}, u32[]{:S(2)}) collective-permute-start(bf16[1024,256]{1,0:T(8,128)(2,1)S(1)} %get-tuple-element.64.refs_0_.refs_6_), channel_id=1, source_target_pairs={{0,32},{32,64},{64,96},{96,0},{1,33},{33,65},{65,97},{97,1},{2,34}... | collective-permute-start | bytes 1572872 | tf_op jit(solution)/shard_map/ppermute | solution.py:18
  78.5 33.7 %collective-permute-start.19 = (bf16[1024,256]{1,0:T(8,128)(2,1)}, bf16[1024,256]{1,0:T(8,128)(2,1)S(1)}, u32[]{:S(2)}, u32[]{:S(2)}) collective-permute-start(bf16[1024,256]{1,0:T(8,128)(2,1)} %collective-permute-done.17.refs_1_.refs_7_), channel_id=1, source_target_pairs={{0,32},{32,64},{64,96},{96,0},{1,33},{33,65},{65,97},{97,1},{2,34}... | collective-permute-start | bytes 1572872 | tf_op jit(solution)/shard_map/ppermute | solution.py:18
  85.3 32.5 %collective-permute-start.12 = (bf16[1024,256]{1,0:T(8,128)(2,1)S(1)}, bf16[1024,256]{1,0:T(8,128)(2,1)S(1)}, u32[]{:S(2)}, u32[]{:S(2)}) collective-permute-start(bf16[1024,256]{1,0:T(8,128)(2,1)S(1)} %collective-permute-done.11.refs_2_.refs_8_), channel_id=1, source_target_pairs={{0,96},{32,0},{64,32},{96,64},{1,97},{33,1},{65,33},{97,65},{2,98}... | collective-permute-start | bytes 1572872 | tf_op jit(solution)/shard_map/ppermute | solution.py:18
  89.7 31.6 %collective-permute-start.15 = (bf16[2,8,32,256]{3,2,1,0:T(8,128)(2,1)}, bf16[2,8,32,256]{3,2,1,0:T(8,128)(2,1)S(1)}, u32[]{:S(2)}, u32[]{:S(2)}) collective-permute-start(bf16[2,8,32,256]{3,2,1,0:T(8,128)(2,1)} %slice.43), channel_id=1, source_target_pairs={{0,32},{32,64},{64,96},{96,0},{1,33},{33,65},{65,97},{97,1},{2,34}... | collective-permute-start | bytes 786440 | tf_op jit(solution)/shard_map/ppermute | solution.py:18
  96.5 24.9 %collective-permute-start.16 = (bf16[2,8,32,256]{3,2,1,0:T(8,128)(2,1)}, bf16[2,8,32,256]{3,2,1,0:T(8,128)(2,1)}, u32[]{:S(2)}, u32[]{:S(2)}) collective-permute-start(bf16[2,8,32,256]{3,2,1,0:T(8,128)(2,1)} %slice.44), channel_id=1, source_target_pairs={{0,96},{32,0},{64,32},{96,64},{1,97},{33,1},{65,33},{97,65},{2,98}... | collective-permute-start | bytes 786440 | tf_op jit(solution)/shard_map/ppermute | solution.py:18
  101.0 30.4 %collective-permute-start.8 = (bf16[2,8,32,256]{3,2,1,0:T(8,128)(2,1)}, bf16[2,8,32,256]{3,2,1,0:T(8,128)(2,1)S(1)}, u32[]{:S(2)}, u32[]{:S(2)}) collective-permute-start(bf16[2,8,32,256]{3,2,1,0:T(8,128)(2,1)} %slice.39), channel_id=1, source_target_pairs={{0,32},{32,64},{64,96},{96,0},{1,33},{33,65},{65,97},{97,1},{2,34}... | collective-permute-start | bytes 786440 | tf_op jit(solution)/shard_map/ppermute | solution.py:18
  112.2 19.2 %collective-permute-start.9 = (bf16[2,8,32,256]{3,2,1,0:T(8,128)(2,1)}, bf16[2,8,32,256]{3,2,1,0:T(8,128)(2,1)S(1)}, u32[]{:S(2)}, u32[]{:S(2)}) collective-permute-start(bf16[2,8,32,256]{3,2,1,0:T(8,128)(2,1)} %slice.40), channel_id=1, source_target_pairs={{0,96},{32,0},{64,32},{96,64},{1,97},{33,1},{65,33},{97,65},{2,98}... | collective-permute-start | bytes 786440 | tf_op jit(solution)/shard_map/ppermute | solution.py:18
  144.6 15.1 %collective-permute-start.28 = (bf16[2,8,32,256]{3,2,1,0:T(8,128)(2,1)}, bf16[2,8,32,256]{3,2,1,0:T(8,128)(2,1)S(1)}, u32[]{:S(2)}, u32[]{:S(2)}) collective-permute-start(bf16[2,8,32,256]{3,2,1,0:T(8,128)(2,1)} %get-tuple-element.49), channel_id=1, source_target_pairs={{0,32},{32,64},{64,96},{96,0},{1,33},{33,65},{65,97},{97,1},{2,34}... | collective-permute-start | bytes 786440 | tf_op jit(solution)/shard_map/ppermute | solution.py:18
  147.5 12.4 %collective-permute-start.29 = (bf16[2,8,32,256]{3,2,1,0:T(8,128)(2,1)}, bf16[2,8,32,256]{3,2,1,0:T(8,128)(2,1)S(1)}, u32[]{:S(2)}, u32[]{:S(2)}) collective-permute-start(bf16[2,8,32,256]{3,2,1,0:T(8,128)(2,1)} %get-tuple-element.50), channel_id=1, source_target_pairs={{0,96},{32,0},{64,32},{96,64},{1,97},{33,1},{65,33},{97,65},{2,98}... | collective-permute-start | bytes 786440 | tf_op jit(solution)/shard_map/ppermute | solution.py:18
  149.8 15.6 %collective-permute-start.22 = (bf16[2,8,32,256]{3,2,1,0:T(8,128)(2,1)S(1)}, bf16[2,8,32,256]{3,2,1,0:T(8,128)(2,1)S(1)}, u32[]{:S(2)}, u32[]{:S(2)}) collective-permute-start(bf16[2,8,32,256]{3,2,1,0:T(8,128)(2,1)S(1)} %copy-done.33), channel_id=1, source_target_pairs={{0,32},{32,64},{64,96},{96,0},{1,33},{33,65},{65,97},{97,1},{2,34}... | collective-permute-start | bytes 786440 | tf_op jit(solution)/shard_map/ppermute | solution.py:18
  153.1 12.4 %collective-permute-start.23 = (bf16[2,8,32,256]{3,2,1,0:T(8,128)(2,1)S(1)}, bf16[2,8,32,256]{3,2,1,0:T(8,128)(2,1)S(1)}, u32[]{:S(2)}, u32[]{:S(2)}) collective-permute-start(bf16[2,8,32,256]{3,2,1,0:T(8,128)(2,1)S(1)} %copy-done.32), channel_id=1, source_target_pairs={{0,96},{32,0},{64,32},{96,64},{1,97},{33,1},{65,33},{97,65},{2,98}... | collective-permute-start | bytes 786440 | tf_op jit(solution)/shard_map/ppermute | solution.py:18
  154.4 15.5 %collective-permute-start.31 = (bf16[2,8,32,256]{3,2,1,0:T(8,128)(2,1)S(1)}, bf16[2,8,32,256]{3,2,1,0:T(8,128)(2,1)S(1)}, u32[]{:S(2)}, u32[]{:S(2)}) collective-permute-start(bf16[2,8,32,256]{3,2,1,0:T(8,128)(2,1)S(1)} %add_convert_fusion), channel_id=1, source_target_pairs={{0,96},{32,0},{64,32},{96,64},{1,97},{33,1},{65,33},{97,65},{2,98}... | collective-permute-start | bytes 786440 | tf_op jit(solution)/shard_map/ppermute | solution.py:18
  159.9 15.7 %collective-permute-start.25 = (bf16[2,8,32,256]{3,2,1,0:T(8,128)(2,1)S(1)}, bf16[2,8,32,256]{3,2,1,0:T(8,128)(2,1)S(1)}, u32[]{:S(2)}, u32[]{:S(2)}) collective-permute-start(bf16[2,8,32,256]{3,2,1,0:T(8,128)(2,1)S(1)} %add_convert_fusion.2), channel_id=1, source_target_pairs={{0,96},{32,0},{64,32},{96,64},{1,97},{33,1},{65,33},{97,65},{2,98}... | collective-permute-start | bytes 786440 | tf_op jit(solution)/shard_map/ppermute | solution.py:18
  180.5 25.0 %all-to-all-start.2 = ((bf16[32,2,32,256]{3,2,1,0:T(8,128)(2,1)}), bf16[32,2,32,256]{3,2,1,0:T(8,128)(2,1)S(1)}, u32[]{:S(2)}, u32[]{:S(2)}) async-start(bf16[32,2,32,256]{3,2,1,0:T(8,128)(2,1)} %bitcast.46), calls=%async_computation.2 | async-start | bytes 2097152 | tf_op jit(solution)/shard_map/all_to_all | solution.py:379
  206.9 12.6 %all-to-all-start.3 = ((bf16[4,8,32,256]{3,2,1,0:T(8,128)(2,1)}), bf16[4,8,32,256]{3,2,1,0:T(8,128)(2,1)S(1)}, u32[]{:S(2)}, u32[]{:S(2)}) async-start(bf16[4,8,32,256]{3,2,1,0:T(8,128)(2,1)} %bitcast.50), calls=%async_computation.3 | async-start | bytes 1048576 | tf_op jit(solution)/shard_map/all_to_all | solution.py:386
  (49 other events, 708.4 us)

commit v3 on v2

v3 whole, which is shorter than its diff:
```python
import functools

import jax
import jax.numpy as jnp
from jax import lax
from jax.experimental import pallas as pl
from jax.experimental.pallas import tpu as pltpu
from jax.sharding import Mesh, PartitionSpec as P


BF = jnp.bfloat16
F32 = jnp.float32
TILE = 1024
VMEM_TURN = 20 * 2**20


def shift(x, by, n):
    return lax.ppermute(x, "dp", [(i, (i + by) % n) for i in range(n)])


def dot(x, y, dims):
    return lax.dot_general(x, y, (dims, ((), ())), preferred_element_type=F32)


NN = ((1,), (0,))
NT = ((1,), (1,))
TN = ((0,), (0,))


def rows_at(me, by, n, size):
    return pl.ds(pl.multiple_of(lax.rem(me + by, n) * size, size), size)


OFFSETS = (0, 3, 1, 2)


def in_vmem(x):
    return pltpu.with_memory_space_constraint(x, pltpu.MemorySpace.VMEM)


def in_hbm(x):
    return pltpu.with_memory_space_constraint(x, pltpu.MemorySpace.HBM)


def starter(sems):
    started = []

    def start(src, dst):
        c = pltpu.make_async_copy(src, dst, sems.at[len(started)])
        c.start()
        started.append(c)
        return c

    return start, started


def cols(k, width):
    return pl.ds(k * width, width)


def prep_kernel(n, s, count, *refs):
    me_ref = refs[0]
    l_parts = refs[1 : 1 + count]
    r_hbm, first_hbm, second_hbm = refs[1 + count : 4 + count]
    lb, lt, r, first, second, sems = refs[-6:]
    me = me_ref[0]
    width = r.shape[1]
    tall = lb.shape[0] // 2
    load, loads = starter(sems)
    for k in range(3):
        load(l_parts[k], lb.at[:, cols(k, width)])
    if count == 4:
        load(l_parts[3], lb.at[:, cols(3, width)])
    else:
        load(l_parts[3], lb.at[pl.ds(0, tall), cols(3, width)])
        load(l_parts[4], lb.at[pl.ds(tall, tall), cols(3, width)])
    for k in range(4):
        load(r_hbm.at[s, rows_at(me, OFFSETS[k], n, width), :], r.at[cols(k, width), :])
    load(first_hbm.at[s], first)
    load(second_hbm.at[s], second)
    for k in range(4):
        loads[k].wait()
        if k == 3 and count == 5:
            loads[4].wait()
        lt[cols(k, width), :] = lb[:, cols(k, width)].T
    for c in loads[count:]:
        c.wait()


def prep(me, s, lb, r, first, second, after, n):
    _, block, width = r.shape
    hbm = pl.BlockSpec(memory_space=pltpu.HBM)
    vmem = pl.BlockSpec(memory_space=pltpu.VMEM)
    return pl.pallas_call(
        functools.partial(prep_kernel, n, s, len(lb)),
        out_shape=[
            pltpu.VMEM((block, block), BF),
            pltpu.VMEM((block, block), BF),
            pltpu.VMEM((block, width), BF),
            pltpu.VMEM((block, width), F32),
            pltpu.VMEM((block, width), F32),
        ],
        in_specs=[pl.BlockSpec(memory_space=pltpu.SMEM)] + [hbm] * (3 + len(lb)) + [vmem] * len(after),
        out_specs=[vmem] * 5,
        scratch_shapes=[pltpu.SemaphoreType.DMA((11,))],
        compiler_params=pltpu.CompilerParams(vmem_limit_bytes=20 * 2**20),
        cost_estimate=pl.CostEstimate(flops=2**22, bytes_accessed=6 * 2**20, transcendentals=0),
        name="prep",
    )(me, *[in_hbm(x) for x in lb], in_hbm(r), in_hbm(first), in_hbm(second), *[in_vmem(x) for x in after])


def load_grad(load, s, parts, g, width, near=False):
    pieces = g.shape[1]
    half = pieces // 2
    waits = []
    if s == 0:
        for k, ref in enumerate(parts[:3]):
            waits += [load(ref.at[q], g.at[:, q, :, cols(k, width)]) for q in range(pieces)]
        for q in range(half):
            if near:
                g[:, q, :, 3 * width :] = parts[3][q]
                g[:, q + half, :, 3 * width :] = parts[4][q]
            else:
                waits.append(load(parts[3].at[q], g.at[:, q, :, cols(3, width)]))
                waits.append(load(parts[4].at[q], g.at[:, q + half, :, cols(3, width)]))
    elif near:
        for k in range(4):
            for q in range(pieces):
                g[:, q, :, k * width : (k + 1) * width] = parts[0][q, :, k]
    else:
        for k in range(4):
            waits += [
                load(parts[0].at[q, :, k], g.at[:, q, :, cols(k, width)]) for q in range(pieces)
            ]
    return waits


def turn_kernel(n, s, count, *refs):
    me_ref = refs[0]
    g_parts = refs[1 : 1 + count]
    lb, lt, r, first, second = refs[1 + count : 6 + count]
    nf_hbm, ns_hbm, own_out, to_right, to_left, right_t, left_b = refs[-16:-9]
    g, z, d, t, p, nf, ns, sems, out_sems = refs[-9:]
    me = me_ref[0]
    _, pieces, piece, block = g.shape
    width = z.shape[1]
    half = pieces // 2
    load, _ = starter(sems)
    store, stores = starter(out_sems)
    for c in load_grad(load, s, g_parts, g, width, near=True):
        c.wait()
    per = TILE // (pieces * piece)
    tiles = block // TILE

    @pl.loop(0, tiles)
    def _(i):
        rows = g[pl.ds(i * per, per)].reshape(TILE, block)
        at = pl.ds(pl.multiple_of(i * TILE, TILE), TILE)
        z[at, :] = dot(rows, r[...], NN).astype(BF)

    for k in range(4):
        at = rows_at(me, OFFSETS[k], n, width)
        turned = dot(lt[cols(k, width), :], z[...], NN)
        a = 0.9 * first[at, :] + 0.1 * turned
        b = 0.999 * second[at, :] + 0.001 * turned * turned
        nf[at, :] = a
        ns[at, :] = b
        d[cols(k, width), :] = (a / (jnp.sqrt(b) + 1e-8)).astype(BF)
    store(nf, nf_hbm.at[s])
    store(ns, ns_hbm.at[s])

    @pl.loop(0, tiles)
    def _(i):
        at = pl.ds(pl.multiple_of(i * TILE, TILE), TILE)
        t[at, :] = dot(lb[at, :], d[...], NN).astype(BF)

    for k in (3, 2, 1, 0):

        @pl.loop(0, tiles)
        def _(i):
            at = pl.ds(pl.multiple_of(i * TILE, TILE), TILE)
            v = dot(t[at, :], r[cols(k, width), :], NT).astype(BF)
            p[pl.ds(i * per, per), :, :, cols(k, width)] = v.reshape(per, pieces, piece, width)

        for q in range(pieces):
            src = p.at[:, q, :, cols(k, width)]
            low = q < half
            if k == 0:
                store(src, own_out.at[q])
            elif k == 3:
                store(src, to_right.at[q] if low else to_left.at[q - half])
            elif k == 2:
                store(src, right_t.at[q] if low else to_right.at[q])
            else:
                store(src, to_left.at[q + half] if low else left_b.at[q - half])
    for c in stores:
        c.wait()


def turn(me, s, g, ready, before, n, per_owner):
    block, width = ready[2].shape
    pieces, bands, piece = g[0].shape[0], g[0].shape[1], g[0].shape[-2]
    hbm = pl.BlockSpec(memory_space=pltpu.HBM)
    vmem = pl.BlockSpec(memory_space=pltpu.VMEM)
    far = 3 if s == 0 else 0
    state = pltpu.HBM((per_owner, block, width), F32)
    whole = pltpu.HBM((pieces, bands, piece, width), BF)
    part = pltpu.HBM((pieces // 2, bands, piece, width), BF)
    return pl.pallas_call(
        functools.partial(turn_kernel, n, s, len(g)),
        out_shape=[state, state, whole, whole, whole, part, part],
        in_specs=[pl.BlockSpec(memory_space=pltpu.SMEM)]
        + [hbm] * far
        + [vmem] * (len(g) - far)
        + [vmem] * 5
        + [hbm] * len(before),
        out_specs=[hbm] * 7,
        scratch_shapes=[
            pltpu.VMEM((bands, pieces, piece, block), BF),
            pltpu.VMEM((block, width), BF),
            pltpu.VMEM((block, width), BF),
            pltpu.VMEM((block, width), BF),
            pltpu.VMEM((bands, pieces, piece, block), BF),
            pltpu.VMEM((block, width), F32),
            pltpu.VMEM((block, width), F32),
            pltpu.SemaphoreType.DMA((16,)),
            pltpu.SemaphoreType.DMA((18,)),
        ],
        input_output_aliases={6 + len(g) + i: i for i in range(len(before))},
        compiler_params=pltpu.CompilerParams(vmem_limit_bytes=VMEM_TURN),
        cost_estimate=pl.CostEstimate(
            flops=8 * block * block * width, bytes_accessed=6 * 2**20, transcendentals=0
        ),
        name="turn",
    )(
        me,
        *[in_hbm(x) for x in g[:far]],
        *[in_vmem(x) for x in (*g[far:], *ready)],
        *[in_hbm(x) for x in before],
    )


def stats_kernel(n, s, count, *refs):
    me_ref = refs[0]
    g_parts = refs[1 : 1 + count]
    lstat, rstat = refs[1 + count : 3 + count]
    new_l, new_r, g, sems = refs[-4:]
    me = me_ref[0]
    _, _, _, block = g.shape
    width = lstat.shape[2]
    load, _ = starter(sems)
    for c in load_grad(load, s, g_parts, g, width):
        c.wait()
    flat = g.reshape(block, block)

    @pl.loop(0, block // TILE)
    def _(i):
        at = pl.ds(pl.multiple_of(i * TILE, TILE), TILE)
        acc = dot(flat[at, :], flat[rows_at(me, 0, n, width), :], NT)
        new_l[0, at, :] = 0.95 * lstat[0, at, :] + 0.05 * acc

    for k in range(4):
        at = rows_at(me, OFFSETS[k], n, width)
        acc = dot(flat[:, cols(k, width)], flat[:, cols(0, width)], TN)
        new_r[0, at, :] = 0.95 * rstat[0, at, :] + 0.05 * acc


def stats(me, s, g, lstat, rstat, before, n):
    _, block, width = lstat.shape
    pieces, bands, piece = g[0].shape[0], g[0].shape[1], g[0].shape[-2]
    slot = pl.BlockSpec((1, block, width), lambda i: (s, 0, 0))
    hbm = pl.BlockSpec(memory_space=pltpu.HBM)
    out = jax.ShapeDtypeStruct(lstat.shape, F32)
    return pl.pallas_call(
        functools.partial(stats_kernel, n, s, len(g)),
        grid=(1,),
        out_shape=[out, out],
        in_specs=[pl.BlockSpec(memory_space=pltpu.SMEM)]
        + [hbm] * len(g)
        + [slot, slot]
        + [hbm] * len(before),
        out_specs=[slot, slot],
        scratch_shapes=[
            pltpu.VMEM((bands, pieces, piece, block), BF),
            pltpu.SemaphoreType.DMA((16,)),
        ],
        input_output_aliases={3 + len(g) + i: i for i in range(len(before))},
        compiler_params=pltpu.CompilerParams(vmem_limit_bytes=24 * 2**20),
        cost_estimate=pl.CostEstimate(
            flops=4 * block * block * width, bytes_accessed=6 * 2**20, transcendentals=0
        ),
        name="stats",
    )(me, *[in_hbm(x) for x in g], lstat, rstat, *before)


def finish_kernel(s, *refs):
    own, from_left, from_right, in_left, in_right = refs[:5]
    out, a, b, sems, out_sems = refs[-5:]
    pieces = own.shape[0]
    half = pieces // 2
    load, loads = starter(sems)
    load(own, a)
    load(from_right.at[pl.ds(half, half)], b.at[pl.ds(0, half)])
    load(from_left.at[pl.ds(half, half)], b.at[pl.ds(half, half)])
    for x in loads:
        x.wait()
    store, stores = starter(out_sems)
    for q in range(pieces):
        c = in_left[q] if q < half else in_right[q - half]
        a[q] = (a[q].astype(F32) + b[q].astype(F32) + c.astype(F32)).astype(BF)
        store(a.at[q], out.at[q, :, s])
    for x in stores:
        x.wait()


def finish(s, own, from_left, from_right, in_left, in_right, before):
    pieces, bands, piece, width = own.shape
    hbm = pl.BlockSpec(memory_space=pltpu.HBM)
    vmem = pl.BlockSpec(memory_space=pltpu.VMEM)
    return pl.pallas_call(
        functools.partial(finish_kernel, s),
        out_shape=pltpu.HBM((pieces, bands, 2, piece, width), BF),
        in_specs=[hbm] * 3 + [vmem] * 2 + [hbm] * len(before),
        out_specs=hbm,
        scratch_shapes=[pltpu.VMEM(own.shape, BF)] * 2
        + [pltpu.SemaphoreType.DMA((3,)), pltpu.SemaphoreType.DMA((pieces,))],
        input_output_aliases={5 + i: i for i in range(len(before))},
        compiler_params=pltpu.CompilerParams(vmem_limit_bytes=16 * 2**20),
        cost_estimate=pl.CostEstimate(flops=2**20, bytes_accessed=2 * 2**20, transcendentals=0),
        name="finish",
    )(
        *[in_hbm(x) for x in (own, from_left, from_right)],
        in_vmem(in_left),
        in_vmem(in_right),
        *[in_hbm(x) for x in before],
    )


def gather_columns(x, n):
    half = x.shape[0] // 2
    left = shift(x, 1, n)
    right = shift(x, n - 1, n)
    top = shift(left[:half], 1, n)
    bottom = shift(right[half:], n - 1, n)
    return x, left, right, top, bottom


def slot_tables(owner, cell, members, per_owner, doubles):
    ids = jnp.arange(owner.shape[0], dtype=jnp.int32)
    shared = (owner[:, None] == owner[None, :]) & (ids[None, :] < ids[:, None])
    rank = jnp.sum(shared.astype(jnp.int32), axis=1)
    cells = jnp.arange(owner.shape[0], dtype=jnp.int32)
    hit = (cell[None, :] == cells[:, None]).astype(jnp.int32)
    cell_slot = jnp.sum(hit * (owner * per_owner + rank)[None, :], axis=1)
    who = jnp.arange(members, dtype=jnp.int32)
    mine = owner[None, :] == who[:, None]
    first = (mine & (rank == 0)[None, :]).astype(jnp.int32)
    second = (mine & (rank == 1)[None, :]).astype(jnp.int32)
    has_first = jnp.sum(first, axis=1)
    first_cell = jnp.sum(first * cell[None, :], axis=1)
    is_second = rank == 1
    before = jnp.sum((is_second[None, :] & (ids[None, :] < ids[:, None])).astype(jnp.int32), axis=1)
    place = jnp.where(is_second, before, doubles)
    second_place = jnp.sum(second * (place - doubles)[None, :], axis=1) + doubles
    spots = jnp.arange(doubles, dtype=jnp.int32)
    second_cell = jnp.sum((place[None, :] == spots[:, None]).astype(jnp.int32) * cell[None, :], axis=1)
    return has_first, first_cell, second_cell, second_place, cell_slot


def added(*xs):
    return sum(x.astype(F32) for x in xs).astype(BF)


def local(gradient, owner, cell, left_basis, right_basis, left_stat, right_stat, first, second):
    n = lax.axis_size("dp")
    me = lax.axis_index("dp")
    grid_rows = lax.axis_size("gr")
    bands = lax.axis_size("band")
    members = grid_rows * bands
    per_owner, _, width = left_basis.shape
    band_rows, grid_cols = gradient.shape[1], gradient.shape[2]
    piece = band_rows // grid_rows
    half = band_rows // 2
    g = gradient[0]

    def chunk(by, lo, hi):
        return lax.dynamic_slice(
            g, (lo, 0, lax.rem(me + by, n) * width), (hi - lo, grid_cols, width)
        )

    doubles = members // 4
    has_first, first_cell, second_cell, second_place, cell_slot = slot_tables(
        owner, cell, members, per_owner, doubles
    )
    from_left = shift(chunk(2, 0, half), 1, n)
    from_right = shift(chunk(2, half, band_rows), n - 1, n)
    in_left_b = shift(chunk(1, half, band_rows), 1, n)
    in_right_a = shift(chunk(n - 1, 0, half), n - 1, n)
    right_sum = added(chunk(1, 0, half), from_left)
    left_sum = added(chunk(n - 1, half, band_rows), from_right)
    in_left_a = shift(right_sum, 1, n)
    in_right_b = shift(left_sum, n - 1, n)
    summed = jnp.concatenate(
        [
            added(chunk(0, 0, half), in_left_a, in_right_a),
            added(chunk(0, half, band_rows), in_left_b, in_right_b),
        ]
    )

    right_bf = right_basis.astype(BF)
    pieces_l = [gather_columns(left_basis[s].astype(BF), n) for s in range(2)]

    spread = lax.all_to_all(
        summed.reshape(grid_rows, piece, grid_cols, width), "gr", 0, 0, tiled=True
    )
    by_cell = jnp.transpose(spread, (0, 2, 1, 3)).reshape(grid_rows * grid_cols, piece, width)
    leaving = jnp.take(by_cell, first_cell, axis=0, mode="clip")
    leaving = jnp.where((has_first > 0)[:, None, None], leaving, jnp.zeros_like(leaving))
    landed0 = lax.all_to_all(leaving, ("gr", "band"), 0, 0, tiled=True)
    pair = jnp.take(by_cell, second_cell, axis=0, mode="clip")
    pair_left = shift(pair, 1, n)
    pair_right = shift(pair, n - 1, n)
    pair_across = shift(pair, 2, n)
    pool = jnp.stack([pair, pair_left, pair_right, pair_across], axis=1)
    pool = jnp.concatenate([pool, jnp.zeros_like(pool[:1])])
    leaving = jnp.take(pool, second_place, axis=0, mode="clip")
    landed1 = lax.all_to_all(leaving, ("gr", "band"), 0, 0, tiled=True)
    pieces_g = [
        gather_columns(landed0.reshape(grid_rows, bands, piece, width), n),
        (landed1.reshape(grid_rows, bands, n, piece, width),),
    ]

    me_s = me.reshape(1).astype(jnp.int32)
    ready, late = [], ((), pieces_g[1])
    for s in range(per_owner):
        ready.append(prep(me_s, s, pieces_l[s], right_bf, first, second, late[s], n))
    state, terms = (), []
    for s in range(per_owner):
        nf, ns, own, to_right, to_left, right_t, left_b = turn(
            me_s, s, pieces_g[s], ready[s], state, n, per_owner
        )
        state = (nf, ns)
        from_left = shift(to_right, 1, n)
        from_right = shift(to_left, n - 1, n)
        top = added(right_t, from_left[: grid_rows // 2])
        bottom = added(left_b, from_right[: grid_rows // 2])
        in_left = shift(top, 1, n)
        in_right = shift(bottom, n - 1, n)
        terms.append((own, from_left, from_right, in_left, in_right))
    parted = ()
    for s in range(per_owner):
        parted = (finish(s, *terms[s], parted),)
    homed = lax.all_to_all(
        parted[0].reshape(members, per_owner, piece, width),
        ("gr", "band"), 0, 0, tiled=True,
    )
    per_cell = jnp.take(
        homed.reshape(members * per_owner, piece, width), cell_slot, axis=0, mode="clip"
    )
    final = lax.all_to_all(
        per_cell.reshape(grid_rows, grid_cols, piece, width), "gr", 0, 0, tiled=True
    )
    update = jnp.transpose(final, (0, 2, 1, 3)).reshape(band_rows, grid_cols, width)

    done = ()
    for s in range(per_owner):
        done = stats(me_s, s, pieces_g[s], left_stat, right_stat, done, n)
    return tuple(done) + state + (update,)


def solution(mesh):
    n, members = mesh.shape["dp"], mesh.shape["fsdp"]

    def run(gradient, owner, cell, *state):
        bands = state[0].shape[1] // (gradient.shape[1] // members)
        inner = Mesh(mesh.devices.reshape(n, members // bands, bands), ("dp", "gr", "band"))
        fsdp = ("gr", "band")
        part = P(fsdp, None, "dp")

        f = jax.shard_map(
            local,
            mesh=inner,
            in_specs=(P("dp", fsdp, None, None), P(), P()) + (part,) * 6,
            out_specs=(part,) * 5,
            check_vma=False,
        )
        return f(gradient, owner, cell, *state)

    return run
```

time: 221 us -> 226 us (1.023)
  starting transfers between devices: 60.2 us -> 73.4 us
  local copies, waits for them, and re-layouts: 14 us -> 10.4 us
  waiting for transfers between devices: 103 us -> 99.9 us
    all_to_all x2 -> x3, starting transfers between devices: 16.9 us -> 28.1 us  [the longest x1 11.2 us: local(): lax.all_to_all(parted[0].reshape(members, per_owner, piece, width), ('gr'...]
    all_to_all x2 -> x3, waiting for transfers between devices: 27.9 us -> 17 us  [the longest x1 17 us: local(): lax.all_to_all(parted[0].reshape(members, per_owner, piece, width), ('gr'...]
    ppermute x32 -> x29, waiting for transfers between devices: 67.8 us -> 76 us  [shift(): return lax.ppermute(x, 'dp', [(i, (i + by) % n) for i in range(n)])]
    unnamed x74 -> x54, local copies, waits for them, and re-layouts: 6.23 us -> 2.4 us
    gather x1 -> x3, local copies, waits for them, and re-layouts: 0.61 us -> 3.14 us  [the longest x1 2 us: local(): leaving = jnp.take(pool, second_place, axis=0, mode='clip')]
    ppermute x32 -> x29, starting transfers between devices: 34.7 us -> 36.4 us  [shift(): return lax.ppermute(x, 'dp', [(i, (i + by) % n) for i in range(n)])]
    pallas_call x7 -> x8, Pallas kernels: 32.9 us -> 31.2 us  [the longest x2 12.7 us: turn(): pl.pallas_call(functools.partial(turn_kernel, n, s, len(g)), out_shape=[s...]
  transfers between devices with their start and end apart: 36 -> 34, of which waited for: 23 -> 20; matrix products, arithmetic and copies ran while one was open for 4% -> 4% of each run, Pallas kernels for 9% -> 13%
where the time goes in v3:
time: 226 us; the launch traced here: 225 us
  waiting for transfers between devices  99.9 us (44%)
  starting transfers between devices  73.4 us (32%)
  Pallas kernels  31.2 us (14%)
  local copies, waits for them, and re-layouts  10.4 us (5%)
  other arithmetic  8.98 us (4%)
    ppermute x29, waiting for transfers between devices, shift(): return lax.ppermute(x, 'dp', [(i, (i + by) % n) for i in range(n)])  76 us
    ppermute x29, starting transfers between devices, shift(): return lax.ppermute(x, 'dp', [(i, (i + by) % n) for i in range(n)])  36.4 us
    all_to_all x1, waiting for transfers between devices, local(): lax.all_to_all(parted[0].reshape(members, per_owner, piece, width), ('gr'...  17 us
    pallas_call x2, Pallas kernels, turn(): pl.pallas_call(functools.partial(turn_kernel, n, s, len(g)), out_shape=[s...  12.7 us
    all_to_all x1, starting transfers between devices, local(): lax.all_to_all(parted[0].reshape(members, per_owner, piece, width), ('gr'...  11.2 us
    all_to_all x1, starting transfers between devices, local(): landed0 = lax.all_to_all(leaving, ('gr', 'band'), 0, 0, tiled=True)  8.8 us
    pallas_call x2, Pallas kernels, stats(): pl.pallas_call(functools.partial(stats_kernel, n, s, len(g)), grid=(1,),...  8.68 us
    all_to_all x1, starting transfers between devices, local(): landed1 = lax.all_to_all(leaving, ('gr', 'band'), 0, 0, tiled=True)  8.08 us
  transfers between devices with their start and end apart: 34, of which 20 were waited for; matrix products, arithmetic and copies ran while one was open for 4% of the time, Pallas kernels for 13%

profile of v3, /device:TPU:1, one launch (start us, length us, event | category | flops | bytes accessed | tf_op | source)
XLA Modules:
  0.0 225.0 jit_solution(10375284044586836686)
XLA Ops:
  7.9 4.2 %collective-permute-done = bf16[64,8,256]{2,1,0:T(8,128)(2,1)} collective-permute-done((bf16[64,8,256]{2,1,0:T(8,128)(2,1)}, bf16[64,8,256]{2,1,0:T(8,128)(2,1)}, u32[]{:S(2)}, u32[]{:S(2)}) %collective-permute-start) | collective-permute-done | bytes 262176 | tf_op jit(solution)/shard_map/ppermute | solution.py:18
  17.6 4.9 %collective-permute-done.1 = bf16[64,8,256]{2,1,0:T(8,128)(2,1)S(1)} collective-permute-done((bf16[64,8,256]{2,1,0:T(8,128)(2,1)S(1)}, bf16[64,8,256]{2,1,0:T(8,128)(2,1)S(1)}, u32[]{:S(2)}, u32[]{:S(2)}) %collective-permute-start.1) | collective-permute-done | bytes 262176 | tf_op jit(solution)/shard_map/ppermute | solution.py:18
  23.5 5.4 %all-to-all-start = ((bf16[4,32,8,256]{3,2,1,0:T(8,128)(2,1)}), bf16[4,32,8,256]{3,2,1,0:T(8,128)(2,1)S(1)}, u32[]{:S(2)}, u32[]{:S(2)}) async-start(bf16[4,32,8,256]{3,2,1,0:T(8,128)(2,1)} %bitcast.9), calls=%async_computation | async-start | bytes 1048576 | tf_op jit(solution)/shard_map/all_to_all | solution.py:413
  29.1 6.8 %all-to-all-done = bf16[4,32,8,256]{3,2,1,0:T(8,128)(2,1)S(1)} async-done(((bf16[4,32,8,256]{3,2,1,0:T(8,128)(2,1)}), bf16[4,32,8,256]{3,2,1,0:T(8,128)(2,1)S(1)}, u32[]{:S(2)}, u32[]{:S(2)}) %all-to-all-start) | async-done | bytes 524320 | tf_op jit(solution)/shard_map/all_to_all | solution.py:413
  37.5 8.8 %all-to-all-start.2 = ((bf16[32,32,256]{2,1,0:T(8,128)(2,1)}), bf16[32,32,256]{2,1,0:T(8,128)(2,1)S(1)}, u32[]{:S(2)}, u32[]{:S(2)}) async-start(bf16[32,32,256]{2,1,0:T(8,128)(2,1)} %broadcast_select_fusion), calls=%async_computation.2 | async-start | bytes 1048576 | tf_op jit(solution)/shard_map/all_to_all | solution.py:419
  53.0 3.8 %collective-permute-done.8 = bf16[8,32,256]{2,1,0:T(8,128)(2,1)S(1)} collective-permute-done((bf16[8,32,256]{2,1,0:T(8,128)(2,1)S(1)}, bf16[8,32,256]{2,1,0:T(8,128)(2,1)S(1)}, u32[]{:S(2)}, u32[]{:S(2)}) %collective-permute-start.8) | collective-permute-done | bytes 131104 | tf_op jit(solution)/shard_map/ppermute | solution.py:18
  58.9 8.1 %all-to-all-start.1 = ((bf16[32,4,32,256]{3,2,1,0:T(8,128)(2,1)}), bf16[32,4,32,256]{3,2,1,0:T(8,128)(2,1)S(1)}, u32[]{:S(2)}, u32[]{:S(2)}) async-start(bf16[32,4,32,256]{3,2,1,0:T(8,128)(2,1)} %gather_fusion.1), calls=%async_computation.1 | async-start | bytes 4194304 | tf_op jit(solution)/shard_map/all_to_all | solution.py:427
  74.2 9.1 %collective-permute-done.17.refs_2_ = bf16[1024,256]{1,0:T(8,128)(2,1)S(1)} collective-permute-done((bf16[1024,256]{1,0:T(8,128)(2,1)S(1)}, bf16[1024,256]{1,0:T(8,128)(2,1)S(1)}, u32[]{:S(2)}, u32[]{:S(2)}) %collective-permute-start.17) | collective-permute-done | bytes 524320 | tf_op jit(solution)/shard_map/ppermute | solution.py:18
  86.2 8.4 %collective-permute-done.9.refs_2_ = bf16[4,8,32,256]{3,2,1,0:T(8,128)(2,1)S(1)} collective-permute-done((bf16[4,8,32,256]{3,2,1,0:T(8,128)(2,1)S(1)}, bf16[4,8,32,256]{3,2,1,0:T(8,128)(2,1)S(1)}, u32[]{:S(2)}, u32[]{:S(2)}) %collective-permute-start.9) | collective-permute-done | bytes 524320 | tf_op jit(solution)/shard_map/ppermute | solution.py:18
  96.1 4.0 %collective-permute-done.19.refs_4_ = bf16[512,256]{1,0:T(8,128)(2,1)S(1)} collective-permute-done((bf16[512,256]{1,0:T(8,128)(2,1)S(1)}, bf16[512,256]{1,0:T(8,128)(2,1)S(1)}, u32[]{:S(2)}, u32[]{:S(2)}) %collective-permute-start.19) | collective-permute-done | bytes 262176 | tf_op jit(solution)/shard_map/ppermute | solution.py:18
  101.7 9.1 %collective-permute-done.20.refs_5_ = bf16[512,256]{1,0:T(8,128)(2,1)S(1)} collective-permute-done((bf16[512,256]{1,0:T(8,128)(2,1)S(1)}, bf16[512,256]{1,0:T(8,128)(2,1)S(1)}, u32[]{:S(2)}, u32[]{:S(2)}) %collective-permute-start.20) | collective-permute-done | bytes 262176 | tf_op jit(solution)/shard_map/ppermute | solution.py:18
  117.0 7.2 %turn.2 = (f32[2,1024,256]{2,1,0:T(8,128)}, f32[2,1024,256]{2,1,0:T(8,128)}, bf16[4,8,32,256]{3,2,1,0:T(8,128)(2,1)}, bf16[4,8,32,256]{3,2,1,0:T(8,128)(2,1)}, b...) custom-call(s32[1]{0:T(128)} %bitcast.refs_0_, ...), custom_call_target="tpu_custom_call" | custom-call | flops 2147483648 | bytes 6291456 | tf_op jit(solution)/shard_map/turn/pallas_call | solution.py:209
  129.4 4.6 %collective-permute-done.15.refs_4_ = bf16[512,256]{1,0:T(8,128)(2,1)S(1)} collective-permute-done((bf16[512,256]{1,0:T(8,128)(2,1)S(1)}, bf16[512,256]{1,0:T(8,128)(2,1)S(1)}, u32[]{:S(2)}, u32[]{:S(2)}) %collective-permute-start.15) | collective-permute-done | bytes 262176 | tf_op jit(solution)/shard_map/ppermute | solution.py:18
  134.1 8.5 %collective-permute-done.16.refs_5_ = bf16[512,256]{1,0:T(8,128)(2,1)} collective-permute-done((bf16[512,256]{1,0:T(8,128)(2,1)S(1)}, bf16[512,256]{1,0:T(8,128)(2,1)}, u32[]{:S(2)}, u32[]{:S(2)}) %collective-permute-start.16) | collective-permute-done | bytes 262176 | tf_op jit(solution)/shard_map/ppermute | solution.py:18
  145.8 5.5 %turn.3 = (f32[2,1024,256]{2,1,0:T(8,128)}, f32[2,1024,256]{2,1,0:T(8,128)}, bf16[4,8,32,256]{3,2,1,0:T(8,128)(2,1)}, bf16[4,8,32,256]{3,2,1,0:T(8,128)(2,1)}, b...) custom-call(s32[1]{0:T(128)} %bitcast.refs_0_, ...), custom_call_target="tpu_custom_call", output_to_operand_aliasing={{0}: (7, {}), {1}: (8, {})} | custom-call | flops 2147483648 | bytes 6291456 | tf_op jit(solution)/shard_map/turn/pallas_call | solution.py:209
  151.4 3.3 %collective-permute-start.22 = (bf16[4,8,32,256]{3,2,1,0:T(8,128)(2,1)}, bf16[4,8,32,256]{3,2,1,0:T(8,128)(2,1)S(1)}, u32[]{:S(2)}, u32[]{:S(2)}) collective-permute-start(bf16[4,8,32,256]{3,2,1,0:T(8,128)(2,1)} %get-tuple-element.53), channel_id=1, source_target_pairs={{0,96},{32,0},{64,32},{96,64},{1,97},{33,1},{65,33},{97,65},{2,98}... | collective-permute-start | bytes 1572872 | tf_op jit(solution)/shard_map/ppermute | solution.py:18
  158.7 5.4 %collective-permute-done.22.refs_2_ = bf16[4,8,32,256]{3,2,1,0:T(8,128)(2,1)S(1)} collective-permute-done((bf16[4,8,32,256]{3,2,1,0:T(8,128)(2,1)}, bf16[4,8,32,256]{3,2,1,0:T(8,128)(2,1)S(1)}, u32[]{:S(2)}, u32[]{:S(2)}) %collective-permute-start.22) | collective-permute-done | bytes 524320 | tf_op jit(solution)/shard_map/ppermute | solution.py:18
  165.3 3.4 %collective-permute-start.24 = (bf16[2,8,32,256]{3,2,1,0:T(8,128)(2,1)S(1)}, bf16[2,8,32,256]{3,2,1,0:T(8,128)(2,1)S(1)}, u32[]{:S(2)}, u32[]{:S(2)}) collective-permute-start(bf16[2,8,32,256]{3,2,1,0:T(8,128)(2,1)S(1)} %add_convert_fusion.2), channel_id=1, source_target_pairs={{0,96},{32,0},{64,32},{96,64},{1,97},{33,1},{65,33},{97,65},{2,98}... | collective-permute-start | bytes 786440 | tf_op jit(solution)/shard_map/ppermute | solution.py:18
  175.1 3.3 %collective-permute-done.23.refs_3_ = bf16[2,8,32,256]{3,2,1,0:T(8,128)(2,1)S(1)} collective-permute-done((bf16[2,8,32,256]{3,2,1,0:T(8,128)(2,1)S(1)}, bf16[2,8,32,256]{3,2,1,0:T(8,128)(2,1)S(1)}, u32[]{:S(2)}, u32[]{:S(2)}) %collective-permute-start.23) | collective-permute-done | bytes 262176 | tf_op jit(solution)/shard_map/ppermute | solution.py:18
  180.5 11.2 %all-to-all-start.3 = ((bf16[32,2,32,256]{3,2,1,0:T(8,128)(2,1)}), bf16[32,2,32,256]{3,2,1,0:T(8,128)(2,1)S(1)}, u32[]{:S(2)}, u32[]{:S(2)}) async-start(bf16[32,2,32,256]{3,2,1,0:T(8,128)(2,1)} %bitcast.42), calls=%async_computation.3 | async-start | bytes 2097152 | tf_op jit(solution)/shard_map/all_to_all | solution.py:453
  191.8 17.0 %all-to-all-done.3 = bf16[32,2,32,256]{3,2,1,0:T(8,128)(2,1)S(1)} async-done(((bf16[32,2,32,256]{3,2,1,0:T(8,128)(2,1)}), bf16[32,2,32,256]{3,2,1,0:T(8,128)(2,1)S(1)}, u32[]{:S(2)}, u32[]{:S(2)}) %all-to-all-start.3) | async-done | bytes 1048608 | tf_op jit(solution)/shard_map/all_to_all | solution.py:453
  210.2 3.5 %all-to-all-start.4 = ((bf16[4,8,32,256]{3,2,1,0:T(8,128)(2,1)}), bf16[4,8,32,256]{3,2,1,0:T(8,128)(2,1)S(1)}, u32[]{:S(2)}, u32[]{:S(2)}) async-start(bf16[4,8,32,256]{3,2,1,0:T(8,128)(2,1)} %bitcast.51), calls=%async_computation.4 | async-start | bytes 1048576 | tf_op jit(solution)/shard_map/all_to_all | solution.py:460
  215.2 4.3 %stats.2 = (f32[2,1024,256]{2,1,0:T(8,128)}, f32[2,1024,256]{2,1,0:T(8,128)}) custom-call(s32[1]{0:T(128)} %bitcast.refs_0_, bf16[4,8,32,256]{3,2,1,0:T(8,128)(2,1)} %bitcast.46, bf16[4,8,32,256]{3,2,1,0:T(8,128)(2,1)} %copy-done.6, bf16[4,8,32,256]{3,2,1,0:T(8,128)(2,1)} %copy-done.7, bf16[2,8,32,256]{3,2,1,0:T(8,128)(2,1)} %copy-done.3, ...), custom_call_target="tpu_custom_call" | custom-call | flops 1073741824 | bytes 6291456 | tf_op jit(solution)/shard_map/stats/pallas_call | solution.py:274
  219.6 4.4 %stats.3 = (f32[2,1024,256]{2,1,0:T(8,128)}, f32[2,1024,256]{2,1,0:T(8,128)}) custom-call(s32[1]{0:T(128)} %bitcast.refs_0_, bf16[4,8,4,32,256]{4,3,2,1,0:T(8,128)(2,1)} %bitcast.41, f32[2,1024,256]{2,1,0:T(8,128)S(1)} %copy-done.1, f32[2,1024,256]{2,1,0:T(8,128)S(1)} %copy-done.2, ...), custom_call_target="tpu_custom_call", output_to_operand_aliasing={{0}: (4, {}), {1}: (5, {})} | custom-call | flops 1073741824 | bytes 6291456 | tf_op jit(solution)/shard_map/stats/pallas_call | solution.py:274
  (143 shorter events, 69.7 us)
Async XLA Ops:
  6.1 11.3 %collective-permute-start.2 = (bf16[64,8,256]{2,1,0:T(8,128)(2,1)S(1)}, bf16[64,8,256]{2,1,0:T(8,128)(2,1)S(1)}, u32[]{:S(2)}, u32[]{:S(2)}) collective-permute-start(bf16[64,8,256]{2,1,0:T(8,128)(2,1)S(1)} %get-tuple-element.73), channel_id=1, source_target_pairs={{0,96},{32,0},{64,32},{96,64},{1,97},{33,1},{65,33},{97,65},{2,98}... | collective-permute-start | bytes 786440 | tf_op jit(solution)/shard_map/ppermute | solution.py:18
  7.6 10.0 %collective-permute-start.3 = (bf16[64,8,256]{2,1,0:T(8,128)(2,1)S(1)}, bf16[64,8,256]{2,1,0:T(8,128)(2,1)S(1)}, u32[]{:S(2)}, u32[]{:S(2)}) collective-permute-start(bf16[64,8,256]{2,1,0:T(8,128)(2,1)S(1)} %get-tuple-element.72), channel_id=1, source_target_pairs={{0,32},{32,64},{64,96},{96,0},{1,33},{33,65},{65,97},{97,1},{2,34}... | collective-permute-start | bytes 786440 | tf_op jit(solution)/shard_map/ppermute | solution.py:18
  23.5 12.4 %all-to-all-start = ((bf16[4,32,8,256]{3,2,1,0:T(8,128)(2,1)}), bf16[4,32,8,256]{3,2,1,0:T(8,128)(2,1)S(1)}, u32[]{:S(2)}, u32[]{:S(2)}) async-start(bf16[4,32,8,256]{3,2,1,0:T(8,128)(2,1)} %bitcast.9), calls=%async_computation | async-start | bytes 1048576 | tf_op jit(solution)/shard_map/all_to_all | solution.py:413
  37.5 21.4 %all-to-all-start.2 = ((bf16[32,32,256]{2,1,0:T(8,128)(2,1)}), bf16[32,32,256]{2,1,0:T(8,128)(2,1)S(1)}, u32[]{:S(2)}, u32[]{:S(2)}) async-start(bf16[32,32,256]{2,1,0:T(8,128)(2,1)} %broadcast_select_fusion), calls=%async_computation.2 | async-start | bytes 1048576 | tf_op jit(solution)/shard_map/all_to_all | solution.py:419
  58.9 83.7 %all-to-all-start.1 = ((bf16[32,4,32,256]{3,2,1,0:T(8,128)(2,1)}), bf16[32,4,32,256]{3,2,1,0:T(8,128)(2,1)S(1)}, u32[]{:S(2)}, u32[]{:S(2)}) async-start(bf16[32,4,32,256]{3,2,1,0:T(8,128)(2,1)} %gather_fusion.1), calls=%async_computation.1 | async-start | bytes 4194304 | tf_op jit(solution)/shard_map/all_to_all | solution.py:427
  68.8 14.5 %collective-permute-start.17 = (bf16[1024,256]{1,0:T(8,128)(2,1)S(1)}, bf16[1024,256]{1,0:T(8,128)(2,1)S(1)}, u32[]{:S(2)}, u32[]{:S(2)}) collective-permute-start(bf16[1024,256]{1,0:T(8,128)(2,1)S(1)} %get-tuple-element.75.refs_1_), channel_id=1, source_target_pairs={{0,32},{32,64},{64,96},{96,0},{1,33},{33,65},{65,97},{97,1},{2,34}... | collective-permute-start | bytes 1572872 | tf_op jit(solution)/shard_map/ppermute | solution.py:18
  69.7 13.8 %collective-permute-start.18 = (bf16[1024,256]{1,0:T(8,128)(2,1)S(1)}, bf16[1024,256]{1,0:T(8,128)(2,1)S(1)}, u32[]{:S(2)}, u32[]{:S(2)}) collective-permute-start(bf16[1024,256]{1,0:T(8,128)(2,1)S(1)} %get-tuple-element.75.refs_1_), channel_id=1, source_target_pairs={{0,96},{32,0},{64,32},{96,64},{1,97},{33,1},{65,33},{97,65},{2,98}... | collective-permute-start | bytes 1572872 | tf_op jit(solution)/shard_map/ppermute | solution.py:18
  71.5 23.0 %collective-permute-start.9 = (bf16[4,8,32,256]{3,2,1,0:T(8,128)(2,1)S(1)}, bf16[4,8,32,256]{3,2,1,0:T(8,128)(2,1)S(1)}, u32[]{:S(2)}, u32[]{:S(2)}) collective-permute-start(bf16[4,8,32,256]{3,2,1,0:T(8,128)(2,1)S(1)} %bitcast.43), channel_id=1, source_target_pairs={{0,32},{32,64},{64,96},{96,0},{1,33},{33,65},{65,97},{97,1},{2,34}... | collective-permute-start | bytes 1572872 | tf_op jit(solution)/shard_map/ppermute | solution.py:18
  71.5 23.5 %collective-permute-start.10 = (bf16[4,8,32,256]{3,2,1,0:T(8,128)(2,1)S(1)}, bf16[4,8,32,256]{3,2,1,0:T(8,128)(2,1)S(1)}, u32[]{:S(2)}, u32[]{:S(2)}) collective-permute-start(bf16[4,8,32,256]{3,2,1,0:T(8,128)(2,1)S(1)} %bitcast.44), channel_id=1, source_target_pairs={{0,96},{32,0},{64,32},{96,64},{1,97},{33,1},{65,33},{97,65},{2,98}... | collective-permute-start | bytes 1572872 | tf_op jit(solution)/shard_map/ppermute | solution.py:18
  83.3 16.8 %collective-permute-start.19 = (bf16[512,256]{1,0:T(8,128)(2,1)S(1)}, bf16[512,256]{1,0:T(8,128)(2,1)S(1)}, u32[]{:S(2)}, u32[]{:S(2)}) collective-permute-start(bf16[512,256]{1,0:T(8,128)(2,1)S(1)} %slice.64), channel_id=1, source_target_pairs={{0,32},{32,64},{64,96},{96,0},{1,33},{33,65},{65,97},{97,1},{2,34}... | collective-permute-start | bytes 786440 | tf_op jit(solution)/shard_map/ppermute | solution.py:18
  83.4 43.2 %collective-permute-start.13 = (bf16[1024,256]{1,0:T(8,128)(2,1)S(1)}, bf16[1024,256]{1,0:T(8,128)(2,1)S(1)}, u32[]{:S(2)}, u32[]{:S(2)}) collective-permute-start(bf16[1024,256]{1,0:T(8,128)(2,1)S(1)} %get-tuple-element.76.refs_1_), channel_id=1, source_target_pairs={{0,32},{32,64},{64,96},{96,0},{1,33},{33,65},{65,97},{97,1},{2,34}... | collective-permute-start | bytes 1572872 | tf_op jit(solution)/shard_map/ppermute | solution.py:18
  83.5 43.2 %collective-permute-start.14 = (bf16[1024,256]{1,0:T(8,128)(2,1)S(1)}, bf16[1024,256]{1,0:T(8,128)(2,1)S(1)}, u32[]{:S(2)}, u32[]{:S(2)}) collective-permute-start(bf16[1024,256]{1,0:T(8,128)(2,1)S(1)} %get-tuple-element.76.refs_1_), channel_id=1, source_target_pairs={{0,96},{32,0},{64,32},{96,64},{1,97},{33,1},{65,33},{97,65},{2,98}... | collective-permute-start | bytes 1572872 | tf_op jit(solution)/shard_map/ppermute | solution.py:18
  94.5 16.2 %collective-permute-start.20 = (bf16[512,256]{1,0:T(8,128)(2,1)S(1)}, bf16[512,256]{1,0:T(8,128)(2,1)S(1)}, u32[]{:S(2)}, u32[]{:S(2)}) collective-permute-start(bf16[512,256]{1,0:T(8,128)(2,1)S(1)} %slice.65), channel_id=1, source_target_pairs={{0,96},{32,0},{64,32},{96,64},{1,97},{33,1},{65,33},{97,65},{2,98}... | collective-permute-start | bytes 786440 | tf_op jit(solution)/shard_map/ppermute | solution.py:18
  95.0 22.0 %collective-permute-start.11 = (bf16[2,8,32,256]{3,2,1,0:T(8,128)(2,1)S(1)}, bf16[2,8,32,256]{3,2,1,0:T(8,128)(2,1)S(1)}, u32[]{:S(2)}, u32[]{:S(2)}) collective-permute-start(bf16[2,8,32,256]{3,2,1,0:T(8,128)(2,1)S(1)} %slice.58), channel_id=1, source_target_pairs={{0,32},{32,64},{64,96},{96,0},{1,33},{33,65},{65,97},{97,1},{2,34}... | collective-permute-start | bytes 786440 | tf_op jit(solution)/shard_map/ppermute | solution.py:18
  100.2 16.9 %collective-permute-start.12 = (bf16[2,8,32,256]{3,2,1,0:T(8,128)(2,1)S(1)}, bf16[2,8,32,256]{3,2,1,0:T(8,128)(2,1)S(1)}, u32[]{:S(2)}, u32[]{:S(2)}) collective-permute-start(bf16[2,8,32,256]{3,2,1,0:T(8,128)(2,1)S(1)} %slice.59), channel_id=1, source_target_pairs={{0,96},{32,0},{64,32},{96,64},{1,97},{33,1},{65,33},{97,65},{2,98}... | collective-permute-start | bytes 786440 | tf_op jit(solution)/shard_map/ppermute | solution.py:18
  124.2 30.5 %collective-permute-start.26 = (bf16[4,8,32,256]{3,2,1,0:T(8,128)(2,1)}, bf16[4,8,32,256]{3,2,1,0:T(8,128)(2,1)S(1)}, u32[]{:S(2)}, u32[]{:S(2)}) collective-permute-start(bf16[4,8,32,256]{3,2,1,0:T(8,128)(2,1)} %get-tuple-element.58), channel_id=1, source_target_pairs={{0,96},{32,0},{64,32},{96,64},{1,97},{33,1},{65,33},{97,65},{2,98}... | collective-permute-start | bytes 1572872 | tf_op jit(solution)/shard_map/ppermute | solution.py:18
  126.7 15.9 %collective-permute-start.16 = (bf16[512,256]{1,0:T(8,128)(2,1)S(1)}, bf16[512,256]{1,0:T(8,128)(2,1)}, u32[]{:S(2)}, u32[]{:S(2)}) collective-permute-start(bf16[512,256]{1,0:T(8,128)(2,1)S(1)} %slice.62), channel_id=1, source_target_pairs={{0,96},{32,0},{64,32},{96,64},{1,97},{33,1},{65,33},{97,65},{2,98}... | collective-permute-start | bytes 786440 | tf_op jit(solution)/shard_map/ppermute | solution.py:18
  129.4 28.1 %collective-permute-start.25 = (bf16[4,8,32,256]{3,2,1,0:T(8,128)(2,1)}, bf16[4,8,32,256]{3,2,1,0:T(8,128)(2,1)}, u32[]{:S(2)}, u32[]{:S(2)}) collective-permute-start(bf16[4,8,32,256]{3,2,1,0:T(8,128)(2,1)} %get-tuple-element.57), channel_id=1, source_target_pairs={{0,32},{32,64},{64,96},{96,0},{1,33},{33,65},{65,97},{97,1},{2,34}... | collective-permute-start | bytes 1572872 | tf_op jit(solution)/shard_map/ppermute | solution.py:18
  151.4 12.7 %collective-permute-start.22 = (bf16[4,8,32,256]{3,2,1,0:T(8,128)(2,1)}, bf16[4,8,32,256]{3,2,1,0:T(8,128)(2,1)S(1)}, u32[]{:S(2)}, u32[]{:S(2)}) collective-permute-start(bf16[4,8,32,256]{3,2,1,0:T(8,128)(2,1)} %get-tuple-element.53), channel_id=1, source_target_pairs={{0,96},{32,0},{64,32},{96,64},{1,97},{33,1},{65,33},{97,65},{2,98}... | collective-permute-start | bytes 1572872 | tf_op jit(solution)/shard_map/ppermute | solution.py:18
  154.7 13.9 %collective-permute-start.21 = (bf16[4,8,32,256]{3,2,1,0:T(8,128)(2,1)}, bf16[4,8,32,256]{3,2,1,0:T(8,128)(2,1)S(1)}, u32[]{:S(2)}, u32[]{:S(2)}) collective-permute-start(bf16[4,8,32,256]{3,2,1,0:T(8,128)(2,1)} %get-tuple-element.52), channel_id=1, source_target_pairs={{0,32},{32,64},{64,96},{96,0},{1,33},{33,65},{65,97},{97,1},{2,34}... | collective-permute-start | bytes 1572872 | tf_op jit(solution)/shard_map/ppermute | solution.py:18
  154.8 14.8 %collective-permute-start.28 = (bf16[2,8,32,256]{3,2,1,0:T(8,128)(2,1)S(1)}, bf16[2,8,32,256]{3,2,1,0:T(8,128)(2,1)S(1)}, u32[]{:S(2)}, u32[]{:S(2)}) collective-permute-start(bf16[2,8,32,256]{3,2,1,0:T(8,128)(2,1)S(1)} %add_convert_fusion), channel_id=1, source_target_pairs={{0,96},{32,0},{64,32},{96,64},{1,97},{33,1},{65,33},{97,65},{2,98}... | collective-permute-start | bytes 786440 | tf_op jit(solution)/shard_map/ppermute | solution.py:18
  158.6 14.1 %collective-permute-start.27 = (bf16[2,8,32,256]{3,2,1,0:T(8,128)(2,1)S(1)}, bf16[2,8,32,256]{3,2,1,0:T(8,128)(2,1)S(1)}, u32[]{:S(2)}, u32[]{:S(2)}) collective-permute-start(bf16[2,8,32,256]{3,2,1,0:T(8,128)(2,1)S(1)} %add_convert_fusion.1), channel_id=1, source_target_pairs={{0,32},{32,64},{64,96},{96,0},{1,33},{33,65},{65,97},{97,1},{2,34}... | collective-permute-start | bytes 786440 | tf_op jit(solution)/shard_map/ppermute | solution.py:18
  180.5 28.3 %all-to-all-start.3 = ((bf16[32,2,32,256]{3,2,1,0:T(8,128)(2,1)}), bf16[32,2,32,256]{3,2,1,0:T(8,128)(2,1)S(1)}, u32[]{:S(2)}, u32[]{:S(2)}) async-start(bf16[32,2,32,256]{3,2,1,0:T(8,128)(2,1)} %bitcast.42), calls=%async_computation.3 | async-start | bytes 2097152 | tf_op jit(solution)/shard_map/all_to_all | solution.py:453
  210.2 13.8 %all-to-all-start.4 = ((bf16[4,8,32,256]{3,2,1,0:T(8,128)(2,1)}), bf16[4,8,32,256]{3,2,1,0:T(8,128)(2,1)S(1)}, u32[]{:S(2)}, u32[]{:S(2)}) async-start(bf16[4,8,32,256]{3,2,1,0:T(8,128)(2,1)} %bitcast.51), calls=%async_computation.4 | async-start | bytes 1048576 | tf_op jit(solution)/shard_map/all_to_all | solution.py:460
  (37 other events, 457.9 us)

commit v4 on v3

--- a/solution.py
+++ b/solution.py
@@ -11,7 +11,6 @@
 BF = jnp.bfloat16
 F32 = jnp.float32
 TILE = 1024
-VMEM_TURN = 20 * 2**20
 
 
 def shift(x, by, n):
@@ -58,41 +57,53 @@
     return pl.ds(k * width, width)
 
 
-def prep_kernel(n, s, count, *refs):
+def load_left(load, parts, lb, width):
+    tall = lb.shape[0] // 2
+    waits = [[load(parts[k], lb.at[:, cols(k, width)])] for k in range(3)]
+    waits.append(
+        [
+            load(parts[3], lb.at[pl.ds(0, tall), cols(3, width)]),
+            load(parts[4], lb.at[pl.ds(tall, tall), cols(3, width)]),
+        ]
+    )
+    return waits
+
+
+def load_state(load, s, me, n, r_hbm, first_hbm, second_hbm, rf, first, second):
+    width = rf.shape[1]
+    waits = [
+        load(r_hbm.at[s, rows_at(me, OFFSETS[k], n, width), :], rf.at[cols(k, width), :])
+        for k in range(4)
+    ]
+    return waits, [load(first_hbm.at[s], first), load(second_hbm.at[s], second)]
+
+
+def prep_kernel(n, s, *refs):
     me_ref = refs[0]
-    l_parts = refs[1 : 1 + count]
-    r_hbm, first_hbm, second_hbm = refs[1 + count : 4 + count]
-    lb, lt, r, first, second, sems = refs[-6:]
+    l_parts = refs[1:6]
+    lb, lt, r, first, second, rf, sems = refs[-7:]
     me = me_ref[0]
     width = r.shape[1]
-    tall = lb.shape[0] // 2
-    load, loads = starter(sems)
-    for k in range(3):
-        load(l_parts[k], lb.at[:, cols(k, width)])
-    if count == 4:
-        load(l_parts[3], lb.at[:, cols(3, width)])
-    else:
-        load(l_parts[3], lb.at[pl.ds(0, tall), cols(3, width)])
-        load(l_parts[4], lb.at[pl.ds(tall, tall), cols(3, width)])
+    load, _ = starter(sems)
+    w_l = load_left(load, l_parts, lb, width)
+    w_r, w_m = load_state(load, s, me, n, *refs[6:9], rf, first, second)
     for k in range(4):
-        load(r_hbm.at[s, rows_at(me, OFFSETS[k], n, width), :], r.at[cols(k, width), :])
-    load(first_hbm.at[s], first)
-    load(second_hbm.at[s], second)
-    for k in range(4):
-        loads[k].wait()
-        if k == 3 and count == 5:
-            loads[4].wait()
+        for c in w_l[k]:
+            c.wait()
         lt[cols(k, width), :] = lb[:, cols(k, width)].T
-    for c in loads[count:]:
-        c.wait()
-
-
-def prep(me, s, lb, r, first, second, after, n):
+    for c in w_r:
+        c.wait()
+    r[...] = rf[...].astype(BF)
+    for c in w_m:
+        c.wait()
+
+
+def prep(me, s, lb, r, first, second, n):
     _, block, width = r.shape
     hbm = pl.BlockSpec(memory_space=pltpu.HBM)
     vmem = pl.BlockSpec(memory_space=pltpu.VMEM)
     return pl.pallas_call(
-        functools.partial(prep_kernel, n, s, len(lb)),
+        functools.partial(prep_kernel, n, s),
         out_shape=[
             pltpu.VMEM((block, block), BF),
             pltpu.VMEM((block, block), BF),
@@ -100,13 +111,49 @@
             pltpu.VMEM((block, width), F32),
             pltpu.VMEM((block, width), F32),
         ],
-        in_specs=[pl.BlockSpec(memory_space=pltpu.SMEM)] + [hbm] * (3 + len(lb)) + [vmem] * len(after),
+        in_specs=[pl.BlockSpec(memory_space=pltpu.SMEM)] + [hbm] * 8,
         out_specs=[vmem] * 5,
-        scratch_shapes=[pltpu.SemaphoreType.DMA((11,))],
+        scratch_shapes=[pltpu.VMEM((block, width), F32), pltpu.SemaphoreType.DMA((11,))],
         compiler_params=pltpu.CompilerParams(vmem_limit_bytes=20 * 2**20),
         cost_estimate=pl.CostEstimate(flops=2**22, bytes_accessed=6 * 2**20, transcendentals=0),
         name="prep",
-    )(me, *[in_hbm(x) for x in lb], in_hbm(r), in_hbm(first), in_hbm(second), *[in_vmem(x) for x in after])
+    )(me, *[in_hbm(x) for x in (*lb, r, first, second)])
+
+
+def flip_kernel(*refs):
+    l_parts, out = refs[:5], refs[5]
+    lb, lt, sems, out_sems = refs[6:]
+    width = l_parts[0].shape[1]
+    load, _ = starter(sems)
+    store, stores = starter(out_sems)
+    w_l = load_left(load, l_parts, lb, width)
+    for k in range(4):
+        for c in w_l[k]:
+            c.wait()
+        lt[cols(k, width), :] = lb[:, cols(k, width)].T
+        store(lt.at[cols(k, width), :], out.at[cols(k, width), :])
+    for c in stores:
+        c.wait()
+
+
+def flip(lb):
+    block = lb[0].shape[0]
+    hbm = pl.BlockSpec(memory_space=pltpu.HBM)
+    return pl.pallas_call(
+        flip_kernel,
+        out_shape=pltpu.HBM((block, block), BF),
+        in_specs=[hbm] * 5,
+        out_specs=hbm,
+        scratch_shapes=[
+            pltpu.VMEM((block, block), BF),
+            pltpu.VMEM((block, block), BF),
+            pltpu.SemaphoreType.DMA((5,)),
+            pltpu.SemaphoreType.DMA((4,)),
+        ],
+        compiler_params=pltpu.CompilerParams(vmem_limit_bytes=20 * 2**20),
+        cost_estimate=pl.CostEstimate(flops=2**22, bytes_accessed=4 * 2**20, transcendentals=0),
+        name="flip",
+    )(*[in_hbm(x) for x in lb])
 
 
 def load_grad(load, s, parts, g, width, near=False):
@@ -138,7 +185,14 @@
 def turn_kernel(n, s, count, *refs):
     me_ref = refs[0]
     g_parts = refs[1 : 1 + count]
-    lb, lt, r, first, second = refs[1 + count : 6 + count]
+    if s == 0:
+        lb, lt, r, first, second = refs[1 + count : 6 + count]
+    else:
+        l_parts = refs[1 + count : 6 + count]
+        lt_hbm = refs[6 + count]
+        hold = refs[7 + count : 10 + count]
+        lb, lt, r, first, second, rf, own_sems = refs[-16:-9]
+        refs = refs[:-16] + refs[-9:]
     nf_hbm, ns_hbm, own_out, to_right, to_left, right_t, left_b = refs[-16:-9]
     g, z, d, t, p, nf, ns, sems, out_sems = refs[-9:]
     me = me_ref[0]
@@ -147,8 +201,18 @@
     half = pieces // 2
     load, _ = starter(sems)
     store, stores = starter(out_sems)
+    w_r, w_t, w_m, w_l = [], [], [], []
+    if s == 1:
+        fetch, _ = starter(own_sems)
+        w_r, w_m = load_state(fetch, s, me, n, *hold, rf, first, second)
+        w_t = [fetch(lt_hbm, lt)]
+        w_l = load_left(fetch, l_parts, lb, width)
     for c in load_grad(load, s, g_parts, g, width, near=True):
         c.wait()
+    for c in w_r:
+        c.wait()
+    if s == 1:
+        r[...] = rf[...].astype(BF)
     per = TILE // (pieces * piece)
     tiles = block // TILE
 
@@ -158,6 +222,8 @@
         at = pl.ds(pl.multiple_of(i * TILE, TILE), TILE)
         z[at, :] = dot(rows, r[...], NN).astype(BF)
 
+    for c in w_t + w_m:
+        c.wait()
     for k in range(4):
         at = rows_at(me, OFFSETS[k], n, width)
         turned = dot(lt[cols(k, width), :], z[...], NN)
@@ -168,6 +234,9 @@
         d[cols(k, width), :] = (a / (jnp.sqrt(b) + 1e-8)).astype(BF)
     store(nf, nf_hbm.at[s])
     store(ns, ns_hbm.at[s])
+    for group in w_l:
+        for c in group:
+            c.wait()
 
     @pl.loop(0, tiles)
     def _(i):
@@ -198,11 +267,15 @@
 
 
 def turn(me, s, g, ready, before, n, per_owner):
-    block, width = ready[2].shape
+    block, width = ready[0].shape[0], g[0].shape[-1]
     pieces, bands, piece = g[0].shape[0], g[0].shape[1], g[0].shape[-2]
     hbm = pl.BlockSpec(memory_space=pltpu.HBM)
     vmem = pl.BlockSpec(memory_space=pltpu.VMEM)
     far = 3 if s == 0 else 0
+    extra = []
+    if s == 1:
+        extra = [pltpu.VMEM((block, block), BF)] * 2 + [pltpu.VMEM((block, width), BF)]
+        extra += [pltpu.VMEM((block, width), F32)] * 3 + [pltpu.SemaphoreType.DMA((12,))]
     state = pltpu.HBM((per_owner, block, width), F32)
     whole = pltpu.HBM((pieces, bands, piece, width), BF)
     part = pltpu.HBM((pieces // 2, bands, piece, width), BF)
@@ -212,10 +285,11 @@
         in_specs=[pl.BlockSpec(memory_space=pltpu.SMEM)]
         + [hbm] * far
         + [vmem] * (len(g) - far)
-        + [vmem] * 5
+        + [vmem if s == 0 else hbm] * len(ready)
         + [hbm] * len(before),
         out_specs=[hbm] * 7,
-        scratch_shapes=[
+        scratch_shapes=extra
+        + [
             pltpu.VMEM((bands, pieces, piece, block), BF),
             pltpu.VMEM((block, width), BF),
             pltpu.VMEM((block, width), BF),
@@ -226,8 +300,8 @@
             pltpu.SemaphoreType.DMA((16,)),
             pltpu.SemaphoreType.DMA((18,)),
         ],
-        input_output_aliases={6 + len(g) + i: i for i in range(len(before))},
-        compiler_params=pltpu.CompilerParams(vmem_limit_bytes=VMEM_TURN),
+        input_output_aliases={1 + len(ready) + len(g) + i: i for i in range(len(before))},
+        compiler_params=pltpu.CompilerParams(vmem_limit_bytes=(20 if s == 0 else 32) * 2**20),
         cost_estimate=pl.CostEstimate(
             flops=8 * block * block * width, bytes_accessed=6 * 2**20, transcendentals=0
         ),
@@ -235,7 +309,8 @@
     )(
         me,
         *[in_hbm(x) for x in g[:far]],
-        *[in_vmem(x) for x in (*g[far:], *ready)],
+        *[in_vmem(x) for x in g[far:]],
+        *[in_vmem(x) if s == 0 else in_hbm(x) for x in ready],
         *[in_hbm(x) for x in before],
     )
 
@@ -407,7 +482,6 @@
         ]
     )
 
-    right_bf = right_basis.astype(BF)
     pieces_l = [gather_columns(left_basis[s].astype(BF), n) for s in range(2)]
 
     spread = lax.all_to_all(
@@ -431,9 +505,9 @@
     ]
 
     me_s = me.reshape(1).astype(jnp.int32)
-    ready, late = [], ((), pieces_g[1])
-    for s in range(per_owner):
-        ready.append(prep(me_s, s, pieces_l[s], right_bf, first, second, late[s], n))
+    held = prep(me_s, 0, pieces_l[0], right_basis, first, second, n)
+    flipped = flip(pieces_l[1])
+    ready = [held, (*pieces_l[1], flipped, right_basis, first, second)]
     state, terms = (), []
     for s in range(per_owner):
         nf, ns, own, to_right, to_left, right_t, left_b = turn(

time: 226 us -> 229 us (1.013)
  Pallas kernels: 31.2 us -> 33.6 us
    pallas_call x2, Pallas kernels: 12.7 us -> 15.4 us  [turn(): pl.pallas_call(functools.partial(turn_kernel, n, s, len(g)), out_shape=[s...]
  transfers between devices with their start and end apart: 34 -> 34, of which waited for: 20 -> 20; matrix products, arithmetic and copies ran while one was open for 4% -> 3% of each run, Pallas kernels for 13% -> 14%
where the time goes in v4:
time: 229 us; the launch traced here: 228 us
  waiting for transfers between devices  102 us (45%)
  starting transfers between devices  73.4 us (32%)
  Pallas kernels  33.6 us (15%)
  local copies, waits for them, and re-layouts  11 us (5%)
  other arithmetic  6.96 us (3%)
    ppermute x29, waiting for transfers between devices, shift(): return lax.ppermute(x, 'dp', [(i, (i + by) % n) for i in range(n)])  77.8 us
    ppermute x29, starting transfers between devices, shift(): return lax.ppermute(x, 'dp', [(i, (i + by) % n) for i in range(n)])  36.4 us
    all_to_all x1, waiting for transfers between devices, local(): lax.all_to_all(parted[0].reshape(members, per_owner, piece, width), ('gr'...  17 us
    pallas_call x2, Pallas kernels, turn(): pl.pallas_call(functools.partial(turn_kernel, n, s, len(g)), out_shape=[s...  15.4 us
    all_to_all x1, starting transfers between devices, local(): lax.all_to_all(parted[0].reshape(members, per_owner, piece, width), ('gr'...  11.2 us
    all_to_all x1, starting transfers between devices, local(): landed0 = lax.all_to_all(leaving, ('gr', 'band'), 0, 0, tiled=True)  8.8 us
    pallas_call x2, Pallas kernels, stats(): pl.pallas_call(functools.partial(stats_kernel, n, s, len(g)), grid=(1,),...  8.68 us
    all_to_all x1, starting transfers between devices, local(): landed1 = lax.all_to_all(leaving, ('gr', 'band'), 0, 0, tiled=True)  8.08 us
  transfers between devices with their start and end apart: 34, of which 20 were waited for; matrix products, arithmetic and copies ran while one was open for 3% of the time, Pallas kernels for 14%

profile of v4, /device:TPU:1, one launch (start us, length us, event | category | flops | bytes accessed | tf_op | source)
XLA Modules:
  0.0 227.8 jit_solution(3478648045063577170)
XLA Ops:
  7.9 4.2 %collective-permute-done = bf16[64,8,256]{2,1,0:T(8,128)(2,1)} collective-permute-done((bf16[64,8,256]{2,1,0:T(8,128)(2,1)}, bf16[64,8,256]{2,1,0:T(8,128)(2,1)}, u32[]{:S(2)}, u32[]{:S(2)}) %collective-permute-start) | collective-permute-done | bytes 262176 | tf_op jit(solution)/shard_map/ppermute | solution.py:17
  17.6 4.9 %collective-permute-done.1 = bf16[64,8,256]{2,1,0:T(8,128)(2,1)S(1)} collective-permute-done((bf16[64,8,256]{2,1,0:T(8,128)(2,1)S(1)}, bf16[64,8,256]{2,1,0:T(8,128)(2,1)S(1)}, u32[]{:S(2)}, u32[]{:S(2)}) %collective-permute-start.1) | collective-permute-done | bytes 262176 | tf_op jit(solution)/shard_map/ppermute | solution.py:17
  23.5 5.4 %all-to-all-start = ((bf16[4,32,8,256]{3,2,1,0:T(8,128)(2,1)}), bf16[4,32,8,256]{3,2,1,0:T(8,128)(2,1)S(1)}, u32[]{:S(2)}, u32[]{:S(2)}) async-start(bf16[4,32,8,256]{3,2,1,0:T(8,128)(2,1)} %bitcast.9), calls=%async_computation | async-start | bytes 1048576 | tf_op jit(solution)/shard_map/all_to_all | solution.py:487
  29.1 6.8 %all-to-all-done = bf16[4,32,8,256]{3,2,1,0:T(8,128)(2,1)S(1)} async-done(((bf16[4,32,8,256]{3,2,1,0:T(8,128)(2,1)}), bf16[4,32,8,256]{3,2,1,0:T(8,128)(2,1)S(1)}, u32[]{:S(2)}, u32[]{:S(2)}) %all-to-all-start) | async-done | bytes 524320 | tf_op jit(solution)/shard_map/all_to_all | solution.py:487
  37.5 8.8 %all-to-all-start.2 = ((bf16[32,32,256]{2,1,0:T(8,128)(2,1)}), bf16[32,32,256]{2,1,0:T(8,128)(2,1)S(1)}, u32[]{:S(2)}, u32[]{:S(2)}) async-start(bf16[32,32,256]{2,1,0:T(8,128)(2,1)} %broadcast_select_fusion), calls=%async_computation.2 | async-start | bytes 1048576 | tf_op jit(solution)/shard_map/all_to_all | solution.py:493
  53.0 3.8 %collective-permute-done.8 = bf16[8,32,256]{2,1,0:T(8,128)(2,1)S(1)} collective-permute-done((bf16[8,32,256]{2,1,0:T(8,128)(2,1)S(1)}, bf16[8,32,256]{2,1,0:T(8,128)(2,1)S(1)}, u32[]{:S(2)}, u32[]{:S(2)}) %collective-permute-start.8) | collective-permute-done | bytes 131104 | tf_op jit(solution)/shard_map/ppermute | solution.py:17
  58.9 8.1 %all-to-all-start.1 = ((bf16[32,4,32,256]{3,2,1,0:T(8,128)(2,1)}), bf16[32,4,32,256]{3,2,1,0:T(8,128)(2,1)S(1)}, u32[]{:S(2)}, u32[]{:S(2)}) async-start(bf16[32,4,32,256]{3,2,1,0:T(8,128)(2,1)} %gather_fusion.1), calls=%async_computation.1 | async-start | bytes 4194304 | tf_op jit(solution)/shard_map/all_to_all | solution.py:501
  74.2 9.1 %collective-permute-done.17.refs_2_ = bf16[1024,256]{1,0:T(8,128)(2,1)S(1)} collective-permute-done((bf16[1024,256]{1,0:T(8,128)(2,1)S(1)}, bf16[1024,256]{1,0:T(8,128)(2,1)S(1)}, u32[]{:S(2)}, u32[]{:S(2)}) %collective-permute-start.17) | collective-permute-done | bytes 524320 | tf_op jit(solution)/shard_map/ppermute | solution.py:17
  86.2 8.4 %collective-permute-done.9.refs_2_ = bf16[4,8,32,256]{3,2,1,0:T(8,128)(2,1)S(1)} collective-permute-done((bf16[4,8,32,256]{3,2,1,0:T(8,128)(2,1)S(1)}, bf16[4,8,32,256]{3,2,1,0:T(8,128)(2,1)S(1)}, u32[]{:S(2)}, u32[]{:S(2)}) %collective-permute-start.9) | collective-permute-done | bytes 524320 | tf_op jit(solution)/shard_map/ppermute | solution.py:17
  96.1 4.0 %collective-permute-done.19.refs_4_ = bf16[512,256]{1,0:T(8,128)(2,1)S(1)} collective-permute-done((bf16[512,256]{1,0:T(8,128)(2,1)S(1)}, bf16[512,256]{1,0:T(8,128)(2,1)S(1)}, u32[]{:S(2)}, u32[]{:S(2)}) %collective-permute-start.19) | collective-permute-done | bytes 262176 | tf_op jit(solution)/shard_map/ppermute | solution.py:17
  100.6 10.2 %collective-permute-done.20.refs_5_ = bf16[512,256]{1,0:T(8,128)(2,1)S(1)} collective-permute-done((bf16[512,256]{1,0:T(8,128)(2,1)S(1)}, bf16[512,256]{1,0:T(8,128)(2,1)S(1)}, u32[]{:S(2)}, u32[]{:S(2)}) %collective-permute-start.20) | collective-permute-done | bytes 262176 | tf_op jit(solution)/shard_map/ppermute | solution.py:17
  117.0 7.2 %turn.2 = (f32[2,1024,256]{2,1,0:T(8,128)}, f32[2,1024,256]{2,1,0:T(8,128)}, bf16[4,8,32,256]{3,2,1,0:T(8,128)(2,1)}, bf16[4,8,32,256]{3,2,1,0:T(8,128)(2,1)}, b...) custom-call(s32[1]{0:T(128)} %bitcast.refs_0_, ...), custom_call_target="tpu_custom_call" | custom-call | flops 2147483648 | bytes 6291456 | tf_op jit(solution)/shard_map/turn/pallas_call | solution.py:282
  129.4 4.6 %collective-permute-done.15.refs_3_.refs_5_ = bf16[512,256]{1,0:T(8,128)(2,1)S(1)} collective-permute-done((bf16[512,256]{1,0:T(8,128)(2,1)S(1)}, bf16[512,256]{1,0:T(8,128)(2,1)S(1)}, u32[]{:S(2)}, u32[]{:S(2)}) %collective-permute-start.15) | collective-permute-done | bytes 262176 | tf_op jit(solution)/shard_map/ppermute | solution.py:17
  134.1 8.4 %collective-permute-done.16.refs_4_.refs_6_ = bf16[512,256]{1,0:T(8,128)(2,1)S(1)} collective-permute-done((bf16[512,256]{1,0:T(8,128)(2,1)S(1)}, bf16[512,256]{1,0:T(8,128)(2,1)S(1)}, u32[]{:S(2)}, u32[]{:S(2)}) %collective-permute-start.16) | collective-permute-done | bytes 262176 | tf_op jit(solution)/shard_map/ppermute | solution.py:17
  146.0 8.2 %turn.3 = (f32[2,1024,256]{2,1,0:T(8,128)}, f32[2,1024,256]{2,1,0:T(8,128)}, bf16[4,8,32,256]{3,2,1,0:T(8,128)(2,1)}, bf16[4,8,32,256]{3,2,1,0:T(8,128)(2,1)}, b...) custom-call(s32[1]{0:T(128)} %bitcast.refs_0_, ...), custom_call_target="tpu_custom_call", output_to_operand_aliasing={{0}: (11, {}), {1}: (12, {})} | custom-call | flops 2147483648 | bytes 6291456 | tf_op jit(solution)/shard_map/turn/pallas_call | solution.py:282
  154.2 3.3 %collective-permute-start.22 = (bf16[4,8,32,256]{3,2,1,0:T(8,128)(2,1)}, bf16[4,8,32,256]{3,2,1,0:T(8,128)(2,1)S(1)}, u32[]{:S(2)}, u32[]{:S(2)}) collective-permute-start(bf16[4,8,32,256]{3,2,1,0:T(8,128)(2,1)} %get-tuple-element.43), channel_id=1, source_target_pairs={{0,96},{32,0},{64,32},{96,64},{1,97},{33,1},{65,33},{97,65},{2,98}... | collective-permute-start | bytes 1572872 | tf_op jit(solution)/shard_map/ppermute | solution.py:17
  160.5 6.3 %collective-permute-done.22.refs_2_ = bf16[4,8,32,256]{3,2,1,0:T(8,128)(2,1)S(1)} collective-permute-done((bf16[4,8,32,256]{3,2,1,0:T(8,128)(2,1)}, bf16[4,8,32,256]{3,2,1,0:T(8,128)(2,1)S(1)}, u32[]{:S(2)}, u32[]{:S(2)}) %collective-permute-start.22) | collective-permute-done | bytes 524320 | tf_op jit(solution)/shard_map/ppermute | solution.py:17
  168.1 3.6 %collective-permute-start.24 = (bf16[2,8,32,256]{3,2,1,0:T(8,128)(2,1)S(1)}, bf16[2,8,32,256]{3,2,1,0:T(8,128)(2,1)S(1)}, u32[]{:S(2)}, u32[]{:S(2)}) collective-permute-start(bf16[2,8,32,256]{3,2,1,0:T(8,128)(2,1)S(1)} %add_convert_fusion.2), channel_id=1, source_target_pairs={{0,96},{32,0},{64,32},{96,64},{1,97},{33,1},{65,33},{97,65},{2,98}... | collective-permute-start | bytes 786440 | tf_op jit(solution)/shard_map/ppermute | solution.py:17
  178.0 3.3 %collective-permute-done.23.refs_3_ = bf16[2,8,32,256]{3,2,1,0:T(8,128)(2,1)S(1)} collective-permute-done((bf16[2,8,32,256]{3,2,1,0:T(8,128)(2,1)S(1)}, bf16[2,8,32,256]{3,2,1,0:T(8,128)(2,1)S(1)}, u32[]{:S(2)}, u32[]{:S(2)}) %collective-permute-start.23) | collective-permute-done | bytes 262176 | tf_op jit(solution)/shard_map/ppermute | solution.py:17
  183.3 11.2 %all-to-all-start.3 = ((bf16[32,2,32,256]{3,2,1,0:T(8,128)(2,1)}), bf16[32,2,32,256]{3,2,1,0:T(8,128)(2,1)S(1)}, u32[]{:S(2)}, u32[]{:S(2)}) async-start(bf16[32,2,32,256]{3,2,1,0:T(8,128)(2,1)} %bitcast.41), calls=%async_computation.3 | async-start | bytes 2097152 | tf_op jit(solution)/shard_map/all_to_all | solution.py:527
  194.6 17.0 %all-to-all-done.3 = bf16[32,2,32,256]{3,2,1,0:T(8,128)(2,1)S(1)} async-done(((bf16[32,2,32,256]{3,2,1,0:T(8,128)(2,1)}), bf16[32,2,32,256]{3,2,1,0:T(8,128)(2,1)S(1)}, u32[]{:S(2)}, u32[]{:S(2)}) %all-to-all-start.3) | async-done | bytes 1048608 | tf_op jit(solution)/shard_map/all_to_all | solution.py:527
  213.0 3.5 %all-to-all-start.4 = ((bf16[4,8,32,256]{3,2,1,0:T(8,128)(2,1)}), bf16[4,8,32,256]{3,2,1,0:T(8,128)(2,1)S(1)}, u32[]{:S(2)}, u32[]{:S(2)}) async-start(bf16[4,8,32,256]{3,2,1,0:T(8,128)(2,1)} %bitcast.50), calls=%async_computation.4 | async-start | bytes 1048576 | tf_op jit(solution)/shard_map/all_to_all | solution.py:534
  218.0 4.3 %stats.2 = (f32[2,1024,256]{2,1,0:T(8,128)}, f32[2,1024,256]{2,1,0:T(8,128)}) custom-call(s32[1]{0:T(128)} %bitcast.refs_0_, bf16[4,8,32,256]{3,2,1,0:T(8,128)(2,1)} %bitcast.45, bf16[4,8,32,256]{3,2,1,0:T(8,128)(2,1)} %copy-done.7, bf16[4,8,32,256]{3,2,1,0:T(8,128)(2,1)} %copy-done.8, bf16[2,8,32,256]{3,2,1,0:T(8,128)(2,1)} %copy-done.3, ...), custom_call_target="tpu_custom_call" | custom-call | flops 1073741824 | bytes 6291456 | tf_op jit(solution)/shard_map/stats/pallas_call | solution.py:349
  222.4 4.4 %stats.3 = (f32[2,1024,256]{2,1,0:T(8,128)}, f32[2,1024,256]{2,1,0:T(8,128)}) custom-call(s32[1]{0:T(128)} %bitcast.refs_0_, bf16[4,8,4,32,256]{4,3,2,1,0:T(8,128)(2,1)} %bitcast.40, f32[2,1024,256]{2,1,0:T(8,128)S(1)} %copy-done.1, f32[2,1024,256]{2,1,0:T(8,128)S(1)} %copy-done.2, ...), custom_call_target="tpu_custom_call", output_to_operand_aliasing={{0}: (4, {}), {1}: (5, {})} | custom-call | flops 1073741824 | bytes 6291456 | tf_op jit(solution)/shard_map/stats/pallas_call | solution.py:349
  (144 shorter events, 67.7 us)
Async XLA Ops:
  6.1 11.3 %collective-permute-start.2 = (bf16[64,8,256]{2,1,0:T(8,128)(2,1)S(1)}, bf16[64,8,256]{2,1,0:T(8,128)(2,1)S(1)}, u32[]{:S(2)}, u32[]{:S(2)}) collective-permute-start(bf16[64,8,256]{2,1,0:T(8,128)(2,1)S(1)} %get-tuple-element.63), channel_id=1, source_target_pairs={{0,96},{32,0},{64,32},{96,64},{1,97},{33,1},{65,33},{97,65},{2,98}... | collective-permute-start | bytes 786440 | tf_op jit(solution)/shard_map/ppermute | solution.py:17
  7.6 10.0 %collective-permute-start.3 = (bf16[64,8,256]{2,1,0:T(8,128)(2,1)S(1)}, bf16[64,8,256]{2,1,0:T(8,128)(2,1)S(1)}, u32[]{:S(2)}, u32[]{:S(2)}) collective-permute-start(bf16[64,8,256]{2,1,0:T(8,128)(2,1)S(1)} %get-tuple-element.62), channel_id=1, source_target_pairs={{0,32},{32,64},{64,96},{96,0},{1,33},{33,65},{65,97},{97,1},{2,34}... | collective-permute-start | bytes 786440 | tf_op jit(solution)/shard_map/ppermute | solution.py:17
  23.5 12.4 %all-to-all-start = ((bf16[4,32,8,256]{3,2,1,0:T(8,128)(2,1)}), bf16[4,32,8,256]{3,2,1,0:T(8,128)(2,1)S(1)}, u32[]{:S(2)}, u32[]{:S(2)}) async-start(bf16[4,32,8,256]{3,2,1,0:T(8,128)(2,1)} %bitcast.9), calls=%async_computation | async-start | bytes 1048576 | tf_op jit(solution)/shard_map/all_to_all | solution.py:487
  37.5 21.4 %all-to-all-start.2 = ((bf16[32,32,256]{2,1,0:T(8,128)(2,1)}), bf16[32,32,256]{2,1,0:T(8,128)(2,1)S(1)}, u32[]{:S(2)}, u32[]{:S(2)}) async-start(bf16[32,32,256]{2,1,0:T(8,128)(2,1)} %broadcast_select_fusion), calls=%async_computation.2 | async-start | bytes 1048576 | tf_op jit(solution)/shard_map/all_to_all | solution.py:493
  58.9 87.1 %all-to-all-start.1 = ((bf16[32,4,32,256]{3,2,1,0:T(8,128)(2,1)}), bf16[32,4,32,256]{3,2,1,0:T(8,128)(2,1)S(1)}, u32[]{:S(2)}, u32[]{:S(2)}) async-start(bf16[32,4,32,256]{3,2,1,0:T(8,128)(2,1)} %gather_fusion.1), calls=%async_computation.1 | async-start | bytes 4194304 | tf_op jit(solution)/shard_map/all_to_all | solution.py:501
  68.8 14.5 %collective-permute-start.17 = (bf16[1024,256]{1,0:T(8,128)(2,1)S(1)}, bf16[1024,256]{1,0:T(8,128)(2,1)S(1)}, u32[]{:S(2)}, u32[]{:S(2)}) collective-permute-start(bf16[1024,256]{1,0:T(8,128)(2,1)S(1)} %get-tuple-element.65.refs_1_), channel_id=1, source_target_pairs={{0,32},{32,64},{64,96},{96,0},{1,33},{33,65},{65,97},{97,1},{2,34}... | collective-permute-start | bytes 1572872 | tf_op jit(solution)/shard_map/ppermute | solution.py:17
  69.7 13.8 %collective-permute-start.18 = (bf16[1024,256]{1,0:T(8,128)(2,1)S(1)}, bf16[1024,256]{1,0:T(8,128)(2,1)S(1)}, u32[]{:S(2)}, u32[]{:S(2)}) collective-permute-start(bf16[1024,256]{1,0:T(8,128)(2,1)S(1)} %get-tuple-element.65.refs_1_), channel_id=1, source_target_pairs={{0,96},{32,0},{64,32},{96,64},{1,97},{33,1},{65,33},{97,65},{2,98}... | collective-permute-start | bytes 1572872 | tf_op jit(solution)/shard_map/ppermute | solution.py:17
  71.5 23.0 %collective-permute-start.9 = (bf16[4,8,32,256]{3,2,1,0:T(8,128)(2,1)S(1)}, bf16[4,8,32,256]{3,2,1,0:T(8,128)(2,1)S(1)}, u32[]{:S(2)}, u32[]{:S(2)}) collective-permute-start(bf16[4,8,32,256]{3,2,1,0:T(8,128)(2,1)S(1)} %bitcast.42), channel_id=1, source_target_pairs={{0,32},{32,64},{64,96},{96,0},{1,33},{33,65},{65,97},{97,1},{2,34}... | collective-permute-start | bytes 1572872 | tf_op jit(solution)/shard_map/ppermute | solution.py:17
  71.5 23.5 %collective-permute-start.10 = (bf16[4,8,32,256]{3,2,1,0:T(8,128)(2,1)S(1)}, bf16[4,8,32,256]{3,2,1,0:T(8,128)(2,1)S(1)}, u32[]{:S(2)}, u32[]{:S(2)}) collective-permute-start(bf16[4,8,32,256]{3,2,1,0:T(8,128)(2,1)S(1)} %bitcast.43), channel_id=1, source_target_pairs={{0,96},{32,0},{64,32},{96,64},{1,97},{33,1},{65,33},{97,65},{2,98}... | collective-permute-start | bytes 1572872 | tf_op jit(solution)/shard_map/ppermute | solution.py:17
  83.3 16.8 %collective-permute-start.19 = (bf16[512,256]{1,0:T(8,128)(2,1)S(1)}, bf16[512,256]{1,0:T(8,128)(2,1)S(1)}, u32[]{:S(2)}, u32[]{:S(2)}) collective-permute-start(bf16[512,256]{1,0:T(8,128)(2,1)S(1)} %slice.64), channel_id=1, source_target_pairs={{0,32},{32,64},{64,96},{96,0},{1,33},{33,65},{65,97},{97,1},{2,34}... | collective-permute-start | bytes 786440 | tf_op jit(solution)/shard_map/ppermute | solution.py:17
  83.4 43.2 %collective-permute-start.13 = (bf16[1024,256]{1,0:T(8,128)(2,1)S(1)}, bf16[1024,256]{1,0:T(8,128)(2,1)S(1)}, u32[]{:S(2)}, u32[]{:S(2)}) collective-permute-start(bf16[1024,256]{1,0:T(8,128)(2,1)S(1)} %get-tuple-element.66.refs_0_.refs_2_), channel_id=1, source_target_pairs={{0,32},{32,64},{64,96},{96,0},{1,33},{33,65},{65,97},{97,1},{2,34}... | collective-permute-start | bytes 1572872 | tf_op jit(solution)/shard_map/ppermute | solution.py:17
  83.5 43.2 %collective-permute-start.14 = (bf16[1024,256]{1,0:T(8,128)(2,1)S(1)}, bf16[1024,256]{1,0:T(8,128)(2,1)S(1)}, u32[]{:S(2)}, u32[]{:S(2)}) collective-permute-start(bf16[1024,256]{1,0:T(8,128)(2,1)S(1)} %get-tuple-element.66.refs_0_.refs_2_), channel_id=1, source_target_pairs={{0,96},{32,0},{64,32},{96,64},{1,97},{33,1},{65,33},{97,65},{2,98}... | collective-permute-start | bytes 1572872 | tf_op jit(solution)/shard_map/ppermute | solution.py:17
  94.5 16.2 %collective-permute-start.20 = (bf16[512,256]{1,0:T(8,128)(2,1)S(1)}, bf16[512,256]{1,0:T(8,128)(2,1)S(1)}, u32[]{:S(2)}, u32[]{:S(2)}) collective-permute-start(bf16[512,256]{1,0:T(8,128)(2,1)S(1)} %slice.65), channel_id=1, source_target_pairs={{0,96},{32,0},{64,32},{96,64},{1,97},{33,1},{65,33},{97,65},{2,98}... | collective-permute-start | bytes 786440 | tf_op jit(solution)/shard_map/ppermute | solution.py:17
  95.0 22.0 %collective-permute-start.11 = (bf16[2,8,32,256]{3,2,1,0:T(8,128)(2,1)S(1)}, bf16[2,8,32,256]{3,2,1,0:T(8,128)(2,1)S(1)}, u32[]{:S(2)}, u32[]{:S(2)}) collective-permute-start(bf16[2,8,32,256]{3,2,1,0:T(8,128)(2,1)S(1)} %slice.58), channel_id=1, source_target_pairs={{0,32},{32,64},{64,96},{96,0},{1,33},{33,65},{65,97},{97,1},{2,34}... | collective-permute-start | bytes 786440 | tf_op jit(solution)/shard_map/ppermute | solution.py:17
  100.1 16.9 %collective-permute-start.12 = (bf16[2,8,32,256]{3,2,1,0:T(8,128)(2,1)S(1)}, bf16[2,8,32,256]{3,2,1,0:T(8,128)(2,1)S(1)}, u32[]{:S(2)}, u32[]{:S(2)}) collective-permute-start(bf16[2,8,32,256]{3,2,1,0:T(8,128)(2,1)S(1)} %slice.59), channel_id=1, source_target_pairs={{0,96},{32,0},{64,32},{96,64},{1,97},{33,1},{65,33},{97,65},{2,98}... | collective-permute-start | bytes 786440 | tf_op jit(solution)/shard_map/ppermute | solution.py:17
  124.2 33.3 %collective-permute-start.26 = (bf16[4,8,32,256]{3,2,1,0:T(8,128)(2,1)}, bf16[4,8,32,256]{3,2,1,0:T(8,128)(2,1)S(1)}, u32[]{:S(2)}, u32[]{:S(2)}) collective-permute-start(bf16[4,8,32,256]{3,2,1,0:T(8,128)(2,1)} %get-tuple-element.48), channel_id=1, source_target_pairs={{0,96},{32,0},{64,32},{96,64},{1,97},{33,1},{65,33},{97,65},{2,98}... | collective-permute-start | bytes 1572872 | tf_op jit(solution)/shard_map/ppermute | solution.py:17
  126.7 15.8 %collective-permute-start.16 = (bf16[512,256]{1,0:T(8,128)(2,1)S(1)}, bf16[512,256]{1,0:T(8,128)(2,1)S(1)}, u32[]{:S(2)}, u32[]{:S(2)}) collective-permute-start(bf16[512,256]{1,0:T(8,128)(2,1)S(1)} %slice.62), channel_id=1, source_target_pairs={{0,96},{32,0},{64,32},{96,64},{1,97},{33,1},{65,33},{97,65},{2,98}... | collective-permute-start | bytes 786440 | tf_op jit(solution)/shard_map/ppermute | solution.py:17
  129.4 30.9 %collective-permute-start.25 = (bf16[4,8,32,256]{3,2,1,0:T(8,128)(2,1)}, bf16[4,8,32,256]{3,2,1,0:T(8,128)(2,1)S(1)}, u32[]{:S(2)}, u32[]{:S(2)}) collective-permute-start(bf16[4,8,32,256]{3,2,1,0:T(8,128)(2,1)} %get-tuple-element.47), channel_id=1, source_target_pairs={{0,32},{32,64},{64,96},{96,0},{1,33},{33,65},{65,97},{97,1},{2,34}... | collective-permute-start | bytes 1572872 | tf_op jit(solution)/shard_map/ppermute | solution.py:17
  154.2 12.6 %collective-permute-start.22 = (bf16[4,8,32,256]{3,2,1,0:T(8,128)(2,1)}, bf16[4,8,32,256]{3,2,1,0:T(8,128)(2,1)S(1)}, u32[]{:S(2)}, u32[]{:S(2)}) collective-permute-start(bf16[4,8,32,256]{3,2,1,0:T(8,128)(2,1)} %get-tuple-element.43), channel_id=1, source_target_pairs={{0,96},{32,0},{64,32},{96,64},{1,97},{33,1},{65,33},{97,65},{2,98}... | collective-permute-start | bytes 1572872 | tf_op jit(solution)/shard_map/ppermute | solution.py:17
  157.5 14.2 %collective-permute-start.21 = (bf16[4,8,32,256]{3,2,1,0:T(8,128)(2,1)}, bf16[4,8,32,256]{3,2,1,0:T(8,128)(2,1)S(1)}, u32[]{:S(2)}, u32[]{:S(2)}) collective-permute-start(bf16[4,8,32,256]{3,2,1,0:T(8,128)(2,1)} %get-tuple-element.42), channel_id=1, source_target_pairs={{0,32},{32,64},{64,96},{96,0},{1,33},{33,65},{65,97},{97,1},{2,34}... | collective-permute-start | bytes 1572872 | tf_op jit(solution)/shard_map/ppermute | solution.py:17
  157.6 14.8 %collective-permute-start.28 = (bf16[2,8,32,256]{3,2,1,0:T(8,128)(2,1)S(1)}, bf16[2,8,32,256]{3,2,1,0:T(8,128)(2,1)S(1)}, u32[]{:S(2)}, u32[]{:S(2)}) collective-permute-start(bf16[2,8,32,256]{3,2,1,0:T(8,128)(2,1)S(1)} %add_convert_fusion), channel_id=1, source_target_pairs={{0,96},{32,0},{64,32},{96,64},{1,97},{33,1},{65,33},{97,65},{2,98}... | collective-permute-start | bytes 786440 | tf_op jit(solution)/shard_map/ppermute | solution.py:17
  160.4 15.1 %collective-permute-start.27 = (bf16[2,8,32,256]{3,2,1,0:T(8,128)(2,1)S(1)}, bf16[2,8,32,256]{3,2,1,0:T(8,128)(2,1)S(1)}, u32[]{:S(2)}, u32[]{:S(2)}) collective-permute-start(bf16[2,8,32,256]{3,2,1,0:T(8,128)(2,1)S(1)} %add_convert_fusion.1), channel_id=1, source_target_pairs={{0,32},{32,64},{64,96},{96,0},{1,33},{33,65},{65,97},{97,1},{2,34}... | collective-permute-start | bytes 786440 | tf_op jit(solution)/shard_map/ppermute | solution.py:17
  183.3 28.3 %all-to-all-start.3 = ((bf16[32,2,32,256]{3,2,1,0:T(8,128)(2,1)}), bf16[32,2,32,256]{3,2,1,0:T(8,128)(2,1)S(1)}, u32[]{:S(2)}, u32[]{:S(2)}) async-start(bf16[32,2,32,256]{3,2,1,0:T(8,128)(2,1)} %bitcast.41), calls=%async_computation.3 | async-start | bytes 2097152 | tf_op jit(solution)/shard_map/all_to_all | solution.py:527
  213.0 13.8 %all-to-all-start.4 = ((bf16[4,8,32,256]{3,2,1,0:T(8,128)(2,1)}), bf16[4,8,32,256]{3,2,1,0:T(8,128)(2,1)S(1)}, u32[]{:S(2)}, u32[]{:S(2)}) async-start(bf16[4,8,32,256]{3,2,1,0:T(8,128)(2,1)} %bitcast.50), calls=%async_computation.4 | async-start | bytes 1048576 | tf_op jit(solution)/shard_map/all_to_all | solution.py:534
  (38 other events, 512.4 us)
